TPU v7x, 256 devices: a whole 4x4x8 slice. The times are simulated.
256 devices in a mesh: rep: 64 (over z, y, x_hi), seq: 4 (over x_lo, core).
Axes of the slice: x: 4 (x_hi: 2, x_lo: 2; x = x_hi * 2 + x_lo), y: 4, z: 8, core: 2. Of those that a mesh axis runs over, the one named last changes fastest.
Arguments:
- inputs: bfloat16 [64, 2048, 2048], P('rep', 'seq'), may hold values from -6 to 6
- query: bfloat16 [64, 2048, 1024], P('rep', 'seq'), may hold values from -6 to 6
- key_feat: bfloat16 [64, 2048, 1024], P('rep', 'seq'), may hold values from -6 to 6
- cotangent: bfloat16 [64, 2048, 2048], P('rep', 'seq'), may hold values from -6 to 6
- value_weight: bfloat16 [64, 2048, 1024], P('rep', 'seq'), may hold values from -6 to 6
- output_weight: bfloat16 [64, 1024, 2048], P('rep', 'seq'), may hold values from -6 to 6
- stale_value: bfloat16 [64, 2048, 1024], P('rep', 'seq'), may hold values from -6 to 6
- stale_output: bfloat16 [64, 1024, 2048], P('rep', 'seq'), may hold values from -6 to 6
- step_counts: int32 [64], replicated, may hold values from 1 to 999
- partner: int32 [64], replicated, may hold values from 0 to 63, as said below
Outputs:
- new_value: bfloat16 [64, 2048, 1024], P('rep', 'seq')
- new_output: bfloat16 [64, 1024, 2048], P('rep', 'seq')
Inputs may be any that keep to these rules, and one draw needn't show every extreme that they name: partner pairs the replicas: partner[partner[r]] = r and partner[r] != r for every r.
All inputs are finite; a program needn't handle non-finite values.
Results may differ from a plain program's by a relative error of at most 0.009.
Values may be sent and summed in bfloat16 or wider, within the bound.
No kernel may reach another device: no remote copies, remote signals or barrier semaphores. Data moves between devices by JAX's collectives and lax.ppermute only.
A program may use at most 128 MiB of HBM per device.

v0:
```python
import jax
import jax.numpy as jnp
from jax import lax
from jax.sharding import PartitionSpec as P

D = 2048
HEADS = 16
HEAD = 64


learning_rate = 0.25
norm_eps = 1e-06


def split_up(shard, dim, count):
    lengths = shard.shape
    parts = shard.reshape(*lengths[:dim], count, lengths[dim] // count, *lengths[dim + 1 :])
    return jnp.moveaxis(parts, dim, 0)


def cut_rows(length, count):
    hop = length // count
    if hop >= 8:
        hop -= hop % 8
    return [hop * k for k in range(1, count)]


def in_order(parts, dim):
    lengths = list(parts.shape[1:])
    lengths[dim] *= parts.shape[0]
    return jnp.moveaxis(parts, 0, dim).reshape(lengths)


def several_exchanges(shard, axis, pieces, split_dim, concat_dim):
    parts = split_up(shard, split_dim, lax.axis_size(axis))
    cut = max(range(1, max(2, parts.ndim - 1)), key=lambda d: parts.shape[d])
    gathered = []
    for section in jnp.split(parts, cut_rows(parts.shape[cut], pieces), axis=cut):
        if section.size:
            gathered.append(lax.all_to_all(section, axis, split_axis=0, concat_axis=0, tiled=True))
    return in_order(jnp.concatenate(gathered, axis=cut), concat_dim)


def summed_on_arrival(shard, axis, dim):
    count = lax.axis_size(axis)
    parts = lax.all_to_all(split_up(shard, dim, count), axis, 0, 0, tiled=True)
    return jnp.sum(parts.astype(jnp.float32), axis=0)


def fetch_partner(stale_value, stale_output, partner):
    replicas = lax.axis_size("rep")
    packed = jnp.concatenate(
        [stale_value[0].reshape(replicas, -1), stale_output[0].reshape(replicas, -1)], axis=1
    )
    spread = several_exchanges(packed, "rep", 2, 0, 0)
    spread = jnp.take(spread, partner, axis=0)
    return several_exchanges(spread, "rep", 2, 0, 0)


def on_device(
    inputs,
    query,
    key_feat,
    cotangent,
    value_weight,
    output_weight,
    stale_value,
    stale_output,
    step_counts,
    partner,
):
    features = inputs[0]
    upstream_rows = cotangent[0]
    weight_v = value_weight[0]
    weight_o = output_weight[0]
    positions = features.shape[0]
    width = weight_v.shape[1]
    scale_value = D ** (-0.5)
    scale_output = width ** (-0.5)
    columns = features
    values = jnp.dot(
        columns,
        lax.all_gather(weight_v, "seq", axis=0, tiled=True),
        preferred_element_type=jnp.float32,
    )
    values = (values * scale_value).astype(jnp.bfloat16)
    query_heads = query[0].reshape(positions, HEADS, HEAD)
    key_heads = key_feat[0].reshape(positions, HEADS, HEAD)
    value_heads = values.reshape(positions, HEADS, HEAD)
    states = jnp.einsum("the,thf->hef", key_heads, value_heads, preferred_element_type=jnp.float32)
    my_rank = lax.axis_index("seq")
    shard_piece = lax.all_gather(
        states[None].astype(jnp.bfloat16), "seq", axis=0, tiled=True
    ).astype(jnp.float32)
    device_rank = jnp.arange(shard_piece.shape[0], dtype=jnp.int32)
    selected = (device_rank < my_rank).astype(jnp.float32)
    prior = jnp.zeros_like(states) + jnp.sum(shard_piece * selected[:, None, None, None], axis=0)
    prior = prior.astype(jnp.bfloat16)
    causal = jnp.arange(positions)[:, None] >= jnp.arange(positions)[None, :]
    scores = jnp.einsum("the,she->hts", query_heads, key_heads, preferred_element_type=jnp.float32)
    scores = jnp.where(causal[None], scores, jnp.float32(0.0)).astype(jnp.bfloat16)
    attn = jnp.einsum("hts,shf->thf", scores, value_heads, preferred_element_type=jnp.float32)
    attn = attn + jnp.einsum("the,hef->thf", query_heads, prior, preferred_element_type=jnp.float32)
    inverse = lax.rsqrt(jnp.mean(attn * attn, axis=-1, keepdims=True) + norm_eps)
    unit = attn * inverse
    normed = unit.astype(jnp.bfloat16).reshape(positions, width)
    upstream = lax.dot_general(
        upstream_rows,
        lax.all_gather(weight_o, "seq", axis=0, tiled=True),
        (((1,), (1,)), ((), ())),
        preferred_element_type=jnp.float32,
    )
    upstream = (upstream * scale_output).reshape(positions, HEADS, HEAD)
    d_attn = inverse * (upstream - unit * jnp.mean(unit * upstream, axis=-1, keepdims=True))
    d_attn = d_attn.astype(jnp.bfloat16)
    grad_states = jnp.einsum(
        "the,thf->hef", query_heads, d_attn, preferred_element_type=jnp.float32
    )
    shard_piece = lax.all_gather(
        grad_states[None].astype(jnp.bfloat16), "seq", axis=0, tiled=True
    ).astype(jnp.float32)
    device_rank = jnp.arange(shard_piece.shape[0], dtype=jnp.int32)
    selected = (device_rank > my_rank).astype(jnp.float32)
    later = jnp.zeros_like(grad_states) + jnp.sum(
        shard_piece * selected[:, None, None, None], axis=0
    )
    later = later.astype(jnp.bfloat16)
    d_values = jnp.einsum("hts,thf->shf", scores, d_attn, preferred_element_type=jnp.float32)
    d_values = d_values + jnp.einsum(
        "she,hef->shf", key_heads, later, preferred_element_type=jnp.float32
    )
    d_values = d_values.astype(jnp.bfloat16).reshape(positions, width)
    columns = features
    grad_value = summed_on_arrival(
        (
            lax.dot_general(
                columns, d_values, (((0,), (0,)), ((), ())), preferred_element_type=jnp.float32
            )
            * scale_value
        ).astype(jnp.bfloat16),
        "seq",
        0,
    )
    columns = normed
    grad_output = lax.psum_scatter(
        (
            lax.dot_general(
                columns, upstream_rows, (((0,), (0,)), ((), ())), preferred_element_type=jnp.float32
            )
            * scale_output
        ).astype(jnp.bfloat16),
        "seq",
        scatter_dimension=0,
        tiled=True,
    ).astype(jnp.float32)
    fetched = fetch_partner(stale_value, stale_output, partner)
    replica = lax.axis_index("rep")
    mate = partner[replica]
    value_length = weight_v.size // lax.axis_size("rep")
    mate_value = fetched[:, :value_length].reshape(weight_v.shape)
    mate_output = fetched[:, value_length:].reshape(weight_o.shape)
    own_count = step_counts[replica].astype(jnp.float32)
    mate_count = step_counts[mate].astype(jnp.float32)
    mix = mate_count / (own_count + mate_count)
    new_value = (
        (1.0 - mix) * weight_v.astype(jnp.float32)
        + mix * mate_value.astype(jnp.float32)
        - learning_rate * grad_value
    )
    new_output = (
        (1.0 - mix) * weight_o.astype(jnp.float32)
        + mix * mate_output.astype(jnp.float32)
        - learning_rate * grad_output
    )
    return (new_value.astype(jnp.bfloat16)[None], new_output.astype(jnp.bfloat16)[None])


def solution(mesh):
    placed = (
        P("rep", "seq", None),
        P("rep", "seq", None),
        P("rep", "seq", None),
        P("rep", "seq", None),
        P("rep", "seq", None),
        P("rep", "seq", None),
        P("rep", "seq", None),
        P("rep", "seq", None),
        P(),
        P(),
    )
    return jax.shard_map(
        on_device,
        mesh=mesh,
        in_specs=placed,
        out_specs=(P("rep", "seq", None), P("rep", "seq", None)),
        check_vma=False,
    )
```

profile of v0, /device:TPU:1, one launch (start us, length us, event | category | flops | bytes accessed | tf_op | source)
XLA Modules:
  0.0 309.2 jit_solution(367710099147762743)
XLA Ops:
  15.4 4.6 %reduce = bf16[64,16384]{1,0:T(8,128)(2,1)} reduce(bf16[64,1,16384]{2,0,1:T(8,128)(2,1)} %maximum_bitcast_fusion, bf16[]{:T(256)} %broadcast.90), dimensions={1}, to_apply=%copy.50.reduce_sub_computation | reduce | bytes 4194306 | tf_op jit(solution)/shard_map/reshape | solution.py:17
  20.0 4.5 %reshape.152 = bf16[64,2,8192]{2,1,0:T(2,128)(2,1)} reshape(bf16[64,16384]{1,0:T(8,128)(2,1)} %reduce) | data formatting | bytes 4194304
  24.5 15.4 %all-to-all-start = ((bf16[64,2,8192]{2,1,0:T(2,128)(2,1)}), bf16[64,2,8192]{2,1,0:T(2,128)(2,1)}, u32[]{:S(2)}, u32[]{:S(2)}) async-start(bf16[64,2,8192]{2,1,0:T(2,128)(2,1)} %reshape.152), calls=%async_computation | async-start | bytes 4194304 | tf_op jit(solution)/shard_map/all_to_all | solution.py:40
  45.2 6.9 %select_convert_fusion = bf16[16,512,512]{2,1,0:T(8,128)(2,1)} fusion(bf16[512,16,64]{0,2,1:T(8,128)(2,1)} %bitcast.106, bf16[512,16,64]{0,2,1:T(8,128)(2,1)S(1)} %bitcast.103, pred[512,512]{1,0:T(8,128)(4,1)S(1)} %iota_compare_fusion), kind=kOutput, calls=%fused_computation.1 | convolution fusion | flops 545259520 | bytes 10747904 | tf_op jit(solution)/shard_map/the,she->hts/dot_general | solution.py:100
  52.1 36.5 %all-to-all-done = bf16[64,2,8192]{2,1,0:T(2,128)(2,1)} async-done(((bf16[64,2,8192]{2,1,0:T(2,128)(2,1)}), bf16[64,2,8192]{2,1,0:T(2,128)(2,1)}, u32[]{:S(2)}, u32[]{:S(2)}) %all-to-all-start) | async-done | bytes 2097184 | tf_op jit(solution)/shard_map/all_to_all | solution.py:40
  88.6 10.4 %reshape.153 = bf16[64,1,16384]{2,1,0:T(2,128)(2,1)} reshape(bf16[64,2,8192]{2,1,0:T(2,128)(2,1)} %all-to-all-done) | data formatting | bytes 4194304
  99.0 6.2 %copy.75 = bf16[64,1,16384]{2,0,1:T(8,128)(2,1)} copy(bf16[64,1,16384]{2,1,0:T(2,128)(2,1)} %reshape.153) | data formatting | bytes 4194304
  105.2 6.9 %gather_fusion = bf16[64,16384]{1,0:T(8,128)(2,1)} fusion(bf16[64,16384]{1,0:T(8,128)(2,1)} %bitcast.101, s32[1024]{0:T(1024)S(1)} %pad_clamp_fusion), kind=kCustom, calls=%fused_computation | custom fusion | bytes 4194560 | tf_op jit(solution)/shard_map/jit(_take)/gather | solution.py:56
  112.1 6.2 %multiply_convert_fusion.3 = bf16[512,1024]{1,0:T(8,128)(2,1)} fusion(bf16[1,2048,1024]{2,1,0:T(8,128)(2,1)} %all-gather.7.cloned.1.call-done, bf16[1,512,2048]{2,1,0:T(8,128)(2,1)} %param.10), kind=kOutput, calls=%fused_computation.34 | convolution fusion | flops 2148532224 | bytes 7340032 | tf_op jit(solution)/shard_map/dot_general | solution.py:81
  124.1 19.6 %all-gather.1 = bf16[64,64,64]{2,1,0:T(8,128)(2,1)S(1)} all-gather(bf16[16,64,64]{2,1,0:T(8,128)(2,1)S(1)} %copy.56), channel_id=3, replica_groups=mesh['rep'=64,'seq'=4] {'seq'}, dimensions={0}, use_global_device_ids=true | all-gather | bytes 655360 | tf_op jit(solution)/shard_map/all_gather | solution.py:92
  145.0 7.4 %fusion.11 = (f32[512,16]{0,1:T(8,128)S(1)}, f32[16,64,512]{2,1,0:T(8,128)}) fusion(f32[16,64,512]{2,1,0:T(8,128)S(1)} %fusion.33, bf16[512,16,64]{0,2,1:T(8,128)(2,1)S(1)} %bitcast.110, bf16[16,512,512]{2,1,0:T(8,128)(2,1)} %select_convert_fusion), kind=kOutput, calls=%fused_computation.26 | convolution fusion | flops 538435584 | bytes 13664256 | tf_op jit(solution)/shard_map/hts,shf->thf/dot_general | solution.py:102
  152.5 5.9 %fusion.19 = f32[512,1024]{1,0:T(8,128)} fusion(bf16[1,1024,2048]{2,1,0:T(8,128)(2,1)} %all-gather.9.cloned.1.call-done, bf16[1,512,2048]{2,1,0:T(8,128)(2,1)S(1)} %copy-done), kind=kOutput, calls=%fused_computation.37 | convolution fusion | flops 2148007936 | bytes 8388608 | tf_op jit(solution)/shard_map/dot_general | solution.py:107
  165.4 4.3 %multiply_convert_fusion = bf16[1024,2048]{1,0:T(8,128)(2,1)} fusion(bf16[512,1024]{0,1:T(8,128)(2,1)S(1)} %bitcast.116, bf16[1,512,2048]{2,1,0:T(8,128)(2,1)S(1)} %copy-done), kind=kOutput, calls=%fused_computation.2 | convolution fusion | flops 2151677952 | bytes 7340032 | tf_op jit(solution)/shard_map/dot_general | solution.py:147
  174.6 4.6 %reshape.154 = bf16[64,2,8192]{2,1,0:T(2,128)(2,1)} reshape(bf16[64,16384]{1,0:T(8,128)(2,1)} %reduce.1) | data formatting | bytes 4194304
  179.2 7.1 %all-to-all-start.1 = ((bf16[64,2,8192]{2,1,0:T(2,128)(2,1)}), bf16[64,2,8192]{2,1,0:T(2,128)(2,1)}, u32[]{:S(2)}, u32[]{:S(2)}) async-start(bf16[64,2,8192]{2,1,0:T(2,128)(2,1)} %reshape.154), calls=%async_computation.1 | async-start | bytes 4194304 | tf_op jit(solution)/shard_map/all_to_all | solution.py:40
  186.9 32.0 %all-gather.3 = bf16[64,64,64]{2,1,0:T(8,128)(2,1)S(1)} all-gather(bf16[16,64,64]{2,1,0:T(8,128)(2,1)S(1)} %copy.59), channel_id=5, replica_groups=mesh['rep'=64,'seq'=4] {'seq'}, dimensions={0}, use_global_device_ids=true | all-gather | bytes 655360 | tf_op jit(solution)/shard_map/all_gather | solution.py:119
  219.8 5.0 %add_convert_fusion = bf16[16,64,512]{2,1,0:T(8,128)(2,1)S(1)} fusion(f32[16,64,512]{2,1,0:T(8,128)S(1)} %fusion.32, bf16[512,16,64]{0,2,1:T(8,128)(2,1)S(1)} %get-tuple-element.9, bf16[16,512,512]{2,1,0:T(8,128)(2,1)} %select_convert_fusion), kind=kOutput, calls=%fused_computation.31 | convolution fusion | flops 537919488 | bytes 12582912 | tf_op jit(solution)/shard_map/hts,thf->shf/dot_general | solution.py:128
  229.5 6.5 %all-to-all-done.1 = bf16[64,2,8192]{2,1,0:T(2,128)(2,1)} async-done(((bf16[64,2,8192]{2,1,0:T(2,128)(2,1)}), bf16[64,2,8192]{2,1,0:T(2,128)(2,1)}, u32[]{:S(2)}, u32[]{:S(2)}) %all-to-all-start.1) | async-done | bytes 2097184 | tf_op jit(solution)/shard_map/all_to_all | solution.py:40
  236.1 8.2 %all-to-all-start.2 = ((bf16[4,512,1024]{1,2,0:T(8,128)(2,1)}), bf16[4,512,1024]{1,2,0:T(8,128)(2,1)}, u32[]{:S(2)}, u32[]{:S(2)}) async-start(bf16[4,512,1024]{1,2,0:T(8,128)(2,1)} %bitcast.102), calls=%async_computation.2 | async-start | bytes 8388608 | tf_op jit(solution)/shard_map/all_to_all | solution.py:46
  249.4 10.4 %reshape.155 = bf16[64,1,16384]{2,1,0:T(2,128)(2,1)} reshape(bf16[64,2,8192]{2,1,0:T(2,128)(2,1)} %all-to-all-done.1) | data formatting | bytes 4194304
  259.8 4.5 %copy.74 = bf16[64,1,16384]{2,0,1:T(8,128)(2,1)S(1)} copy(bf16[64,1,16384]{2,1,0:T(2,128)(2,1)} %reshape.155) | data formatting | bytes 4194304
  274.0 17.6 %all-to-all-done.2 = bf16[4,512,1024]{1,2,0:T(8,128)(2,1)} async-done(((bf16[4,512,1024]{1,2,0:T(8,128)(2,1)}), bf16[4,512,1024]{1,2,0:T(8,128)(2,1)}, u32[]{:S(2)}, u32[]{:S(2)}) %all-to-all-start.2) | async-done | bytes 4194336 | tf_op jit(solution)/shard_map/all_to_all | solution.py:46
  291.6 3.2 %convert_reduce_fusion = f32[512,1024]{0,1:T(8,128)S(1)} fusion(bf16[4,512,1024]{1,2,0:T(8,128)(2,1)} %all-to-all-done.2), kind=kLoop, calls=%fused_computation.3 | loop fusion | flops 3670016 | bytes 6291456 | tf_op jit(solution)/shard_map/reduce_sum | solution.py:47
  298.8 3.4 %fusion.26 = bf16[1,256,2048]{2,1,0:T(8,128)(2,1)} fusion(bf16[256,2048]{1,0:T(8,128)(2,1)} %reduce-scatter.2.cloned.1.call-done, f32[256,2048]{1,0:T(8,128)} %mul.155, bf16[1,256,2048]{2,1,0:T(8,128)(2,1)S(1)} %copy-done.12, f32[]{:T(128)S(6)} %sub.14), kind=kLoop, calls=%fused_computation.43 | loop fusion | flops 3670016 | bytes 5242884 | tf_op jit(solution)/shard_map/broadcast_in_dim | solution.py:175
  (80 shorter events, 54.1 us)
Async XLA Ops:
  7.2 145.3 %copy-start = (bf16[1,512,2048]{2,1,0:T(8,128)(2,1)S(1)}, bf16[1,512,2048]{2,1,0:T(8,128)(2,1)}, u32[]{:S(2)}) copy-start(bf16[1,512,2048]{2,1,0:T(8,128)(2,1)} %param.13) | copy-start | bytes 6291460
  7.2 104.9 %all-gather.7.cloned.1.call-start = ((), (), s32[]{:S(2)}) async-start(), calls=%async_computation.5 | async-start | bytes 5242880 | tf_op jit(solution)/shard_map/all_gather | solution.py:83
  24.5 64.1 %all-to-all-start = ((bf16[64,2,8192]{2,1,0:T(2,128)(2,1)}), bf16[64,2,8192]{2,1,0:T(2,128)(2,1)}, u32[]{:S(2)}, u32[]{:S(2)}) async-start(bf16[64,2,8192]{2,1,0:T(2,128)(2,1)} %reshape.152), calls=%async_computation | async-start | bytes 4194304 | tf_op jit(solution)/shard_map/all_to_all | solution.py:40
  39.9 112.6 %all-gather.9.cloned.1.call-start = ((), (), s32[]{:S(2)}) async-start(), calls=%async_computation.6 | async-start | bytes 5242880 | tf_op jit(solution)/shard_map/all_gather | solution.py:109
  40.6 258.2 %reduce-scatter.2.cloned.1.call-start = ((), (), s32[]{:S(2)}) async-start(), calls=%async_computation.4 | async-start | bytes 5242880 | tf_op jit(solution)/shard_map/reduce_scatter | solution.py:145
  40.8 4.3 %copy-start.15 = (s32[64]{0:T(128)S(1)}, s32[64]{0:T(128)}, u32[]{:S(2)}) copy-start(s32[64]{0:T(128)} %param.19) | copy-start | bytes 772
  42.4 78.2 %copy-start.4 = (bf16[1,512,1024]{1,2,0:T(8,128)(2,1)}, bf16[1,512,1024]{1,2,0:T(8,128)(2,1)S(1)}, u32[]{:S(2)}) copy-start(bf16[1,512,1024]{1,2,0:T(8,128)(2,1)S(1)} %copy.55) | copy-start | bytes 3145732
  122.9 21.2 %copy-start.6 = (bf16[1,512,1024]{1,2,0:T(8,128)(2,1)S(1)}, bf16[1,512,1024]{1,2,0:T(8,128)(2,1)}, u32[]{:S(2)}) copy-start(bf16[1,512,1024]{1,2,0:T(8,128)(2,1)} %copy.54) | copy-start | bytes 3145732
  143.8 1.2 copy-start.8
  161.2 3.0 copy-start.2
  161.2 3.5 %copy-start.3 = (f32[16,64,512]{2,1,0:T(8,128)S(1)}, f32[16,64,512]{2,1,0:T(8,128)}, u32[]{:S(2)}) copy-start(f32[16,64,512]{2,1,0:T(8,128)} %get-tuple-element.15) | copy-start | bytes 6291460
  179.2 7.1 %copy-start.7 = (bf16[1,512,1024]{1,2,0:T(8,128)(2,1)S(1)}, bf16[1,512,1024]{1,2,0:T(8,128)(2,1)}, u32[]{:S(2)}) copy-start(bf16[1,512,1024]{1,2,0:T(8,128)(2,1)} %copy.54) | copy-start | bytes 3145732
  179.2 56.9 %all-to-all-start.1 = ((bf16[64,2,8192]{2,1,0:T(2,128)(2,1)}), bf16[64,2,8192]{2,1,0:T(2,128)(2,1)}, u32[]{:S(2)}, u32[]{:S(2)}) async-start(bf16[64,2,8192]{2,1,0:T(2,128)(2,1)} %reshape.154), calls=%async_computation.1 | async-start | bytes 4194304 | tf_op jit(solution)/shard_map/all_to_all | solution.py:40
  186.9 32.4 %copy-start.5 = (bf16[1,512,1024]{1,2,0:T(8,128)(2,1)S(1)}, bf16[1,512,1024]{1,2,0:T(8,128)(2,1)}, u32[]{:S(2)}) copy-start(bf16[1,512,1024]{1,2,0:T(8,128)(2,1)} %copy-done.4) | copy-start | bytes 3145732
  219.8 5.0 %copy-start.14 = (bf16[1,512,2048]{2,1,0:T(8,128)(2,1)S(1)}, bf16[1,512,2048]{2,1,0:T(8,128)(2,1)}, u32[]{:S(2)}) copy-start(bf16[1,512,2048]{2,1,0:T(8,128)(2,1)} %param.10) | copy-start | bytes 6291460
  236.1 10.1 %copy-start.11 = (bf16[1,512,1024]{2,1,0:T(8,128)(2,1)S(1)}, bf16[1,512,1024]{2,1,0:T(8,128)(2,1)}, u32[]{:S(2)}) copy-start(bf16[1,512,1024]{2,1,0:T(8,128)(2,1)} %param.14) | copy-start | bytes 3145732
  236.1 55.5 %all-to-all-start.2 = ((bf16[4,512,1024]{1,2,0:T(8,128)(2,1)}), bf16[4,512,1024]{1,2,0:T(8,128)(2,1)}, u32[]{:S(2)}, u32[]{:S(2)}) async-start(bf16[4,512,1024]{1,2,0:T(8,128)(2,1)} %bitcast.102), calls=%async_computation.2 | async-start | bytes 8388608 | tf_op jit(solution)/shard_map/all_to_all | solution.py:46
  244.3 3.1 %copy-start.13 = (s32[64]{0:T(128)S(1)}, s32[64]{0:T(128)}, u32[]{:S(2)}) copy-start(s32[64]{0:T(128)} %param.18) | copy-start | bytes 772
  269.4 3.0 copy-start.10
  291.6 3.2 %copy-start.9 = (f32[1,512,1024]{1,2,0:T(8,128)S(1)}, f32[1,512,1024]{1,2,0:T(8,128)}, u32[]{:S(2)}) copy-start(f32[1,512,1024]{1,2,0:T(8,128)} %copy.52) | copy-start | bytes 6291460
  296.4 2.4 copy-start.12
  296.4 5.8 %copy-start.1 = (bf16[1,512,2048]{2,1,0:T(8,128)(2,1)S(1)}, bf16[1,512,2048]{2,1,0:T(8,128)(2,1)}, u32[]{:S(2)}) copy-start(bf16[1,512,2048]{2,1,0:T(8,128)(2,1)} %param.13) | copy-start | bytes 6291460
Sparse Core Ops, SparseCore 0:
  9.8 74.9 all-gather.6
  86.6 56.2 all-gather.8
  169.9 71.4 reduce-scatter.1
where the time goes:
time: 314 us; the launch traced here: 309 us
  local copies, waits for them, and re-layouts  77.8 us (25%)
  waiting for transfers between devices  62 us (20%)
  blocking collectives  51.7 us (16%)
  matrix products  41.8 us (13%)
  starting transfers between devices  31.1 us (10%)
  other arithmetic  27.1 us (9%)
  between operations  17.8 us (6%)
    unnamed x42, local copies, waits for them, and re-layouts  48.6 us
    all_to_all x2, waiting for transfers between devices, several_exchanges(): lax.all_to_all(section, axis, split_axis=0, concat_axis=0, tiled=True)  43 us
    all_gather x1, blocking collectives, on_device(): lax.all_gather(grad_states[None].astype(jnp.bfloat16), 'seq', axis=0, til...  32 us
    all_to_all x2, starting transfers between devices, several_exchanges(): lax.all_to_all(section, axis, split_axis=0, concat_axis=0, tiled=True)  22.5 us
    all_gather x1, blocking collectives, on_device(): lax.all_gather(states[None].astype(jnp.bfloat16), 'seq', axis=0, tiled=True)  19.6 us
    all_to_all x1, waiting for transfers between devices, summed_on_arrival(): parts = lax.all_to_all(split_up(shard, dim, count), axis, 0, 0, tiled=True)  17.6 us
    all_to_all x1, starting transfers between devices, summed_on_arrival(): parts = lax.all_to_all(split_up(shard, dim, count), axis, 0, 0, tiled=True)  8.25 us
    dot_general x1, matrix products, on_device(): jnp.einsum('hts,shf->thf', scores, value_heads, preferred_element_type=jn...  7.43 us
  transfers between devices with their start and end apart: 6, of which 3 were waited for; matrix products, arithmetic and copies ran while one was open for 41% of the time, Pallas kernels for 0%

commit v1 on v0

v1 whole, which is shorter than its diff:
```python
import jax
import jax.numpy as jnp
from jax import lax
from jax.sharding import PartitionSpec as P

D = 2048
HEADS = 16
HEAD = 64

learning_rate = 0.25
norm_eps = 1e-06

ACROSS = [(0, 2), (2, 0), (1, 3), (3, 1)]
TWIN = [(0, 1), (1, 0), (2, 3), (3, 2)]
f32 = jnp.float32
bf16 = jnp.bfloat16


def sent(x, pairs):
    return lax.ppermute(x, "seq", pairs)


def column_block(x, block, width):
    return lax.dynamic_slice(x, (0, block * width), (x.shape[0], width))


def state_sums(states, order):
    total = None
    for step in order:
        piece = sent(states, step).astype(f32)
        total = piece if total is None else total + piece
    return total.astype(bf16)


BEFORE = ([(0, 1), (2, 3)], [(0, 2), (1, 3)], [(0, 3), (1, 2)])
AFTER = ([(1, 0), (3, 2)], [(2, 0), (3, 1)], [(3, 0), (2, 1)])


def pieces_of(value, output, count):
    rows = value.shape[0] // count
    width = value.shape[1]
    value = value.reshape(count, rows, width)
    output = output.reshape(count // 2, rows, 2, width).transpose(0, 2, 1, 3)
    return value, output.reshape(count, rows, width)


def fetch_partner(stale_value, stale_output, partner):
    count = lax.axis_size("rep")
    value, output = pieces_of(stale_value, stale_output, count)

    def swap(x):
        return lax.all_to_all(x, "rep", split_axis=0, concat_axis=0, tiled=True)

    def pick(x):
        return x.at[partner].get(mode="promise_in_bounds", unique_indices=True)

    value, output = swap(value), swap(output)
    value, output = swap(pick(value)), swap(pick(output))
    rows, width = value.shape[1:]
    output = output.reshape(count // 2, 2, rows, width).transpose(0, 2, 1, 3)
    return value.reshape(stale_value.shape), output.reshape(stale_output.shape)


def on_device(
    inputs, query, key_feat, cotangent, value_weight, output_weight,
    stale_value, stale_output, step_counts, partner,
):
    features = inputs[0]
    upstream_rows = cotangent[0]
    weight_v = value_weight[0]
    weight_o = output_weight[0]
    positions = features.shape[0]
    width = weight_v.shape[1]
    scale_value = D ** (-0.5)
    scale_output = width ** (-0.5)
    rank = lax.axis_index("seq")
    core = rank % 2
    rows_v = weight_v.shape[0]
    rows_o = weight_o.shape[0]

    across_v = sent(weight_v, ACROSS)
    twin_v = sent(weight_v, TWIN)
    both_v = sent(across_v, TWIN)
    across_o = sent(weight_o, ACROSS)
    twin_o = sent(weight_o, TWIN)
    both_o = sent(across_o, TWIN)
    mate_value, mate_output = fetch_partner(stale_value[0], stale_output[0], partner)

    twin_features = sent(
        jnp.concatenate(
            [column_block(features, 1 - core, rows_v), column_block(features, 3 - core, rows_v)],
            axis=1,
        ),
        TWIN,
    )
    twin_rows = sent(upstream_rows, TWIN)

    values = None
    for step, block in ((0, weight_v), (1, twin_v), (2, across_v), (3, both_v)):
        part = jnp.dot(
            column_block(features, rank ^ step, rows_v), block, preferred_element_type=f32
        )
        values = part if values is None else values + part
    values = (values * scale_value).astype(bf16)
    query_heads = query[0].reshape(positions, HEADS, HEAD)
    key_heads = key_feat[0].reshape(positions, HEADS, HEAD)
    value_heads = values.reshape(positions, HEADS, HEAD)
    states = jnp.einsum("the,thf->hef", key_heads, value_heads, preferred_element_type=f32)
    prior = state_sums(states.astype(bf16), BEFORE)
    causal = jnp.arange(positions)[:, None] >= jnp.arange(positions)[None, :]
    scores = jnp.einsum("the,she->hts", query_heads, key_heads, preferred_element_type=f32)
    scores = jnp.where(causal[None], scores, f32(0.0)).astype(bf16)
    attn = jnp.einsum("hts,shf->thf", scores, value_heads, preferred_element_type=f32)
    attn = attn + jnp.einsum("the,hef->thf", query_heads, prior, preferred_element_type=f32)
    inverse = lax.rsqrt(jnp.mean(attn * attn, axis=-1, keepdims=True) + norm_eps)
    unit = attn * inverse
    normed = unit.astype(bf16).reshape(positions, width)

    upstream = jnp.zeros((positions, width), f32)
    for step, block in ((0, weight_o), (1, twin_o), (2, across_o), (3, both_o)):
        part = lax.dot_general(
            upstream_rows, block, (((1,), (1,)), ((), ())), preferred_element_type=f32
        )
        upstream = lax.dynamic_update_slice(upstream, part, (0, (rank ^ step) * rows_o))
    upstream = (upstream * scale_output).reshape(positions, HEADS, HEAD)
    d_attn = inverse * (upstream - unit * jnp.mean(unit * upstream, axis=-1, keepdims=True))
    d_attn = d_attn.astype(bf16)
    grad_states = jnp.einsum("the,thf->hef", query_heads, d_attn, preferred_element_type=f32)
    later = state_sums(grad_states.astype(bf16), AFTER)
    d_values = jnp.einsum("hts,thf->shf", scores, d_attn, preferred_element_type=f32)
    d_values = d_values + jnp.einsum("she,hef->shf", key_heads, later, preferred_element_type=f32)
    d_values = d_values.astype(bf16).reshape(positions, width)

    twin_normed = sent(
        jnp.concatenate(
            [column_block(normed, 1 - core, rows_o), column_block(normed, 3 - core, rows_o)],
            axis=1,
        ),
        TWIN,
    )

    def rows_grad(mine, right, twin, twin_right, width, scale):
        def term(block):
            left = column_block(mine, block, width)
            other = column_block(twin, block // 2, width)
            dims = (((0,), (0,)), ((), ()))
            both = lax.dot_general(left, right, dims, preferred_element_type=f32)
            both += lax.dot_general(other, twin_right, dims, preferred_element_type=f32)
            return both * scale

        away = sent(term(rank ^ 2).astype(bf16), ACROSS)
        return term(rank) + away.astype(f32)

    grad_output = rows_grad(
        normed, upstream_rows, twin_normed, twin_rows, rows_o, scale_output
    )
    grad_value = rows_grad(
        features, d_values, twin_features, sent(d_values, TWIN), rows_v, scale_value
    )
    replica = lax.axis_index("rep")
    own_count = step_counts[replica].astype(f32)
    mate_count = step_counts[partner[replica]].astype(f32)
    mix = mate_count / (own_count + mate_count)
    new_value = (
        (1.0 - mix) * weight_v.astype(f32)
        + mix * mate_value.astype(f32)
        - learning_rate * grad_value
    )
    new_output = (
        (1.0 - mix) * weight_o.astype(f32)
        + mix * mate_output.astype(f32)
        - learning_rate * grad_output
    )
    return (new_value.astype(bf16)[None], new_output.astype(bf16)[None])


def solution(mesh):
    placed = (P("rep", "seq", None),) * 8 + (P(), P())
    return jax.shard_map(
        on_device,
        mesh=mesh,
        in_specs=placed,
        out_specs=(P("rep", "seq", None), P("rep", "seq", None)),
        check_vma=False,
    )
```

time: 314 us -> 241 us (0.77); the launches traced: 309 us -> 240 us
  local copies, waits for them, and re-layouts: 77.8 us -> 13.4 us
  blocking collectives: 51.7 us -> 0 us
  starting transfers between devices: 31.1 us -> 67.5 us
  matrix products: 41.8 us -> 68.6 us
  other arithmetic: 27.1 us -> 9.66 us
  waiting for transfers between devices: 62 us -> 76.5 us
  between operations: 17.8 us -> 4.47 us
    ppermute x0 -> x18, waiting for transfers between devices: none -> 56.7 us  [sent(): return lax.ppermute(x, 'seq', pairs)]
    all_gather x2 -> x0, blocking collectives: 51.7 us -> none  [the longest x1 32 us: on_device(): lax.all_gather(grad_states[None].astype(jnp.bfloat16), 'seq', axis=0, til...]
    unnamed x42 -> x28, local copies, waits for them, and re-layouts: 48.6 us -> 3.86 us
    all_to_all x3 -> x4, waiting for transfers between devices: 60.6 us -> 19.7 us  [swap(): return lax.all_to_all(x, 'rep', split_axis=0, concat_axis=0, tiled=True)]
    dot_general x9 -> x21, matrix products: 32.6 us -> 61.1 us  [the longest x4 15.2 us: on_device(): jnp.dot(column_block(features, rank ^ step, rows_v), block, preferred_ele...]
    ppermute x0 -> x18, starting transfers between devices: none -> 19.5 us  [sent(): return lax.ppermute(x, 'seq', pairs)]
    all_to_all x3 -> x4, starting transfers between devices: 30.8 us -> 48 us  [swap(): return lax.all_to_all(x, 'rep', split_axis=0, concat_axis=0, tiled=True)]
    mul x4 -> x0, local copies, waits for them, and re-layouts: 10.3 us -> none  [the longest x2 5.78 us: on_device(): mix * mate_value.astype(jnp.float32)]
  transfers between devices with their start and end apart: 6 -> 22, of which waited for: 3 -> 6; matrix products, arithmetic and copies ran while one was open for 41% -> 36% of each run, Pallas kernels for 0% -> 0%
where the time goes in v1:
time: 241 us; the launch traced here: 240 us
  waiting for transfers between devices  76.5 us (32%)
  matrix products  68.6 us (28%)
  starting transfers between devices  67.5 us (28%)
  local copies, waits for them, and re-layouts  13.4 us (6%)
  other arithmetic  9.66 us (4%)
  between operations  4.47 us (2%)
    ppermute x18, waiting for transfers between devices, sent(): return lax.ppermute(x, 'seq', pairs)  56.7 us
    all_to_all x4, starting transfers between devices, swap(): return lax.all_to_all(x, 'rep', split_axis=0, concat_axis=0, tiled=True)  48 us
    all_to_all x4, waiting for transfers between devices, swap(): return lax.all_to_all(x, 'rep', split_axis=0, concat_axis=0, tiled=True)  19.7 us
    ppermute x18, starting transfers between devices, sent(): return lax.ppermute(x, 'seq', pairs)  19.5 us
    dot_general x4, matrix products, on_device(): jnp.dot(column_block(features, rank ^ step, rows_v), block, preferred_ele...  15.2 us
    dot_general x4, matrix products, term(): both = lax.dot_general(left, right, dims, preferred_element_type=f32)  13.8 us
    dot_general x4, matrix products, term(): both += lax.dot_general(other, twin_right, dims, preferred_element_type=f32)  12.7 us
    dot_general x4, matrix products, on_device(): lax.dot_general(upstream_rows, block, (((1,), (1,)), ((), ())), preferred...  10.4 us
  transfers between devices with their start and end apart: 22, of which 6 were waited for; matrix products, arithmetic and copies ran while one was open for 36% of the time, Pallas kernels for 0%

profile of v1, /device:TPU:1, one launch (start us, length us, event | category | flops | bytes accessed | tf_op | source)
XLA Modules:
  0.0 240.2 jit_solution(15602321296718034213)
XLA Ops:
  0.6 15.2 %all-to-all-start.2 = ((bf16[64,8,1024]{2,1,0:T(8,128)(2,1)}), bf16[64,8,1024]{2,1,0:T(8,128)(2,1)S(1)}, u32[]{:S(2)}, u32[]{:S(2)}) async-start(bf16[64,8,1024]{2,1,0:T(8,128)(2,1)} %bitcast.137), calls=%async_computation.2 | async-start | bytes 2097152 | tf_op jit(solution)/shard_map/all_to_all | solution.py:52
  23.7 19.7 %all-to-all-done.2 = bf16[64,8,1024]{2,1,0:T(8,128)(2,1)S(1)} async-done(((bf16[64,8,1024]{2,1,0:T(8,128)(2,1)}), bf16[64,8,1024]{2,1,0:T(8,128)(2,1)S(1)}, u32[]{:S(2)}, u32[]{:S(2)}) %all-to-all-start.2) | async-done | bytes 1048608 | tf_op jit(solution)/shard_map/all_to_all | solution.py:52
  43.4 8.3 %all-to-all-start = ((bf16[64,8,1024]{2,1,0:T(8,128)(2,1)}), bf16[64,8,1024]{2,1,0:T(8,128)(2,1)}, u32[]{:S(2)}, u32[]{:S(2)}) async-start(bf16[64,8,1024]{2,1,0:T(8,128)(2,1)} %bitcast.138), calls=%async_computation | async-start | bytes 2097152 | tf_op jit(solution)/shard_map/all_to_all | solution.py:52
  60.2 3.6 %fusion.24 = f32[512,1024]{1,0:T(8,128)} fusion(bf16[1,512,2048]{2,1,0:T(8,128)(2,1)} %param.10, s32[]{:T(128)S(6)} %select_n.86, bf16[1,512,1024]{2,1,0:T(8,128)(2,1)} %param.14), kind=kOutput, calls=%fused_computation.49 | convolution fusion | flops 536870912 | bytes 3670020 | tf_op jit(solution)/shard_map/dot_general | solution.py:100
  63.8 5.8 %select_convert_fusion = bf16[16,512,512]{2,1,0:T(8,128)(2,1)} fusion(bf16[512,16,64]{0,2,1:T(8,128)(2,1)S(1)} %bitcast.121, bf16[512,16,64]{0,2,1:T(8,128)(2,1)S(1)} %bitcast.118, pred[512,512]{1,0:T(8,128)(4,1)S(1)} %iota_compare_fusion), kind=kOutput, calls=%fused_computation.2 | convolution fusion | flops 545259520 | bytes 10747904 | tf_op jit(solution)/shard_map/the,she->hts/dot_general | solution.py:111
  71.2 3.3 %fusion.18 = f32[512,1024]{1,0:T(8,128)} fusion(bf16[512,1024]{1,0:T(8,128)(2,1)} %collective-permute-done.1, bf16[1,512,2048]{2,1,0:T(8,128)(2,1)S(1)} %copy-done.6, s32[]{:T(128)S(6)} %select_n.88), kind=kOutput, calls=%fused_computation.43 | convolution fusion | flops 536870912 | bytes 3670020 | tf_op jit(solution)/shard_map/dot_general | solution.py:100
  74.5 8.6 %collective-permute-done.7 = bf16[256,2048]{1,0:T(8,128)(2,1)} collective-permute-done((bf16[256,2048]{1,0:T(8,128)(2,1)}, bf16[256,2048]{1,0:T(8,128)(2,1)}, u32[]{:S(2)}, u32[]{:S(2)}) %collective-permute-start.7) | collective-permute-done | bytes 1048608 | tf_op jit(solution)/shard_map/ppermute | solution.py:20
  84.9 3.3 %fusion.20 = f32[512,1024]{1,0:T(8,128)} fusion(bf16[512,1024]{1,0:T(8,128)(2,1)} %collective-permute-done, bf16[1,512,2048]{2,1,0:T(8,128)(2,1)S(1)} %copy-done.6, s32[]{:T(128)S(6)} %select_n.87), kind=kOutput, calls=%fused_computation.45 | convolution fusion | flops 536870912 | bytes 3670020 | tf_op jit(solution)/shard_map/dot_general | solution.py:100
  96.2 12.6 %all-to-all-start.3 = ((bf16[64,8,1024]{2,1,0:T(8,128)(2,1)}), bf16[64,8,1024]{2,1,0:T(8,128)(2,1)}, u32[]{:S(2)}, u32[]{:S(2)}) async-start(bf16[64,8,1024]{2,1,0:T(8,128)(2,1)} %gather_fusion.1), calls=%async_computation.3 | async-start | bytes 2097152 | tf_op jit(solution)/shard_map/all_to_all | solution.py:52
  111.6 5.1 %multiply_convert_fusion.2 = bf16[512,1024]{1,0:T(8,128)(2,1)} fusion(f32[512,1024]{1,0:T(8,128)} %fusion.18, f32[512,1024]{1,0:T(8,128)} %fusion.24, f32[512,1024]{1,0:T(8,128)} %fusion.20, bf16[512,1024]{1,0:T(8,128)(2,1)} %collective-permute-done.2, bf16[1,512,2048]{2,1,0:T(8,128)(2,1)} %param.10, s32[]{:T(128)S(6)} %select_n.89), kind=kOutput, calls=%fused_computation.24 | convolution fusion | flops 539492352 | bytes 8912900 | tf_op jit(solution)/shard_map/dot_general | solution.py:100
  124.1 6.0 %fusion.62 = f32[16,64,512]{2,1,0:T(8,128)S(1)} fusion(bf16[512,16,64]{0,2,1:T(8,128)(2,1)S(1)} %bitcast.128, bf16[16,512,512]{2,1,0:T(8,128)(2,1)} %select_convert_fusion), kind=kOutput, calls=%fused_computation.97 | convolution fusion | flops 536870912 | bytes 11534336 | tf_op jit(solution)/shard_map/hts,shf->thf/dot_general | solution.py:113
  134.2 4.2 %collective-permute-done.4 = bf16[16,64,64]{1,2,0:T(8,128)(2,1)S(1)} collective-permute-done((bf16[16,64,64]{1,2,0:T(8,128)(2,1)S(1)}, bf16[16,64,64]{1,2,0:T(8,128)(2,1)S(1)}, u32[]{:S(2)}, u32[]{:S(2)}) %collective-permute-start.4) | collective-permute-done | bytes 131104 | tf_op jit(solution)/shard_map/ppermute | solution.py:20
  145.9 3.7 %fusion.39 = f32[256,2048]{1,0:T(8,128)} fusion(bf16[512,1024]{0,1:T(8,128)(2,1)S(1)} %bitcast.130, s32[]{:T(128)S(6)} %select_n.91, bf16[1,512,2048]{2,1,0:T(8,128)(2,1)} %param.13), kind=kOutput, calls=%fused_computation.68 | convolution fusion | flops 536870912 | bytes 4456452 | tf_op jit(solution)/shard_map/dot_general | solution.py:147
  152.1 4.6 %collective-permute-done.10 = bf16[16,64,64]{1,2,0:T(8,128)(2,1)S(1)} collective-permute-done((bf16[16,64,64]{1,2,0:T(8,128)(2,1)S(1)}, bf16[16,64,64]{1,2,0:T(8,128)(2,1)S(1)}, u32[]{:S(2)}, u32[]{:S(2)}) %collective-permute-start.10) | collective-permute-done | bytes 131104 | tf_op jit(solution)/shard_map/ppermute | solution.py:20
  158.3 3.7 %fusion.36 = f32[256,2048]{1,0:T(8,128)} fusion(bf16[512,1024]{0,1:T(8,128)(2,1)S(1)} %bitcast.132, s32[]{:T(128)S(6)} %select_n.93, bf16[1,512,2048]{2,1,0:T(8,128)(2,1)} %param.13), kind=kOutput, calls=%fused_computation.65 | convolution fusion | flops 536870912 | bytes 4456452 | tf_op jit(solution)/shard_map/dot_general | solution.py:147
  162.0 3.1 %fusion.16 = f32[512,1024]{1,0:T(8,128)} fusion(bf16[512,1024]{0,1:T(8,128)(2,1)S(1)} %bitcast.125, bf16[1,512,2048]{2,1,0:T(8,128)(2,1)} %param.10, s32[]{:T(128)S(6)} %select_n.88), kind=kOutput, calls=%fused_computation.41 | convolution fusion | flops 536870912 | bytes 3670020 | tf_op jit(solution)/shard_map/dot_general | solution.py:147
  165.1 11.9 %all-to-all-start.1 = ((bf16[64,8,1024]{2,1,0:T(8,128)(2,1)}), bf16[64,8,1024]{2,1,0:T(8,128)(2,1)S(1)}, u32[]{:S(2)}, u32[]{:S(2)}) async-start(bf16[64,8,1024]{2,1,0:T(8,128)(2,1)} %gather_fusion), calls=%async_computation.1 | async-start | bytes 2097152 | tf_op jit(solution)/shard_map/all_to_all | solution.py:52
  177.0 3.0 %fusion.5 = bf16[256,2048]{1,0:T(8,128)(2,1)S(1)} fusion(f32[256,2048]{1,0:T(8,128)} %fusion.36, bf16[512,2048]{1,0:T(8,128)(2,1)} %collective-permute-done.16, bf16[512,512]{0,1:T(8,128)(2,1)} %collective-permute-done.15, s32[]{:T(128)S(6)} %select_n.105), kind=kOutput, calls=%fused_computation.10 | convolution fusion | flops 538443776 | bytes 5505028 | tf_op jit(solution)/shard_map/dot_general | solution.py:148
  180.2 3.3 %fusion.22 = f32[512,1024]{1,0:T(8,128)} fusion(bf16[512,1024]{0,1:T(8,128)(2,1)S(1)} %bitcast.126, bf16[1,512,2048]{2,1,0:T(8,128)(2,1)} %param.10, s32[]{:T(128)S(6)} %select_n.86), kind=kOutput, calls=%fused_computation.47 | convolution fusion | flops 536870912 | bytes 3670020 | tf_op jit(solution)/shard_map/dot_general | solution.py:147
  187.6 3.1 %fusion.27 = f32[512,1024]{1,0:T(8,128)} fusion(bf16[512,1024]{0,1:T(8,128)(2,1)S(1)} %collective-permute-done.13, bf16[512,1024]{1,0:T(8,128)(2,1)} %collective-permute-done.12, s32[]{:T(128)S(6)} %select_n.99), kind=kOutput, calls=%fused_computation.52 | convolution fusion | flops 536870912 | bytes 3670020 | tf_op jit(solution)/shard_map/dot_general | solution.py:148
  192.4 20.5 %collective-permute-done.17 = bf16[256,2048]{1,0:T(8,128)(2,1)S(1)} collective-permute-done((bf16[256,2048]{1,0:T(8,128)(2,1)S(1)}, bf16[256,2048]{1,0:T(8,128)(2,1)S(1)}, u32[]{:S(2)}, u32[]{:S(2)}) %collective-permute-start.17) | collective-permute-done | bytes 1048608 | tf_op jit(solution)/shard_map/ppermute | solution.py:20
  212.9 3.8 %fusion.7 = bf16[1,256,2048]{2,1,0:T(8,128)(2,1)} fusion(f32[256,2048]{1,0:T(8,128)S(1)} %copy-done.3, bf16[512,2048]{1,0:T(8,128)(2,1)} %collective-permute-done.16, bf16[256,2048]{1,0:T(8,128)(2,1)S(1)} %collective-permute-done.17, f32[256,2048]{1,0:T(8,128)S(1)} %bitcast.129, f32[]{:T(128)S(6)} %sub.30, bf16[512,512]{0,1:T(8,128)(2,1)} %collective-permute-done.15, ...), kind=kOutput, calls=%fused_computation.12 | convolution fusion | flops 542113792 | bytes 9699336 | tf_op jit(solution)/shard_map/dot_general | solution.py:148
  216.7 18.8 %collective-permute-done.14 = bf16[512,1024]{1,0:T(8,128)(2,1)} collective-permute-done((bf16[512,1024]{1,0:T(8,128)(2,1)}, bf16[512,1024]{1,0:T(8,128)(2,1)}, u32[]{:S(2)}, u32[]{:S(2)}) %collective-permute-start.14) | collective-permute-done | bytes 1048608 | tf_op jit(solution)/shard_map/ppermute | solution.py:20
  235.5 4.7 %fusion.14 = bf16[1,512,1024]{2,1,0:T(8,128)(2,1)} fusion(bf16[512,1024]{1,0:T(8,128)(2,1)} %collective-permute-done.14, f32[512,1024]{1,0:T(8,128)} %fusion.22, f32[512,1024]{1,0:T(8,128)} %fusion.27, bf16[64,8,1024]{2,1,0:T(8,128)(2,1)S(1)} %all-to-all-done.1, f32[]{:T(128)S(6)} %div.26, f32[]{:T(128)S(6)} %sub.30, bf16[1,512,1024]{2,1,0:T(8,128)(2,1)} %param.14), kind=kLoop, calls=%fused_computation.35 | loop fusion | flops 6291456 | bytes 8388616 | tf_op jit(solution)/shard_map/broadcast_in_dim | solution.py:174
  (91 shorter events, 55.8 us)
Async XLA Ops:
  0.6 42.8 %all-to-all-start.2 = ((bf16[64,8,1024]{2,1,0:T(8,128)(2,1)}), bf16[64,8,1024]{2,1,0:T(8,128)(2,1)S(1)}, u32[]{:S(2)}, u32[]{:S(2)}) async-start(bf16[64,8,1024]{2,1,0:T(8,128)(2,1)} %bitcast.137), calls=%async_computation.2 | async-start | bytes 2097152 | tf_op jit(solution)/shard_map/all_to_all | solution.py:52
  15.9 53.6 %collective-permute-start.1 = (bf16[512,1024]{1,0:T(8,128)(2,1)}, bf16[512,1024]{1,0:T(8,128)(2,1)}, u32[]{:S(2)}, u32[]{:S(2)}) collective-permute-start(bf16[512,1024]{1,0:T(8,128)(2,1)} %bitcast.133), channel_id=1, source_target_pairs={{0,2},{2,0},{1,3},{3,1},{4,6},{6,4},{5,7},{7,5},{8,10},{10,8},{9,1... | collective-permute-start | bytes 3145736 | tf_op jit(solution)/shard_map/ppermute | solution.py:20
  16.3 58.2 %collective-permute-start = (bf16[512,1024]{1,0:T(8,128)(2,1)}, bf16[512,1024]{1,0:T(8,128)(2,1)}, u32[]{:S(2)}, u32[]{:S(2)}) collective-permute-start(bf16[512,1024]{1,0:T(8,128)(2,1)} %bitcast.134), channel_id=1, source_target_pairs={{0,1},{1,0},{2,3},{3,2},{4,5},{5,4},{6,7},{7,6},{8,9},{9,8},{10,11... | collective-permute-start | bytes 3145736 | tf_op jit(solution)/shard_map/ppermute | solution.py:20
  17.5 70.6 %collective-permute-start.6 = (bf16[256,2048]{1,0:T(8,128)(2,1)}, bf16[256,2048]{1,0:T(8,128)(2,1)}, u32[]{:S(2)}, u32[]{:S(2)}) collective-permute-start(bf16[256,2048]{1,0:T(8,128)(2,1)} %bitcast.135), channel_id=1, source_target_pairs={{0,1},{1,0},{2,3},{3,2},{4,5},{5,4},{6,7},{7,6},{8,9},{9,8},{10,11... | collective-permute-start | bytes 3145736 | tf_op jit(solution)/shard_map/ppermute | solution.py:20
  17.5 65.6 %collective-permute-start.7 = (bf16[256,2048]{1,0:T(8,128)(2,1)}, bf16[256,2048]{1,0:T(8,128)(2,1)}, u32[]{:S(2)}, u32[]{:S(2)}) collective-permute-start(bf16[256,2048]{1,0:T(8,128)(2,1)} %bitcast.136), channel_id=1, source_target_pairs={{0,2},{2,0},{1,3},{3,1},{4,6},{6,4},{5,7},{7,5},{8,10},{10,8},{9,1... | collective-permute-start | bytes 3145736 | tf_op jit(solution)/shard_map/ppermute | solution.py:20
  19.9 163.6 %collective-permute-start.12 = (bf16[512,1024]{1,0:T(8,128)(2,1)}, bf16[512,1024]{1,0:T(8,128)(2,1)}, u32[]{:S(2)}, u32[]{:S(2)}) collective-permute-start(bf16[512,1024]{1,0:T(8,128)(2,1)} %pad_maximum_fusion), channel_id=1, source_target_pairs={{0,1},{1,0},{2,3},{3,2},{4,5},{5,4},{6,7},{7,6},{8,9},{9,8},{10,11... | collective-permute-start | bytes 3145736 | tf_op jit(solution)/shard_map/ppermute | solution.py:20
  43.4 52.8 %all-to-all-start = ((bf16[64,8,1024]{2,1,0:T(8,128)(2,1)}), bf16[64,8,1024]{2,1,0:T(8,128)(2,1)}, u32[]{:S(2)}, u32[]{:S(2)}) async-start(bf16[64,8,1024]{2,1,0:T(8,128)(2,1)} %bitcast.138), calls=%async_computation | async-start | bytes 2097152 | tf_op jit(solution)/shard_map/all_to_all | solution.py:52
  69.5 42.1 %collective-permute-start.2 = (bf16[512,1024]{1,0:T(8,128)(2,1)}, bf16[512,1024]{1,0:T(8,128)(2,1)}, u32[]{:S(2)}, u32[]{:S(2)}) collective-permute-start(bf16[512,1024]{1,0:T(8,128)(2,1)} %collective-permute-done.1), channel_id=1, source_target_pairs={{0,1},{1,0},{2,3},{3,2},{4,5},{5,4},{6,7},{7,6},{8,9},{9,8},{10,11... | collective-permute-start | bytes 3145736 | tf_op jit(solution)/shard_map/ppermute | solution.py:20
  74.5 102.5 %collective-permute-start.16 = (bf16[512,2048]{1,0:T(8,128)(2,1)}, bf16[512,2048]{1,0:T(8,128)(2,1)}, u32[]{:S(2)}, u32[]{:S(2)}) collective-permute-start(bf16[512,2048]{1,0:T(8,128)(2,1)} %bitcast.15), channel_id=1, source_target_pairs={{0,1},{1,0},{2,3},{3,2},{4,5},{5,4},{6,7},{7,6},{8,9},{9,8},{10,11... | collective-permute-start | bytes 6291464 | tf_op jit(solution)/shard_map/ppermute | solution.py:20
  83.1 47.1 %collective-permute-start.8 = (bf16[256,2048]{1,0:T(8,128)(2,1)}, bf16[256,2048]{1,0:T(8,128)(2,1)}, u32[]{:S(2)}, u32[]{:S(2)}) collective-permute-start(bf16[256,2048]{1,0:T(8,128)(2,1)} %collective-permute-done.7), channel_id=1, source_target_pairs={{0,1},{1,0},{2,3},{3,2},{4,5},{5,4},{6,7},{7,6},{8,9},{9,8},{10,11... | collective-permute-start | bytes 3145736 | tf_op jit(solution)/shard_map/ppermute | solution.py:20
  96.2 68.9 %all-to-all-start.3 = ((bf16[64,8,1024]{2,1,0:T(8,128)(2,1)}), bf16[64,8,1024]{2,1,0:T(8,128)(2,1)}, u32[]{:S(2)}, u32[]{:S(2)}) async-start(bf16[64,8,1024]{2,1,0:T(8,128)(2,1)} %gather_fusion.1), calls=%async_computation.3 | async-start | bytes 2097152 | tf_op jit(solution)/shard_map/all_to_all | solution.py:52
  120.8 13.4 %collective-permute-start.5 = (bf16[16,64,64]{1,2,0:T(8,128)(2,1)S(1)}, bf16[16,64,64]{1,2,0:T(8,128)(2,1)S(1)}, u32[]{:S(2)}, u32[]{:S(2)}) collective-permute-start(bf16[16,64,64]{1,2,0:T(8,128)(2,1)S(1)} %fusion.12), channel_id=1, source_target_pairs={{0,3},{1,2},{4,7},{5,6},{8,11},{9,10},{12,15},{13,14},{16,19},{17,... | collective-permute-start | bytes 393224 | tf_op jit(solution)/shard_map/ppermute | solution.py:20
  122.8 15.6 %collective-permute-start.4 = (bf16[16,64,64]{1,2,0:T(8,128)(2,1)S(1)}, bf16[16,64,64]{1,2,0:T(8,128)(2,1)S(1)}, u32[]{:S(2)}, u32[]{:S(2)}) collective-permute-start(bf16[16,64,64]{1,2,0:T(8,128)(2,1)S(1)} %fusion.12), channel_id=1, source_target_pairs={{0,2},{1,3},{4,6},{5,7},{8,10},{9,11},{12,14},{13,15},{16,18},{17,... | collective-permute-start | bytes 393224 | tf_op jit(solution)/shard_map/ppermute | solution.py:20
  130.1 8.3 %collective-permute-start.3 = (bf16[16,64,64]{1,2,0:T(8,128)(2,1)S(1)}, bf16[16,64,64]{1,2,0:T(8,128)(2,1)S(1)}, u32[]{:S(2)}, u32[]{:S(2)}) collective-permute-start(bf16[16,64,64]{1,2,0:T(8,128)(2,1)S(1)} %fusion.12), channel_id=1, source_target_pairs={{0,1},{2,3},{4,5},{6,7},{8,9},{10,11},{12,13},{14,15},{16,17},{18,... | collective-permute-start | bytes 393224 | tf_op jit(solution)/shard_map/ppermute | solution.py:20
  140.8 11.3 %collective-permute-start.11 = (bf16[16,64,64]{1,2,0:T(8,128)(2,1)S(1)}, bf16[16,64,64]{1,2,0:T(8,128)(2,1)S(1)}, u32[]{:S(2)}, u32[]{:S(2)}) collective-permute-start(bf16[16,64,64]{1,2,0:T(8,128)(2,1)S(1)} %fusion.13), channel_id=1, source_target_pairs={{3,0},{2,1},{7,4},{6,5},{11,8},{10,9},{15,12},{14,13},{19,16},{18,... | collective-permute-start | bytes 393224 | tf_op jit(solution)/shard_map/ppermute | solution.py:20
  142.2 14.5 %collective-permute-start.10 = (bf16[16,64,64]{1,2,0:T(8,128)(2,1)S(1)}, bf16[16,64,64]{1,2,0:T(8,128)(2,1)S(1)}, u32[]{:S(2)}, u32[]{:S(2)}) collective-permute-start(bf16[16,64,64]{1,2,0:T(8,128)(2,1)S(1)} %fusion.13), channel_id=1, source_target_pairs={{2,0},{3,1},{6,4},{7,5},{10,8},{11,9},{14,12},{15,13},{18,16},{19,... | collective-permute-start | bytes 393224 | tf_op jit(solution)/shard_map/ppermute | solution.py:20
  143.5 13.2 %collective-permute-start.9 = (bf16[16,64,64]{1,2,0:T(8,128)(2,1)S(1)}, bf16[16,64,64]{1,2,0:T(8,128)(2,1)S(1)}, u32[]{:S(2)}, u32[]{:S(2)}) collective-permute-start(bf16[16,64,64]{1,2,0:T(8,128)(2,1)S(1)} %fusion.13), channel_id=1, source_target_pairs={{1,0},{3,2},{5,4},{7,6},{9,8},{11,10},{13,12},{15,14},{17,16},{19,... | collective-permute-start | bytes 393224 | tf_op jit(solution)/shard_map/ppermute | solution.py:20
  152.1 24.9 %collective-permute-start.15 = (bf16[512,512]{0,1:T(8,128)(2,1)}, bf16[512,512]{0,1:T(8,128)(2,1)}, u32[]{:S(2)}, u32[]{:S(2)}) collective-permute-start(bf16[512,512]{0,1:T(8,128)(2,1)} %pad_maximum_fusion.1), channel_id=1, source_target_pairs={{0,1},{1,0},{2,3},{3,2},{4,5},{5,4},{6,7},{7,6},{8,9},{9,8},{10,11... | collective-permute-start | bytes 1572872 | tf_op jit(solution)/shard_map/ppermute | solution.py:20
  157.2 26.3 %collective-permute-start.13 = (bf16[512,1024]{0,1:T(8,128)(2,1)S(1)}, bf16[512,1024]{0,1:T(8,128)(2,1)S(1)}, u32[]{:S(2)}, u32[]{:S(2)}) collective-permute-start(bf16[512,1024]{0,1:T(8,128)(2,1)S(1)} %bitcast.124), channel_id=1, source_target_pairs={{0,1},{1,0},{2,3},{3,2},{4,5},{5,4},{6,7},{7,6},{8,9},{9,8},{10,11... | collective-permute-start | bytes 3145736 | tf_op jit(solution)/shard_map/ppermute | solution.py:20
  165.1 51.6 %all-to-all-start.1 = ((bf16[64,8,1024]{2,1,0:T(8,128)(2,1)}), bf16[64,8,1024]{2,1,0:T(8,128)(2,1)S(1)}, u32[]{:S(2)}, u32[]{:S(2)}) async-start(bf16[64,8,1024]{2,1,0:T(8,128)(2,1)} %gather_fusion), calls=%async_computation.1 | async-start | bytes 2097152 | tf_op jit(solution)/shard_map/all_to_all | solution.py:52
  180.1 32.8 %collective-permute-start.17 = (bf16[256,2048]{1,0:T(8,128)(2,1)S(1)}, bf16[256,2048]{1,0:T(8,128)(2,1)S(1)}, u32[]{:S(2)}, u32[]{:S(2)}) collective-permute-start(bf16[256,2048]{1,0:T(8,128)(2,1)S(1)} %fusion.5), channel_id=1, source_target_pairs={{0,2},{2,0},{1,3},{3,1},{4,6},{6,4},{5,7},{7,5},{8,10},{10,8},{9,1... | collective-permute-start | bytes 3145736 | tf_op jit(solution)/shard_map/ppermute | solution.py:20
  186.3 49.2 %collective-permute-start.14 = (bf16[512,1024]{1,0:T(8,128)(2,1)}, bf16[512,1024]{1,0:T(8,128)(2,1)}, u32[]{:S(2)}, u32[]{:S(2)}) collective-permute-start(bf16[512,1024]{1,0:T(8,128)(2,1)} %multiply_convert_fusion), channel_id=1, source_target_pairs={{0,2},{2,0},{1,3},{3,1},{4,6},{6,4},{5,7},{7,5},{8,10},{10,8},{9,1... | collective-permute-start | bytes 3145736 | tf_op jit(solution)/shard_map/ppermute | solution.py:20
  190.8 22.2 %copy-start.3 = (f32[256,2048]{1,0:T(8,128)S(1)}, f32[256,2048]{1,0:T(8,128)}, u32[]{:S(2)}) copy-start(f32[256,2048]{1,0:T(8,128)} %fusion.39) | copy-start | bytes 6291460
  190.8 22.2 %copy-start.8 = (bf16[1,256,2048]{2,1,0:T(8,128)(2,1)S(1)}, bf16[1,256,2048]{2,1,0:T(8,128)(2,1)}, u32[]{:S(2)}) copy-start(bf16[1,256,2048]{2,1,0:T(8,128)(2,1)} %param.15) | copy-start | bytes 3145732
  (11 other events, 84.0 us)

commit v2 on v1

--- a/solution.py
+++ b/solution.py
@@ -2,6 +2,7 @@
 import jax.numpy as jnp
 from jax import lax
 from jax.sharding import PartitionSpec as P
+
 
 D = 2048
 HEADS = 16
@@ -27,8 +28,8 @@
 def state_sums(states, order):
     total = None
     for step in order:
-        piece = sent(states, step).astype(f32)
-        total = piece if total is None else total + piece
+        piece = sent(states, step)
+        total = piece.astype(f32) if total is None else total + piece.astype(f32)
     return total.astype(bf16)
 
 
@@ -36,29 +37,28 @@
 AFTER = ([(1, 0), (3, 2)], [(2, 0), (3, 1)], [(3, 0), (2, 1)])
 
 
-def pieces_of(value, output, count):
+def after(x, *others):
+    return lax.optimization_barrier((x, *others))[0]
+
+
+def swap(x):
+    return lax.all_to_all(x, "rep", split_axis=0, concat_axis=0, tiled=True)
+
+
+def packed_pieces(value, output, count):
     rows = value.shape[0] // count
     width = value.shape[1]
     value = value.reshape(count, rows, width)
     output = output.reshape(count // 2, rows, 2, width).transpose(0, 2, 1, 3)
-    return value, output.reshape(count, rows, width)
+    return jnp.concatenate([value, output.reshape(count, rows, width)], axis=1)
 
 
-def fetch_partner(stale_value, stale_output, partner):
-    count = lax.axis_size("rep")
-    value, output = pieces_of(stale_value, stale_output, count)
-
-    def swap(x):
-        return lax.all_to_all(x, "rep", split_axis=0, concat_axis=0, tiled=True)
-
-    def pick(x):
-        return x.at[partner].get(mode="promise_in_bounds", unique_indices=True)
-
-    value, output = swap(value), swap(output)
-    value, output = swap(pick(value)), swap(pick(output))
-    rows, width = value.shape[1:]
-    output = output.reshape(count // 2, 2, rows, width).transpose(0, 2, 1, 3)
-    return value.reshape(stale_value.shape), output.reshape(stale_output.shape)
+def unpacked(pieces, value_shape, output_shape):
+    count, rows, width = pieces.shape
+    rows //= 2
+    value = pieces[:, :rows].reshape(value_shape)
+    output = pieces[:, rows:].reshape(count // 2, 2, rows, width).transpose(0, 2, 1, 3)
+    return value, output.reshape(output_shape)
 
 
 def on_device(
@@ -78,13 +78,11 @@
     rows_v = weight_v.shape[0]
     rows_o = weight_o.shape[0]
 
+    replicas = lax.axis_size("rep")
     across_v = sent(weight_v, ACROSS)
     twin_v = sent(weight_v, TWIN)
     both_v = sent(across_v, TWIN)
-    across_o = sent(weight_o, ACROSS)
-    twin_o = sent(weight_o, TWIN)
-    both_o = sent(across_o, TWIN)
-    mate_value, mate_output = fetch_partner(stale_value[0], stale_output[0], partner)
+    spread = swap(packed_pieces(stale_value[0], stale_output[0], replicas))
 
     twin_features = sent(
         jnp.concatenate(
@@ -106,7 +104,11 @@
     key_heads = key_feat[0].reshape(positions, HEADS, HEAD)
     value_heads = values.reshape(positions, HEADS, HEAD)
     states = jnp.einsum("the,thf->hef", key_heads, value_heads, preferred_element_type=f32)
-    prior = state_sums(states.astype(bf16), BEFORE)
+    states = states.astype(bf16)
+    prior = state_sums(states, BEFORE)
+    across_o = sent(after(weight_o, states), ACROSS)
+    twin_o = sent(weight_o, TWIN)
+    both_o = sent(across_o, TWIN)
     causal = jnp.arange(positions)[:, None] >= jnp.arange(positions)[None, :]
     scores = jnp.einsum("the,she->hts", query_heads, key_heads, preferred_element_type=f32)
     scores = jnp.where(causal[None], scores, f32(0.0)).astype(bf16)
@@ -126,18 +128,11 @@
     d_attn = inverse * (upstream - unit * jnp.mean(unit * upstream, axis=-1, keepdims=True))
     d_attn = d_attn.astype(bf16)
     grad_states = jnp.einsum("the,thf->hef", query_heads, d_attn, preferred_element_type=f32)
-    later = state_sums(grad_states.astype(bf16), AFTER)
+    grad_states = grad_states.astype(bf16)
+    later = state_sums(grad_states, AFTER)
     d_values = jnp.einsum("hts,thf->shf", scores, d_attn, preferred_element_type=f32)
     d_values = d_values + jnp.einsum("she,hef->shf", key_heads, later, preferred_element_type=f32)
     d_values = d_values.astype(bf16).reshape(positions, width)
-
-    twin_normed = sent(
-        jnp.concatenate(
-            [column_block(normed, 1 - core, rows_o), column_block(normed, 3 - core, rows_o)],
-            axis=1,
-        ),
-        TWIN,
-    )
 
     def rows_grad(mine, right, twin, twin_right, width, scale):
         def term(block):
@@ -148,15 +143,29 @@
             both += lax.dot_general(other, twin_right, dims, preferred_element_type=f32)
             return both * scale
 
-        away = sent(term(rank ^ 2).astype(bf16), ACROSS)
-        return term(rank) + away.astype(f32)
+        away = term(rank ^ 2).astype(bf16)
+        back = sent(away, ACROSS)
+        return away, back, term(rank)
 
-    grad_output = rows_grad(
+    twin_normed = sent(
+        jnp.concatenate(
+            [column_block(normed, 1 - core, rows_o), column_block(normed, 3 - core, rows_o)],
+            axis=1,
+        ),
+        TWIN,
+    )
+    away_o, back_o, own_o = rows_grad(
         normed, upstream_rows, twin_normed, twin_rows, rows_o, scale_output
     )
-    grad_value = rows_grad(
+    grad_output = own_o + back_o.astype(f32)
+    picked = after(spread, grad_states, away_o).at[partner].get(
+        mode="promise_in_bounds", unique_indices=True
+    )
+    mate_value, mate_output = unpacked(swap(picked), weight_v.shape, weight_o.shape)
+    _, back_v, own_v = rows_grad(
         features, d_values, twin_features, sent(d_values, TWIN), rows_v, scale_value
     )
+    grad_value = own_v + back_v.astype(f32)
     replica = lax.axis_index("rep")
     own_count = step_counts[replica].astype(f32)
     mate_count = step_counts[partner[replica]].astype(f32)
@@ -176,6 +185,7 @@
 
 def solution(mesh):
     placed = (P("rep", "seq", None),) * 8 + (P(), P())
+
     return jax.shard_map(
         on_device,
         mesh=mesh,

time: 241 us -> 215 us (0.89)
  matrix products: 68.6 us -> 53.6 us
  starting transfers between devices: 67.5 us -> 54.4 us
  waiting for transfers between devices: 76.5 us -> 79 us
    all_to_all x4 -> x2, starting transfers between devices: 48 us -> 28.3 us  [swap(): return lax.all_to_all(x, 'rep', split_axis=0, concat_axis=0, tiled=True)]
    ppermute x18, waiting for transfers between devices: 56.7 us -> 76.4 us  [sent(): return lax.ppermute(x, 'seq', pairs)]
    all_to_all x4 -> x2, waiting for transfers between devices: 19.7 us -> 2.56 us  [swap(): return lax.all_to_all(x, 'rep', split_axis=0, concat_axis=0, tiled=True)]
    ppermute x18, starting transfers between devices: 19.5 us -> 26.1 us  [sent(): return lax.ppermute(x, 'seq', pairs)]
    dot_general x4, matrix products: 15.2 us -> 8.85 us  [on_device(): jnp.dot(column_block(features, rank ^ step, rows_v), block, preferred_ele...]
    dot_general x4, matrix products: 13.8 us -> 9.86 us  [term(): both = lax.dot_general(left, right, dims, preferred_element_type=f32)]
    dot_general x1, matrix products: 1.55 us -> 4.94 us  [on_device(): jnp.einsum('hts,thf->shf', scores, d_attn, preferred_element_type=f32)]
    dot_general x1, matrix products: 6 us -> 2.64 us  [on_device(): jnp.einsum('hts,shf->thf', scores, value_heads, preferred_element_type=f32)]
  transfers between devices with their start and end apart: 22 -> 20, of which waited for: 6 -> 9; matrix products, arithmetic and copies ran while one was open for 36% -> 31% of each run, Pallas kernels for 0% -> 0%
where the time goes in v2:
time: 215 us; the launch traced here: 214 us
  waiting for transfers between devices  79 us (37%)
  starting transfers between devices  54.4 us (25%)
  matrix products  53.6 us (25%)
  local copies, waits for them, and re-layouts  11.5 us (5%)
  other arithmetic  11.3 us (5%)
  between operations  4.46 us (2%)
    ppermute x18, waiting for transfers between devices, sent(): return lax.ppermute(x, 'seq', pairs)  76.4 us
    all_to_all x2, starting transfers between devices, swap(): return lax.all_to_all(x, 'rep', split_axis=0, concat_axis=0, tiled=True)  28.3 us
    ppermute x18, starting transfers between devices, sent(): return lax.ppermute(x, 'seq', pairs)  26.1 us
    dot_general x4, matrix products, on_device(): lax.dot_general(upstream_rows, block, (((1,), (1,)), ((), ())), preferred...  12 us
    dot_general x4, matrix products, term(): both += lax.dot_general(other, twin_right, dims, preferred_element_type=f32)  11.1 us
    dot_general x4, matrix products, term(): both = lax.dot_general(left, right, dims, preferred_element_type=f32)  9.86 us
    dot_general x4, matrix products, on_device(): jnp.dot(column_block(features, rank ^ step, rows_v), block, preferred_ele...  8.85 us
    dot_general x1, matrix products, on_device(): jnp.einsum('hts,thf->shf', scores, d_attn, preferred_element_type=f32)  4.94 us
  transfers between devices with their start and end apart: 20, of which 9 were waited for; matrix products, arithmetic and copies ran while one was open for 31% of the time, Pallas kernels for 0%

profile of v2, /device:TPU:1, one launch (start us, length us, event | category | flops | bytes accessed | tf_op | source)
XLA Modules:
  0.0 214.3 jit_solution(6695797670251776962)
XLA Ops:
  4.1 3.1 %pad_maximum_fusion = bf16[64,16,1024]{2,1,0:T(8,128)(2,1)} fusion(bf16[64,8,1024]{2,1,0:T(8,128)(2,1)} %bitcast.143, bf16[64,8,1024]{2,1,0:T(8,128)(2,1)} %bitcast.144), kind=kLoop, calls=%fused_computation.12 | loop fusion | flops 4194304 | bytes 4194304 | tf_op jit(solution)/shard_map/concatenate | solution.py:53
  7.2 14.0 %all-to-all-start = ((bf16[64,16,1024]{2,1,0:T(8,128)(2,1)}), bf16[64,16,1024]{2,1,0:T(8,128)(2,1)}, u32[]{:S(2)}, u32[]{:S(2)}) async-start(bf16[64,16,1024]{2,1,0:T(8,128)(2,1)} %pad_maximum_fusion), calls=%async_computation | async-start | bytes 4194304 | tf_op jit(solution)/shard_map/all_to_all | solution.py:45
  22.1 2.8 %collective-permute-done.1 = bf16[512,1024]{1,0:T(8,128)(2,1)} collective-permute-done((bf16[512,1024]{1,0:T(8,128)(2,1)}, bf16[512,1024]{1,0:T(8,128)(2,1)}, u32[]{:S(2)}, u32[]{:S(2)}) %collective-permute-start.1) | collective-permute-done | bytes 1048608 | tf_op jit(solution)/shard_map/ppermute | solution.py:21
  24.9 7.1 %collective-permute-start.2 = (bf16[512,1024]{1,0:T(8,128)(2,1)}, bf16[512,1024]{1,0:T(8,128)(2,1)}, u32[]{:S(2)}, u32[]{:S(2)}) collective-permute-start(bf16[512,1024]{1,0:T(8,128)(2,1)} %collective-permute-done.1), channel_id=1, source_target_pairs={{0,1},{1,0},{2,3},{3,2},{4,5},{5,4},{6,7},{7,6},{8,9},{9,8},{10,11... | collective-permute-start | bytes 3145736 | tf_op jit(solution)/shard_map/ppermute | solution.py:21
  40.1 3.1 %multiply_convert_fusion.2 = bf16[512,1024]{1,0:T(8,128)(2,1)} fusion(f32[512,1024]{1,0:T(8,128)S(1)} %fusion.20, f32[512,1024]{1,0:T(8,128)S(1)} %fusion.26, f32[512,1024]{1,0:T(8,128)S(1)} %fusion.22, bf16[512,1024]{1,0:T(8,128)(2,1)} %collective-permute-done.2, bf16[1,512,2048]{2,1,0:T(8,128)(2,1)S(1)} %copy-done.2, s32[]{:T(128)S(6)} %select_n.87), kind=kOutput, calls=%fused_computation.24 | convolution fusion | flops 539492352 | bytes 8912900 | tf_op jit(solution)/shard_map/dot_general | solution.py:98
  47.5 2.3 %convolution_dynamic-update-slice_fusion.1 = f32[512,1024]{0,1:T(8,128)S(1)} fusion(f32[512,1024]{0,1:T(8,128)S(1)} %broadcast_in_dim.31, s32[]{:T(128)S(6)} %select_n.89, bf16[1,256,2048]{2,1,0:T(8,128)(2,1)S(1)} %copy-done.8, bf16[1,512,2048]{2,1,0:T(8,128)(2,1)} %param.13), kind=kOutput, calls=%fused_computation.28 | convolution fusion | flops 536870912 | bytes 3670020 | tf_op jit(solution)/shard_map/dot_general | solution.py:123
  49.9 2.4 %select_convert_fusion = bf16[16,512,512]{2,1,0:T(8,128)(2,1)S(1)} fusion(bf16[512,16,64]{0,2,1:T(8,128)(2,1)S(1)} %bitcast.127, bf16[512,16,64]{0,2,1:T(8,128)(2,1)S(1)} %bitcast.125, pred[512,512]{1,0:T(8,128)(4,1)S(1)} %iota_compare_fusion), kind=kOutput, calls=%fused_computation.1 | convolution fusion | flops 545259520 | bytes 10747904 | tf_op jit(solution)/shard_map/the,she->hts/dot_general | solution.py:113
  52.3 5.0 %convolution_dynamic-update-slice_fusion = f32[512,1024]{0,1:T(8,128)S(1)} fusion(f32[512,1024]{0,1:T(8,128)S(1)} %convolution_dynamic-update-slice_fusion.1, s32[]{:T(128)S(6)} %select_n.90, bf16[256,2048]{1,0:T(8,128)(2,1)} %collective-permute-done.6, bf16[1,512,2048]{2,1,0:T(8,128)(2,1)} %param.13), kind=kOutput, calls=%fused_computation.27 | convolution fusion | flops 536870912 | bytes 3670020 | tf_op jit(solution)/shard_map/dot_general | solution.py:123
  62.2 17.3 %collective-permute-done.7 = bf16[256,2048]{1,0:T(8,128)(2,1)S(1)} collective-permute-done((bf16[256,2048]{1,0:T(8,128)(2,1)S(1)}, bf16[256,2048]{1,0:T(8,128)(2,1)S(1)}, u32[]{:S(2)}, u32[]{:S(2)}) %collective-permute-start.7) | collective-permute-done | bytes 1048608 | tf_op jit(solution)/shard_map/ppermute | solution.py:21
  80.1 2.6 %fusion.64 = f32[16,64,512]{2,1,0:T(8,128)S(1)} fusion(bf16[512,16,64]{0,2,1:T(8,128)(2,1)S(1)} %bitcast.134, bf16[16,512,512]{2,1,0:T(8,128)(2,1)S(1)} %select_convert_fusion), kind=kOutput, calls=%fused_computation.99 | convolution fusion | flops 536870912 | bytes 11534336 | tf_op jit(solution)/shard_map/hts,shf->thf/dot_general | solution.py:115
  84.3 5.6 %collective-permute-done.4 = bf16[16,64,64]{1,2,0:T(8,128)(2,1)S(1)} collective-permute-done((bf16[16,64,64]{1,2,0:T(8,128)(2,1)S(1)}, bf16[16,64,64]{1,2,0:T(8,128)(2,1)S(1)}, u32[]{:S(2)}, u32[]{:S(2)}) %collective-permute-start.4) | collective-permute-done | bytes 131104 | tf_op jit(solution)/shard_map/ppermute | solution.py:21
  100.9 3.4 %fusion.5 = bf16[256,2048]{1,0:T(8,128)(2,1)} fusion(f32[256,2048]{1,0:T(8,128)S(1)} %fusion.41, bf16[512,2048]{1,0:T(8,128)(2,1)} %collective-permute-done.10, bf16[512,512]{0,1:T(8,128)(2,1)S(1)} %collective-permute-done.9, s32[]{:T(128)S(6)} %select_n.97), kind=kOutput, calls=%fused_computation.9 | convolution fusion | flops 538443776 | bytes 5505028 | tf_op jit(solution)/shard_map/dot_general | solution.py:143
  104.3 3.6 %gather_fusion = bf16[64,16,1024]{2,1,0:T(8,128)(2,1)} fusion(bf16[64,16,1024]{2,1,0:T(8,128)(2,1)} %all-to-all-done, s32[1024]{0:T(1024)S(1)} %pad_clamp_fusion), kind=kCustom, calls=%fused_computation | custom fusion | bytes 4194560 | tf_op jit(solution)/shard_map/gather | solution.py:161
  107.8 14.3 %all-to-all-start.1 = ((bf16[64,16,1024]{2,1,0:T(8,128)(2,1)}), bf16[64,16,1024]{2,1,0:T(8,128)(2,1)}, u32[]{:S(2)}, u32[]{:S(2)}) async-start(bf16[64,16,1024]{2,1,0:T(8,128)(2,1)} %gather_fusion), calls=%async_computation.1 | async-start | bytes 4194304 | tf_op jit(solution)/shard_map/all_to_all | solution.py:45
  129.7 4.9 %fusion.65 = f32[16,64,512]{2,1,0:T(8,128)S(1)} fusion(bf16[512,16,64]{0,2,1:T(8,128)(2,1)S(1)} %get-tuple-element.7, bf16[16,512,512]{2,1,0:T(8,128)(2,1)} %copy-done), kind=kOutput, calls=%fused_computation.100 | convolution fusion | flops 536870912 | bytes 11534336 | tf_op jit(solution)/shard_map/hts,thf->shf/dot_general | solution.py:133
  134.6 6.3 %collective-permute-done.13 = bf16[16,64,64]{1,2,0:T(8,128)(2,1)S(1)} collective-permute-done((bf16[16,64,64]{1,2,0:T(8,128)(2,1)S(1)}, bf16[16,64,64]{1,2,0:T(8,128)(2,1)S(1)}, u32[]{:S(2)}, u32[]{:S(2)}) %collective-permute-start.13) | collective-permute-done | bytes 131104 | tf_op jit(solution)/shard_map/ppermute | solution.py:21
  140.9 9.4 %collective-permute-done.12 = bf16[16,64,64]{1,2,0:T(8,128)(2,1)S(1)} collective-permute-done((bf16[16,64,64]{1,2,0:T(8,128)(2,1)S(1)}, bf16[16,64,64]{1,2,0:T(8,128)(2,1)S(1)}, u32[]{:S(2)}, u32[]{:S(2)}) %collective-permute-start.12) | collective-permute-done | bytes 131104 | tf_op jit(solution)/shard_map/ppermute | solution.py:21
  159.4 2.4 %fusion.38 = f32[256,2048]{1,0:T(8,128)S(1)} fusion(bf16[512,1024]{0,1:T(8,128)(2,1)} %bitcast.138, s32[]{:T(128)S(6)} %select_n.89, bf16[1,512,2048]{2,1,0:T(8,128)(2,1)} %param.13), kind=kOutput, calls=%fused_computation.67 | convolution fusion | flops 536870912 | bytes 4456452 | tf_op jit(solution)/shard_map/dot_general | solution.py:142
  161.8 3.3 %fusion.24 = f32[512,1024]{1,0:T(8,128)} fusion(bf16[512,1024]{0,1:T(8,128)(2,1)S(1)} %bitcast.132, bf16[1,512,2048]{2,1,0:T(8,128)(2,1)} %param.10, s32[]{:T(128)S(6)} %select_n.84), kind=kOutput, calls=%fused_computation.49 | convolution fusion | flops 536870912 | bytes 3670020 | tf_op jit(solution)/shard_map/dot_general | solution.py:142
  168.7 2.6 %all-to-all-done.1 = bf16[64,16,1024]{2,1,0:T(8,128)(2,1)} async-done(((bf16[64,16,1024]{2,1,0:T(8,128)(2,1)}), bf16[64,16,1024]{2,1,0:T(8,128)(2,1)}, u32[]{:S(2)}, u32[]{:S(2)}) %all-to-all-start.1) | async-done | bytes 2097184 | tf_op jit(solution)/shard_map/all_to_all | solution.py:45
  173.0 15.0 %collective-permute-done.16 = bf16[512,1024]{1,0:T(8,128)(2,1)} collective-permute-done((bf16[512,1024]{1,0:T(8,128)(2,1)}, bf16[512,1024]{1,0:T(8,128)(2,1)}, u32[]{:S(2)}, u32[]{:S(2)}) %collective-permute-start.16) | collective-permute-done | bytes 1048608 | tf_op jit(solution)/shard_map/ppermute | solution.py:21
  187.9 4.1 %fusion.16 = bf16[1,512,1024]{2,1,0:T(8,128)(2,1)} fusion(bf16[512,1024]{1,0:T(8,128)(2,1)} %collective-permute-done.16, f32[512,1024]{1,0:T(8,128)S(1)} %copy-done.1, f32[512,1024]{1,0:T(8,128)} %fusion.29, bf16[64,16,1024]{2,1,0:T(8,128)(2,1)} %all-to-all-done.1, f32[]{:T(128)S(6)} %div.26, f32[]{:T(128)S(6)} %sub.30, bf16[1,512,1024]{2,1,0:T(8,128)(2,1)S(1)} %copy-done.5), kind=kLoop, calls=%fused_computation.37 | loop fusion | flops 6291456 | bytes 8388616 | tf_op jit(solution)/shard_map/broadcast_in_dim | solution.py:183
  192.0 18.4 %collective-permute-done.17 = bf16[256,2048]{1,0:T(8,128)(2,1)} collective-permute-done((bf16[256,2048]{1,0:T(8,128)(2,1)}, bf16[256,2048]{1,0:T(8,128)(2,1)}, u32[]{:S(2)}, u32[]{:S(2)}) %collective-permute-start.17) | collective-permute-done | bytes 1048608 | tf_op jit(solution)/shard_map/ppermute | solution.py:21
  210.4 3.9 %fusion.7 = bf16[1,256,2048]{2,1,0:T(8,128)(2,1)} fusion(f32[256,2048]{1,0:T(8,128)S(1)} %fusion.38, bf16[512,2048]{1,0:T(8,128)(2,1)} %collective-permute-done.10, bf16[256,2048]{1,0:T(8,128)(2,1)} %collective-permute-done.17, f32[256,2048]{1,0:T(8,128)S(1)} %bitcast.135, f32[]{:T(128)S(6)} %sub.30, bf16[512,512]{0,1:T(8,128)(2,1)S(1)} %copy-done.14, ...), kind=kOutput, calls=%fused_computation.11 | convolution fusion | flops 542113792 | bytes 9699336 | tf_op jit(solution)/shard_map/dot_general | solution.py:143
  (94 shorter events, 52.9 us)
Async XLA Ops:
  0.6 24.3 %collective-permute-start.1 = (bf16[512,1024]{1,0:T(8,128)(2,1)}, bf16[512,1024]{1,0:T(8,128)(2,1)}, u32[]{:S(2)}, u32[]{:S(2)}) collective-permute-start(bf16[512,1024]{1,0:T(8,128)(2,1)} %bitcast.139), channel_id=1, source_target_pairs={{0,2},{2,0},{1,3},{3,1},{4,6},{6,4},{5,7},{7,5},{8,10},{10,8},{9,1... | collective-permute-start | bytes 3145736 | tf_op jit(solution)/shard_map/ppermute | solution.py:21
  2.7 35.4 %collective-permute-start = (bf16[512,1024]{1,0:T(8,128)(2,1)}, bf16[512,1024]{1,0:T(8,128)(2,1)}, u32[]{:S(2)}, u32[]{:S(2)}) collective-permute-start(bf16[512,1024]{1,0:T(8,128)(2,1)} %bitcast.140), channel_id=1, source_target_pairs={{0,1},{1,0},{2,3},{3,2},{4,5},{5,4},{6,7},{7,6},{8,9},{9,8},{10,11... | collective-permute-start | bytes 3145736 | tf_op jit(solution)/shard_map/ppermute | solution.py:21
  4.0 48.3 %collective-permute-start.6 = (bf16[256,2048]{1,0:T(8,128)(2,1)}, bf16[256,2048]{1,0:T(8,128)(2,1)}, u32[]{:S(2)}, u32[]{:S(2)}) collective-permute-start(bf16[256,2048]{1,0:T(8,128)(2,1)} %bitcast.141), channel_id=1, source_target_pairs={{0,1},{1,0},{2,3},{3,2},{4,5},{5,4},{6,7},{7,6},{8,9},{9,8},{10,11... | collective-permute-start | bytes 3145736 | tf_op jit(solution)/shard_map/ppermute | solution.py:21
  7.2 24.8 %copy-start.10 = (bf16[1,512,1024]{2,1,0:T(8,128)(2,1)S(1)}, bf16[1,512,1024]{2,1,0:T(8,128)(2,1)}, u32[]{:S(2)}) copy-start(bf16[1,512,1024]{2,1,0:T(8,128)(2,1)} %param.11) | copy-start | bytes 3145732
  7.2 97.0 %all-to-all-start = ((bf16[64,16,1024]{2,1,0:T(8,128)(2,1)}), bf16[64,16,1024]{2,1,0:T(8,128)(2,1)}, u32[]{:S(2)}, u32[]{:S(2)}) async-start(bf16[64,16,1024]{2,1,0:T(8,128)(2,1)} %pad_maximum_fusion), calls=%async_computation | async-start | bytes 4194304 | tf_op jit(solution)/shard_map/all_to_all | solution.py:45
  21.2 78.9 %collective-permute-start.10 = (bf16[512,2048]{1,0:T(8,128)(2,1)}, bf16[512,2048]{1,0:T(8,128)(2,1)}, u32[]{:S(2)}, u32[]{:S(2)}) collective-permute-start(bf16[512,2048]{1,0:T(8,128)(2,1)} %bitcast.17), channel_id=1, source_target_pairs={{0,1},{1,0},{2,3},{3,2},{4,5},{5,4},{6,7},{7,6},{8,9},{9,8},{10,11... | collective-permute-start | bytes 6291464 | tf_op jit(solution)/shard_map/ppermute | solution.py:21
  24.9 15.2 %collective-permute-start.2 = (bf16[512,1024]{1,0:T(8,128)(2,1)}, bf16[512,1024]{1,0:T(8,128)(2,1)}, u32[]{:S(2)}, u32[]{:S(2)}) collective-permute-start(bf16[512,1024]{1,0:T(8,128)(2,1)} %collective-permute-done.1), channel_id=1, source_target_pairs={{0,1},{1,0},{2,3},{3,2},{4,5},{5,4},{6,7},{7,6},{8,9},{9,8},{10,11... | collective-permute-start | bytes 3145736 | tf_op jit(solution)/shard_map/ppermute | solution.py:21
  45.9 33.6 %collective-permute-start.7 = (bf16[256,2048]{1,0:T(8,128)(2,1)S(1)}, bf16[256,2048]{1,0:T(8,128)(2,1)S(1)}, u32[]{:S(2)}, u32[]{:S(2)}) collective-permute-start(bf16[256,2048]{1,0:T(8,128)(2,1)S(1)} %bitcast.142), channel_id=1, source_target_pairs={{0,2},{2,0},{1,3},{3,1},{4,6},{6,4},{5,7},{7,5},{8,10},{10,8},{9,1... | collective-permute-start | bytes 3145736 | tf_op jit(solution)/shard_map/ppermute | solution.py:21
  52.3 30.4 %copy-start = (bf16[16,512,512]{2,1,0:T(8,128)(2,1)}, bf16[16,512,512]{2,1,0:T(8,128)(2,1)S(1)}, u32[]{:S(2)}) copy-start(bf16[16,512,512]{2,1,0:T(8,128)(2,1)S(1)} %select_convert_fusion) | copy-start | bytes 25165828
  57.3 27.0 %collective-permute-start.5 = (bf16[16,64,64]{1,2,0:T(8,128)(2,1)S(1)}, bf16[16,64,64]{1,2,0:T(8,128)(2,1)S(1)}, u32[]{:S(2)}, u32[]{:S(2)}) collective-permute-start(bf16[16,64,64]{1,2,0:T(8,128)(2,1)S(1)} %fusion.14), channel_id=1, source_target_pairs={{0,3},{1,2},{4,7},{5,6},{8,11},{9,10},{12,15},{13,14},{16,19},{17,... | collective-permute-start | bytes 393224 | tf_op jit(solution)/shard_map/ppermute | solution.py:21
  59.6 30.3 %collective-permute-start.4 = (bf16[16,64,64]{1,2,0:T(8,128)(2,1)S(1)}, bf16[16,64,64]{1,2,0:T(8,128)(2,1)S(1)}, u32[]{:S(2)}, u32[]{:S(2)}) collective-permute-start(bf16[16,64,64]{1,2,0:T(8,128)(2,1)S(1)} %fusion.14), channel_id=1, source_target_pairs={{0,2},{1,3},{4,6},{5,7},{8,10},{9,11},{12,14},{13,15},{16,18},{17,... | collective-permute-start | bytes 393224 | tf_op jit(solution)/shard_map/ppermute | solution.py:21
  60.9 29.0 %collective-permute-start.3 = (bf16[16,64,64]{1,2,0:T(8,128)(2,1)S(1)}, bf16[16,64,64]{1,2,0:T(8,128)(2,1)S(1)}, u32[]{:S(2)}, u32[]{:S(2)}) collective-permute-start(bf16[16,64,64]{1,2,0:T(8,128)(2,1)S(1)} %fusion.14), channel_id=1, source_target_pairs={{0,1},{2,3},{4,5},{6,7},{8,9},{10,11},{12,13},{14,15},{16,17},{18,... | collective-permute-start | bytes 393224 | tf_op jit(solution)/shard_map/ppermute | solution.py:21
  79.5 13.3 %collective-permute-start.8 = (bf16[256,2048]{1,0:T(8,128)(2,1)S(1)}, bf16[256,2048]{1,0:T(8,128)(2,1)S(1)}, u32[]{:S(2)}, u32[]{:S(2)}) collective-permute-start(bf16[256,2048]{1,0:T(8,128)(2,1)S(1)} %collective-permute-done.7), channel_id=1, source_target_pairs={{0,1},{1,0},{2,3},{3,2},{4,5},{5,4},{6,7},{7,6},{8,9},{9,8},{10,11... | collective-permute-start | bytes 3145736 | tf_op jit(solution)/shard_map/ppermute | solution.py:21
  96.6 3.5 %collective-permute-start.9 = (bf16[512,512]{0,1:T(8,128)(2,1)S(1)}, bf16[512,512]{0,1:T(8,128)(2,1)S(1)}, u32[]{:S(2)}, u32[]{:S(2)}) collective-permute-start(bf16[512,512]{0,1:T(8,128)(2,1)S(1)} %pad_maximum_fusion.2), channel_id=1, source_target_pairs={{0,1},{1,0},{2,3},{3,2},{4,5},{5,4},{6,7},{7,6},{8,9},{9,8},{10,11... | collective-permute-start | bytes 1572872 | tf_op jit(solution)/shard_map/ppermute | solution.py:21
  107.8 63.4 %all-to-all-start.1 = ((bf16[64,16,1024]{2,1,0:T(8,128)(2,1)}), bf16[64,16,1024]{2,1,0:T(8,128)(2,1)}, u32[]{:S(2)}, u32[]{:S(2)}) async-start(bf16[64,16,1024]{2,1,0:T(8,128)(2,1)} %gather_fusion), calls=%async_computation.1 | async-start | bytes 4194304 | tf_op jit(solution)/shard_map/all_to_all | solution.py:45
  124.5 33.1 %collective-permute-start.14 = (bf16[512,1024]{1,0:T(8,128)(2,1)}, bf16[512,1024]{1,0:T(8,128)(2,1)S(1)}, u32[]{:S(2)}, u32[]{:S(2)}) collective-permute-start(bf16[512,1024]{1,0:T(8,128)(2,1)} %pad_maximum_fusion.1), channel_id=1, source_target_pairs={{0,1},{1,0},{2,3},{3,2},{4,5},{5,4},{6,7},{7,6},{8,9},{9,8},{10,11... | collective-permute-start | bytes 3145736 | tf_op jit(solution)/shard_map/ppermute | solution.py:21
  125.2 15.8 %collective-permute-start.13 = (bf16[16,64,64]{1,2,0:T(8,128)(2,1)S(1)}, bf16[16,64,64]{1,2,0:T(8,128)(2,1)S(1)}, u32[]{:S(2)}, u32[]{:S(2)}) collective-permute-start(bf16[16,64,64]{1,2,0:T(8,128)(2,1)S(1)} %fusion.15), channel_id=1, source_target_pairs={{3,0},{2,1},{7,4},{6,5},{11,8},{10,9},{15,12},{14,13},{19,16},{18,... | collective-permute-start | bytes 393224 | tf_op jit(solution)/shard_map/ppermute | solution.py:21
  126.5 23.9 %collective-permute-start.12 = (bf16[16,64,64]{1,2,0:T(8,128)(2,1)S(1)}, bf16[16,64,64]{1,2,0:T(8,128)(2,1)S(1)}, u32[]{:S(2)}, u32[]{:S(2)}) collective-permute-start(bf16[16,64,64]{1,2,0:T(8,128)(2,1)S(1)} %fusion.15), channel_id=1, source_target_pairs={{2,0},{3,1},{6,4},{7,5},{10,8},{11,9},{14,12},{15,13},{18,16},{19,... | collective-permute-start | bytes 393224 | tf_op jit(solution)/shard_map/ppermute | solution.py:21
  127.8 22.6 %collective-permute-start.11 = (bf16[16,64,64]{1,2,0:T(8,128)(2,1)S(1)}, bf16[16,64,64]{1,2,0:T(8,128)(2,1)S(1)}, u32[]{:S(2)}, u32[]{:S(2)}) collective-permute-start(bf16[16,64,64]{1,2,0:T(8,128)(2,1)S(1)} %fusion.15), channel_id=1, source_target_pairs={{1,0},{3,2},{5,4},{7,6},{9,8},{11,10},{13,12},{15,14},{17,16},{19,... | collective-permute-start | bytes 393224 | tf_op jit(solution)/shard_map/ppermute | solution.py:21
  150.8 6.8 %collective-permute-start.15 = (bf16[512,1024]{0,1:T(8,128)(2,1)S(1)}, bf16[512,1024]{0,1:T(8,128)(2,1)S(1)}, u32[]{:S(2)}, u32[]{:S(2)}) collective-permute-start(bf16[512,1024]{0,1:T(8,128)(2,1)S(1)} %bitcast.130), channel_id=1, source_target_pairs={{0,1},{1,0},{2,3},{3,2},{4,5},{5,4},{6,7},{7,6},{8,9},{9,8},{10,11... | collective-permute-start | bytes 3145736 | tf_op jit(solution)/shard_map/ppermute | solution.py:21
  159.4 28.5 %collective-permute-start.16 = (bf16[512,1024]{1,0:T(8,128)(2,1)}, bf16[512,1024]{1,0:T(8,128)(2,1)}, u32[]{:S(2)}, u32[]{:S(2)}) collective-permute-start(bf16[512,1024]{1,0:T(8,128)(2,1)} %multiply_convert_fusion), channel_id=1, source_target_pairs={{0,2},{2,0},{1,3},{3,1},{4,6},{6,4},{5,7},{7,5},{8,10},{10,8},{9,1... | collective-permute-start | bytes 3145736 | tf_op jit(solution)/shard_map/ppermute | solution.py:21
  165.2 45.2 %collective-permute-start.17 = (bf16[256,2048]{1,0:T(8,128)(2,1)}, bf16[256,2048]{1,0:T(8,128)(2,1)}, u32[]{:S(2)}, u32[]{:S(2)}) collective-permute-start(bf16[256,2048]{1,0:T(8,128)(2,1)} %fusion.5), channel_id=1, source_target_pairs={{0,2},{2,0},{1,3},{3,1},{4,6},{6,4},{5,7},{7,5},{8,10},{10,8},{9,1... | collective-permute-start | bytes 3145736 | tf_op jit(solution)/shard_map/ppermute | solution.py:21
  172.9 37.5 %copy-start.9 = (bf16[1,256,2048]{2,1,0:T(8,128)(2,1)S(1)}, bf16[1,256,2048]{2,1,0:T(8,128)(2,1)}, u32[]{:S(2)}) copy-start(bf16[1,256,2048]{2,1,0:T(8,128)(2,1)} %param.15) | copy-start | bytes 3145732
  172.9 37.5 %copy-start.14 = (bf16[512,512]{0,1:T(8,128)(2,1)S(1)}, bf16[512,512]{0,1:T(8,128)(2,1)}, u32[]{:S(2)}) copy-start(bf16[512,512]{0,1:T(8,128)(2,1)} %copy-done.13) | copy-start | bytes 1572868
  (13 other events, 90.6 us)

commit v3 on v2

--- a/solution.py
+++ b/solution.py
@@ -45,20 +45,20 @@
     return lax.all_to_all(x, "rep", split_axis=0, concat_axis=0, tiled=True)
 
 
-def packed_pieces(value, output, count):
-    rows = value.shape[0] // count
-    width = value.shape[1]
-    value = value.reshape(count, rows, width)
-    output = output.reshape(count // 2, rows, 2, width).transpose(0, 2, 1, 3)
-    return jnp.concatenate([value, output.reshape(count, rows, width)], axis=1)
+def value_pieces(x, count):
+    return x.reshape(count, x.shape[0] // count, x.shape[1])
 
 
-def unpacked(pieces, value_shape, output_shape):
+def output_pieces(x, count):
+    rows, width = 2 * x.shape[0] // count, x.shape[1] // 2
+    x = x.reshape(count // 2, rows, 2, width).transpose(0, 2, 1, 3)
+    return x.reshape(count, rows, width)
+
+
+def output_rows(pieces):
     count, rows, width = pieces.shape
-    rows //= 2
-    value = pieces[:, :rows].reshape(value_shape)
-    output = pieces[:, rows:].reshape(count // 2, 2, rows, width).transpose(0, 2, 1, 3)
-    return value, output.reshape(output_shape)
+    x = pieces.reshape(count // 2, 2, rows, width).transpose(0, 2, 1, 3)
+    return x.reshape(count * rows // 2, 2 * width)
 
 
 def on_device(
@@ -82,7 +82,8 @@
     across_v = sent(weight_v, ACROSS)
     twin_v = sent(weight_v, TWIN)
     both_v = sent(across_v, TWIN)
-    spread = swap(packed_pieces(stale_value[0], stale_output[0], replicas))
+    published = [value_pieces(stale_value[0], replicas), output_pieces(stale_output[0], replicas)]
+    spread = swap(jnp.concatenate(published, axis=1))
 
     twin_features = sent(
         jnp.concatenate(
@@ -106,7 +107,7 @@
     states = jnp.einsum("the,thf->hef", key_heads, value_heads, preferred_element_type=f32)
     states = states.astype(bf16)
     prior = state_sums(states, BEFORE)
-    across_o = sent(after(weight_o, states), ACROSS)
+    across_o = sent(weight_o, ACROSS)
     twin_o = sent(weight_o, TWIN)
     both_o = sent(across_o, TWIN)
     causal = jnp.arange(positions)[:, None] >= jnp.arange(positions)[None, :]
@@ -161,7 +162,7 @@
     picked = after(spread, grad_states, away_o).at[partner].get(
         mode="promise_in_bounds", unique_indices=True
     )
-    mate_value, mate_output = unpacked(swap(picked), weight_v.shape, weight_o.shape)
+    fetched = swap(picked)
     _, back_v, own_v = rows_grad(
         features, d_values, twin_features, sent(d_values, TWIN), rows_v, scale_value
     )
@@ -170,17 +171,15 @@
     own_count = step_counts[replica].astype(f32)
     mate_count = step_counts[partner[replica]].astype(f32)
     mix = mate_count / (own_count + mate_count)
-    new_value = (
-        (1.0 - mix) * weight_v.astype(f32)
-        + mix * mate_value.astype(f32)
-        - learning_rate * grad_value
+    kept_value = (1.0 - mix) * weight_v.astype(f32) - learning_rate * grad_value
+    kept_output = (1.0 - mix) * weight_o.astype(f32) - learning_rate * grad_output
+    kept_value, kept_output = lax.optimization_barrier(
+        (value_pieces(kept_value, replicas), output_pieces(kept_output, replicas))
     )
-    new_output = (
-        (1.0 - mix) * weight_o.astype(f32)
-        + mix * mate_output.astype(f32)
-        - learning_rate * grad_output
-    )
-    return (new_value.astype(bf16)[None], new_output.astype(bf16)[None])
+    half = kept_value.shape[1]
+    new_value = (kept_value + mix * fetched[:, :half].astype(f32)).astype(bf16)
+    new_output = (kept_output + mix * fetched[:, half:].astype(f32)).astype(bf16)
+    return new_value.reshape(value_weight.shape), output_rows(new_output)[None]
 
 
 def solution(mesh):

time: 215 us -> 218 us (1.014)
  matrix products: 53.6 us -> 47.8 us
  waiting for transfers between devices: 79 us -> 83.2 us
  local copies, waits for them, and re-layouts: 11.5 us -> 15.4 us
    ppermute x18, waiting for transfers between devices: 76.4 us -> 83.2 us  [sent(): return lax.ppermute(x, 'seq', pairs)]
    dot_general x4, matrix products: 9.86 us -> 3.97 us  [term(): both = lax.dot_general(left, right, dims, preferred_element_type=f32)]
    dot_general x4, matrix products: 12 us -> 7.04 us  [on_device(): lax.dot_general(upstream_rows, block, (((1,), (1,)), ((), ())), preferred...]
    convert_element_type x0 -> x1, other arithmetic: none -> 4.31 us  [on_device(): (kept_output + mix * fetched[:, half:].astype(f32)).astype(bf16)]
    broadcast_in_dim x1 -> x0, other arithmetic: 4.06 us -> none  [on_device(): return (new_value.astype(bf16)[None], new_output.astype(bf16)[None])]
    dot_general x1, matrix products: 2.64 us -> 6 us  [on_device(): jnp.einsum('hts,shf->thf', scores, value_heads, preferred_element_type=f32)]
    dot_general x1, matrix products: 2.44 us -> 5.76 us  [on_device(): jnp.einsum('the,she->hts', query_heads, key_heads, preferred_element_type...]
    unnamed x36 -> x50, local copies, waits for them, and re-layouts: 3.7 us -> 6.9 us
  transfers between devices with their start and end apart: 20 -> 20, of which waited for: 9 -> 7; matrix products, arithmetic and copies ran while one was open for 31% -> 29% of each run, Pallas kernels for 0% -> 0%
where the time goes in v3:
time: 218 us; the launch traced here: 217 us
  waiting for transfers between devices  83.2 us (38%)
  starting transfers between devices  54.2 us (25%)
  matrix products  47.8 us (22%)
  local copies, waits for them, and re-layouts  15.4 us (7%)
  other arithmetic  12.1 us (6%)
  between operations  4.19 us (2%)
    ppermute x18, waiting for transfers between devices, sent(): return lax.ppermute(x, 'seq', pairs)  83.2 us
    all_to_all x2, starting transfers between devices, swap(): return lax.all_to_all(x, 'rep', split_axis=0, concat_axis=0, tiled=True)  27.5 us
    ppermute x18, starting transfers between devices, sent(): return lax.ppermute(x, 'seq', pairs)  26.7 us
    dot_general x4, matrix products, term(): both += lax.dot_general(other, twin_right, dims, preferred_element_type=f32)  10.6 us
    dot_general x4, matrix products, on_device(): lax.dot_general(upstream_rows, block, (((1,), (1,)), ((), ())), preferred...  7.04 us
    unnamed x50, local copies, waits for them, and re-layouts  6.9 us
    dot_general x4, matrix products, on_device(): jnp.dot(column_block(features, rank ^ step, rows_v), block, preferred_ele...  6.44 us
    dot_general x1, matrix products, on_device(): jnp.einsum('hts,shf->thf', scores, value_heads, preferred_element_type=f32)  6 us
  transfers between devices with their start and end apart: 20, of which 7 were waited for; matrix products, arithmetic and copies ran while one was open for 29% of the time, Pallas kernels for 0%

profile of v3, /device:TPU:1, one launch (start us, length us, event | category | flops | bytes accessed | tf_op | source)
XLA Modules:
  0.0 216.9 jit_solution(9143103107786026235)
XLA Ops:
  0.6 2.1 collective-permute-start.1
  6.5 3.2 %pad_maximum_fusion = bf16[64,16,1024]{2,1,0:T(8,128)(2,1)} fusion(bf16[64,8,1024]{2,1,0:T(8,128)(2,1)} %bitcast.134, bf16[64,8,1024]{2,1,0:T(8,128)(2,1)} %bitcast.135), kind=kLoop, calls=%fused_computation.10 | loop fusion | flops 4194304 | bytes 4194304 | tf_op jit(solution)/shard_map/concatenate | solution.py:86
  9.6 13.0 %all-to-all-start = ((bf16[64,16,1024]{2,1,0:T(8,128)(2,1)}), bf16[64,16,1024]{2,1,0:T(8,128)(2,1)}, u32[]{:S(2)}, u32[]{:S(2)}) async-start(bf16[64,16,1024]{2,1,0:T(8,128)(2,1)} %pad_maximum_fusion), calls=%async_computation | async-start | bytes 4194304 | tf_op jit(solution)/shard_map/all_to_all | solution.py:45
  31.4 5.8 %select_convert_fusion = bf16[16,512,512]{2,1,0:T(8,128)(2,1)} fusion(bf16[512,16,64]{0,2,1:T(8,128)(2,1)S(1)} %bitcast.116, bf16[512,16,64]{0,2,1:T(8,128)(2,1)S(1)} %bitcast.113, pred[512,512]{1,0:T(8,128)(4,1)S(1)} %iota_compare_fusion), kind=kOutput, calls=%fused_computation.1 | convolution fusion | flops 545259520 | bytes 10747904 | tf_op jit(solution)/shard_map/the,she->hts/dot_general | solution.py:114
  39.4 25.4 %collective-permute-done.7 = bf16[256,2048]{1,0:T(8,128)(2,1)} collective-permute-done((bf16[256,2048]{1,0:T(8,128)(2,1)}, bf16[256,2048]{1,0:T(8,128)(2,1)}, u32[]{:S(2)}, u32[]{:S(2)}) %collective-permute-start.7) | collective-permute-done | bytes 1048608 | tf_op jit(solution)/shard_map/ppermute | solution.py:21
  64.8 5.6 %collective-permute-start.8 = (bf16[256,2048]{1,0:T(8,128)(2,1)}, bf16[256,2048]{1,0:T(8,128)(2,1)}, u32[]{:S(2)}, u32[]{:S(2)}) collective-permute-start(bf16[256,2048]{1,0:T(8,128)(2,1)} %collective-permute-done.7), channel_id=1, source_target_pairs={{0,1},{1,0},{2,3},{3,2},{4,5},{5,4},{6,7},{7,6},{8,9},{9,8},{10,11... | collective-permute-start | bytes 3145736 | tf_op jit(solution)/shard_map/ppermute | solution.py:21
  72.3 2.1 convolution_dynamic-update-slice_fusion.2
  74.4 2.1 convolution_dynamic-update-slice_fusion.1
  78.4 2.3 %copy.20 = bf16[512,1024]{0,1:T(8,128)(2,1)} copy(bf16[512,1024]{1,0:T(8,128)(2,1)} %multiply_convert_fusion.2) | data formatting | bytes 2097152 | tf_op jit(solution)/shard_map/convert_element_type | solution.py:103
  82.4 3.4 %collective-permute-start.5 = (bf16[16,64,64]{1,2,0:T(8,128)(2,1)S(1)}, bf16[16,64,64]{1,2,0:T(8,128)(2,1)S(1)}, u32[]{:S(2)}, u32[]{:S(2)}) collective-permute-start(bf16[16,64,64]{1,2,0:T(8,128)(2,1)S(1)} %fusion.8), channel_id=1, source_target_pairs={{0,3},{1,2},{4,7},{5,6},{8,11},{9,10},{12,15},{13,14},{16,19},{17,... | collective-permute-start | bytes 393224 | tf_op jit(solution)/shard_map/ppermute | solution.py:21
  88.5 6.0 %fusion.58 = f32[16,64,512]{2,1,0:T(8,128)S(1)} fusion(bf16[512,16,64]{0,2,1:T(8,128)(2,1)S(1)} %bitcast.123, bf16[16,512,512]{2,1,0:T(8,128)(2,1)} %select_convert_fusion), kind=kOutput, calls=%fused_computation.94 | convolution fusion | flops 536870912 | bytes 11534336 | tf_op jit(solution)/shard_map/hts,shf->thf/dot_general | solution.py:116
  102.3 3.4 %fusion.5 = bf16[256,2048]{1,0:T(8,128)(2,1)} fusion(f32[256,2048]{1,0:T(8,128)S(1)} %fusion.32, bf16[512,2048]{1,0:T(8,128)(2,1)} %collective-permute-done.16, bf16[512,512]{0,1:T(8,128)(2,1)S(1)} %collective-permute-done.15, s32[]{:T(128)S(6)} %select_n.103), kind=kOutput, calls=%fused_computation.9 | convolution fusion | flops 538443776 | bytes 5505028 | tf_op jit(solution)/shard_map/dot_general | solution.py:144
  105.7 3.7 %gather_fusion = bf16[64,16,1024]{2,1,0:T(8,128)(2,1)} fusion(bf16[64,16,1024]{2,1,0:T(8,128)(2,1)} %all-to-all-done, s32[1024]{0:T(1024)S(1)} %pad_clamp_fusion), kind=kCustom, calls=%fused_computation | custom fusion | bytes 4194560 | tf_op jit(solution)/shard_map/gather | solution.py:162
  109.4 14.5 %all-to-all-start.1 = ((bf16[64,16,1024]{2,1,0:T(8,128)(2,1)}), bf16[64,16,1024]{2,1,0:T(8,128)(2,1)}, u32[]{:S(2)}, u32[]{:S(2)}) async-start(bf16[64,16,1024]{2,1,0:T(8,128)(2,1)} %gather_fusion), calls=%async_computation.1 | async-start | bytes 4194304 | tf_op jit(solution)/shard_map/all_to_all | solution.py:45
  128.3 2.3 %collective-permute-start.9 = (bf16[16,64,64]{1,2,0:T(8,128)(2,1)S(1)}, bf16[16,64,64]{1,2,0:T(8,128)(2,1)S(1)}, u32[]{:S(2)}, u32[]{:S(2)}) collective-permute-start(bf16[16,64,64]{1,2,0:T(8,128)(2,1)S(1)} %fusion.9), channel_id=1, source_target_pairs={{1,0},{3,2},{5,4},{7,6},{9,8},{11,10},{13,12},{15,14},{17,16},{19,... | collective-permute-start | bytes 393224 | tf_op jit(solution)/shard_map/ppermute | solution.py:21
  130.6 4.9 %fusion.59 = f32[16,64,512]{2,1,0:T(8,128)S(1)} fusion(bf16[512,16,64]{0,2,1:T(8,128)(2,1)S(1)} %get-tuple-element.9, bf16[16,512,512]{2,1,0:T(8,128)(2,1)} %select_convert_fusion), kind=kOutput, calls=%fused_computation.95 | convolution fusion | flops 536870912 | bytes 11534336 | tf_op jit(solution)/shard_map/hts,thf->shf/dot_general | solution.py:134
  135.5 6.7 %collective-permute-done.11 = bf16[16,64,64]{1,2,0:T(8,128)(2,1)S(1)} collective-permute-done((bf16[16,64,64]{1,2,0:T(8,128)(2,1)S(1)}, bf16[16,64,64]{1,2,0:T(8,128)(2,1)S(1)}, u32[]{:S(2)}, u32[]{:S(2)}) %collective-permute-start.11) | collective-permute-done | bytes 131104 | tf_op jit(solution)/shard_map/ppermute | solution.py:21
  142.2 8.8 %collective-permute-done.10 = bf16[16,64,64]{1,2,0:T(8,128)(2,1)S(1)} collective-permute-done((bf16[16,64,64]{1,2,0:T(8,128)(2,1)S(1)}, bf16[16,64,64]{1,2,0:T(8,128)(2,1)S(1)}, u32[]{:S(2)}, u32[]{:S(2)}) %collective-permute-start.10) | collective-permute-done | bytes 131104 | tf_op jit(solution)/shard_map/ppermute | solution.py:21
  157.8 2.3 %multiply_convert_fusion = bf16[512,1024]{1,0:T(8,128)(2,1)S(1)} fusion(f32[512,1024]{1,0:T(8,128)S(1)} %fusion.12, bf16[512,1024]{0,1:T(8,128)(2,1)} %collective-permute-done.13, bf16[512,1024]{1,0:T(8,128)(2,1)} %collective-permute-done.12, s32[]{:T(128)S(6)} %select_n.99), kind=kOutput, calls=%fused_computation.17 | convolution fusion | flops 538443776 | bytes 4718596 | tf_op jit(solution)/shard_map/dot_general | solution.py:144
  164.0 2.3 %fusion.23 = f32[512,1024]{1,0:T(8,128)S(1)} fusion(bf16[512,1024]{0,1:T(8,128)(2,1)} %collective-permute-done.13, bf16[512,1024]{1,0:T(8,128)(2,1)} %collective-permute-done.12, s32[]{:T(128)S(6)} %select_n.97), kind=kOutput, calls=%fused_computation.49 | convolution fusion | flops 536870912 | bytes 3670020 | tf_op jit(solution)/shard_map/dot_general | solution.py:144
  166.3 21.9 %collective-permute-done.17 = bf16[256,2048]{1,0:T(8,128)(2,1)S(1)} collective-permute-done((bf16[256,2048]{1,0:T(8,128)(2,1)S(1)}, bf16[256,2048]{1,0:T(8,128)(2,1)S(1)}, u32[]{:S(2)}, u32[]{:S(2)}) %collective-permute-start.17) | collective-permute-done | bytes 1048608 | tf_op jit(solution)/shard_map/ppermute | solution.py:21
  188.1 2.7 %fusion.4 = f32[256,2048]{1,0:T(8,128)S(1)} fusion(f32[256,2048]{1,0:T(8,128)S(1)} %fusion.35, bf16[512,2048]{1,0:T(8,128)(2,1)} %collective-permute-done.16, bf16[256,2048]{1,0:T(8,128)(2,1)S(1)} %collective-permute-done.17, f32[]{:T(128)S(6)} %sub.30, bf16[512,512]{0,1:T(8,128)(2,1)S(1)} %copy-done.21, s32[]{:T(128)S(6)} %select_n.102, ...), kind=kOutput, calls=%fused_computation.8 | convolution fusion | flops 541065216 | bytes 8650760 | tf_op jit(solution)/shard_map/dot_general | solution.py:144
  190.8 19.8 %collective-permute-done.14 = bf16[512,1024]{1,0:T(8,128)(2,1)S(1)} collective-permute-done((bf16[512,1024]{1,0:T(8,128)(2,1)S(1)}, bf16[512,1024]{1,0:T(8,128)(2,1)S(1)}, u32[]{:S(2)}, u32[]{:S(2)}) %collective-permute-start.14) | collective-permute-done | bytes 1048608 | tf_op jit(solution)/shard_map/ppermute | solution.py:21
  212.6 4.3 %add_convert_fusion = (bf16[64,8,1024]{2,1,0:T(8,128)(2,1)}, bf16[1,512,1024]{2,1,0:T(8,128)(2,1)}) fusion(f32[64,8,1024]{2,1,0:T(8,128)S(1)} %bitcast.125, bf16[64,16,1024]{2,1,0:T(8,128)(2,1)} %all-to-all-done.1, f32[]{:T(128)S(6)} %div.26, f32[64,8,1024]{2,1,0:T(8,128)} %subtract_bitcast_fusion), kind=kLoop, calls=%fused_computation.14 | loop fusion | flops 4194304 | bytes 8388612 | tf_op jit(solution)/shard_map/convert_element_type | solution.py:181
  (108 shorter events, 44.3 us)
Async XLA Ops:
  0.6 36.5 %collective-permute-start.1 = (bf16[512,1024]{1,0:T(8,128)(2,1)}, bf16[512,1024]{1,0:T(8,128)(2,1)}, u32[]{:S(2)}, u32[]{:S(2)}) collective-permute-start(bf16[512,1024]{1,0:T(8,128)(2,1)} %bitcast.129), channel_id=1, source_target_pairs={{0,2},{2,0},{1,3},{3,1},{4,6},{6,4},{5,7},{7,5},{8,10},{10,8},{9,1... | collective-permute-start | bytes 3145736 | tf_op jit(solution)/shard_map/ppermute | solution.py:21
  2.7 67.6 %collective-permute-start = (bf16[512,1024]{1,0:T(8,128)(2,1)}, bf16[512,1024]{1,0:T(8,128)(2,1)}, u32[]{:S(2)}, u32[]{:S(2)}) collective-permute-start(bf16[512,1024]{1,0:T(8,128)(2,1)} %bitcast.130), channel_id=1, source_target_pairs={{0,1},{1,0},{2,3},{3,2},{4,5},{5,4},{6,7},{7,6},{8,9},{9,8},{10,11... | collective-permute-start | bytes 3145736 | tf_op jit(solution)/shard_map/ppermute | solution.py:21
  4.0 68.3 %collective-permute-start.6 = (bf16[256,2048]{1,0:T(8,128)(2,1)}, bf16[256,2048]{1,0:T(8,128)(2,1)}, u32[]{:S(2)}, u32[]{:S(2)}) collective-permute-start(bf16[256,2048]{1,0:T(8,128)(2,1)} %bitcast.131), channel_id=1, source_target_pairs={{0,1},{1,0},{2,3},{3,2},{4,5},{5,4},{6,7},{7,6},{8,9},{9,8},{10,11... | collective-permute-start | bytes 3145736 | tf_op jit(solution)/shard_map/ppermute | solution.py:21
  4.1 60.7 %collective-permute-start.7 = (bf16[256,2048]{1,0:T(8,128)(2,1)}, bf16[256,2048]{1,0:T(8,128)(2,1)}, u32[]{:S(2)}, u32[]{:S(2)}) collective-permute-start(bf16[256,2048]{1,0:T(8,128)(2,1)} %bitcast.132), channel_id=1, source_target_pairs={{0,2},{2,0},{1,3},{3,1},{4,6},{6,4},{5,7},{7,5},{8,10},{10,8},{9,1... | collective-permute-start | bytes 3145736 | tf_op jit(solution)/shard_map/ppermute | solution.py:21
  5.7 95.5 %collective-permute-start.16 = (bf16[512,2048]{1,0:T(8,128)(2,1)}, bf16[512,2048]{1,0:T(8,128)(2,1)}, u32[]{:S(2)}, u32[]{:S(2)}) collective-permute-start(bf16[512,2048]{1,0:T(8,128)(2,1)} %bitcast.124), channel_id=1, source_target_pairs={{0,1},{1,0},{2,3},{3,2},{4,5},{5,4},{6,7},{7,6},{8,9},{9,8},{10,11... | collective-permute-start | bytes 6291464 | tf_op jit(solution)/shard_map/ppermute | solution.py:21
  9.6 96.0 %all-to-all-start = ((bf16[64,16,1024]{2,1,0:T(8,128)(2,1)}), bf16[64,16,1024]{2,1,0:T(8,128)(2,1)}, u32[]{:S(2)}, u32[]{:S(2)}) async-start(bf16[64,16,1024]{2,1,0:T(8,128)(2,1)} %pad_maximum_fusion), calls=%async_computation | async-start | bytes 4194304 | tf_op jit(solution)/shard_map/all_to_all | solution.py:45
  25.7 55.0 %copy-start = (bf16[1,512,1024]{1,2,0:T(8,128)(2,1)}, bf16[1,512,1024]{1,2,0:T(8,128)(2,1)S(1)}, u32[]{:S(2)}) copy-start(bf16[1,512,1024]{1,2,0:T(8,128)(2,1)S(1)} %copy.22) | copy-start | bytes 3145732
  37.1 39.4 %collective-permute-start.2 = (bf16[512,1024]{1,0:T(8,128)(2,1)}, bf16[512,1024]{1,0:T(8,128)(2,1)S(1)}, u32[]{:S(2)}, u32[]{:S(2)}) collective-permute-start(bf16[512,1024]{1,0:T(8,128)(2,1)} %collective-permute-done.1), channel_id=1, source_target_pairs={{0,1},{1,0},{2,3},{3,2},{4,5},{5,4},{6,7},{7,6},{8,9},{9,8},{10,11... | collective-permute-start | bytes 3145736 | tf_op jit(solution)/shard_map/ppermute | solution.py:21
  64.8 29.7 %collective-permute-start.8 = (bf16[256,2048]{1,0:T(8,128)(2,1)}, bf16[256,2048]{1,0:T(8,128)(2,1)}, u32[]{:S(2)}, u32[]{:S(2)}) collective-permute-start(bf16[256,2048]{1,0:T(8,128)(2,1)} %collective-permute-done.7), channel_id=1, source_target_pairs={{0,1},{1,0},{2,3},{3,2},{4,5},{5,4},{6,7},{7,6},{8,9},{9,8},{10,11... | collective-permute-start | bytes 3145736 | tf_op jit(solution)/shard_map/ppermute | solution.py:21
  82.4 14.2 %collective-permute-start.5 = (bf16[16,64,64]{1,2,0:T(8,128)(2,1)S(1)}, bf16[16,64,64]{1,2,0:T(8,128)(2,1)S(1)}, u32[]{:S(2)}, u32[]{:S(2)}) collective-permute-start(bf16[16,64,64]{1,2,0:T(8,128)(2,1)S(1)} %fusion.8), channel_id=1, source_target_pairs={{0,3},{1,2},{4,7},{5,6},{8,11},{9,10},{12,15},{13,14},{16,19},{17,... | collective-permute-start | bytes 393224 | tf_op jit(solution)/shard_map/ppermute | solution.py:21
  85.8 11.1 %collective-permute-start.4 = (bf16[16,64,64]{1,2,0:T(8,128)(2,1)S(1)}, bf16[16,64,64]{1,2,0:T(8,128)(2,1)S(1)}, u32[]{:S(2)}, u32[]{:S(2)}) collective-permute-start(bf16[16,64,64]{1,2,0:T(8,128)(2,1)S(1)} %fusion.8), channel_id=1, source_target_pairs={{0,2},{1,3},{4,6},{5,7},{8,10},{9,11},{12,14},{13,15},{16,18},{17,... | collective-permute-start | bytes 393224 | tf_op jit(solution)/shard_map/ppermute | solution.py:21
  87.2 9.7 %collective-permute-start.3 = (bf16[16,64,64]{1,2,0:T(8,128)(2,1)S(1)}, bf16[16,64,64]{1,2,0:T(8,128)(2,1)S(1)}, u32[]{:S(2)}, u32[]{:S(2)}) collective-permute-start(bf16[16,64,64]{1,2,0:T(8,128)(2,1)S(1)} %fusion.8), channel_id=1, source_target_pairs={{0,1},{2,3},{4,5},{6,7},{8,9},{10,11},{12,13},{14,15},{16,17},{18,... | collective-permute-start | bytes 393224 | tf_op jit(solution)/shard_map/ppermute | solution.py:21
  98.8 2.7 %collective-permute-start.15 = (bf16[512,512]{0,1:T(8,128)(2,1)S(1)}, bf16[512,512]{0,1:T(8,128)(2,1)S(1)}, u32[]{:S(2)}, u32[]{:S(2)}) collective-permute-start(bf16[512,512]{0,1:T(8,128)(2,1)S(1)} %pad_maximum_fusion.2), channel_id=1, source_target_pairs={{0,1},{1,0},{2,3},{3,2},{4,5},{5,4},{6,7},{7,6},{8,9},{9,8},{10,11... | collective-permute-start | bytes 1572872 | tf_op jit(solution)/shard_map/ppermute | solution.py:21
  109.4 103.3 %all-to-all-start.1 = ((bf16[64,16,1024]{2,1,0:T(8,128)(2,1)}), bf16[64,16,1024]{2,1,0:T(8,128)(2,1)}, u32[]{:S(2)}, u32[]{:S(2)}) async-start(bf16[64,16,1024]{2,1,0:T(8,128)(2,1)} %gather_fusion), calls=%async_computation.1 | async-start | bytes 4194304 | tf_op jit(solution)/shard_map/all_to_all | solution.py:45
  125.0 26.0 %copy-start.1 = (bf16[1,512,1024]{1,2,0:T(8,128)(2,1)S(1)}, bf16[1,512,1024]{1,2,0:T(8,128)(2,1)}, u32[]{:S(2)}) copy-start(bf16[1,512,1024]{1,2,0:T(8,128)(2,1)} %copy-done) | copy-start | bytes 3145732
  125.0 32.8 %collective-permute-start.12 = (bf16[512,1024]{1,0:T(8,128)(2,1)}, bf16[512,1024]{1,0:T(8,128)(2,1)}, u32[]{:S(2)}, u32[]{:S(2)}) collective-permute-start(bf16[512,1024]{1,0:T(8,128)(2,1)} %pad_maximum_fusion.1), channel_id=1, source_target_pairs={{0,1},{1,0},{2,3},{3,2},{4,5},{5,4},{6,7},{7,6},{8,9},{9,8},{10,11... | collective-permute-start | bytes 3145736 | tf_op jit(solution)/shard_map/ppermute | solution.py:21
  125.7 16.6 %collective-permute-start.11 = (bf16[16,64,64]{1,2,0:T(8,128)(2,1)S(1)}, bf16[16,64,64]{1,2,0:T(8,128)(2,1)S(1)}, u32[]{:S(2)}, u32[]{:S(2)}) collective-permute-start(bf16[16,64,64]{1,2,0:T(8,128)(2,1)S(1)} %fusion.9), channel_id=1, source_target_pairs={{3,0},{2,1},{7,4},{6,5},{11,8},{10,9},{15,12},{14,13},{19,16},{18,... | collective-permute-start | bytes 393224 | tf_op jit(solution)/shard_map/ppermute | solution.py:21
  127.0 24.1 %collective-permute-start.10 = (bf16[16,64,64]{1,2,0:T(8,128)(2,1)S(1)}, bf16[16,64,64]{1,2,0:T(8,128)(2,1)S(1)}, u32[]{:S(2)}, u32[]{:S(2)}) collective-permute-start(bf16[16,64,64]{1,2,0:T(8,128)(2,1)S(1)} %fusion.9), channel_id=1, source_target_pairs={{2,0},{3,1},{6,4},{7,5},{10,8},{11,9},{14,12},{15,13},{18,16},{19,... | collective-permute-start | bytes 393224 | tf_op jit(solution)/shard_map/ppermute | solution.py:21
  128.3 22.8 %collective-permute-start.9 = (bf16[16,64,64]{1,2,0:T(8,128)(2,1)S(1)}, bf16[16,64,64]{1,2,0:T(8,128)(2,1)S(1)}, u32[]{:S(2)}, u32[]{:S(2)}) collective-permute-start(bf16[16,64,64]{1,2,0:T(8,128)(2,1)S(1)} %fusion.9), channel_id=1, source_target_pairs={{1,0},{3,2},{5,4},{7,6},{9,8},{11,10},{13,12},{15,14},{17,16},{19,... | collective-permute-start | bytes 393224 | tf_op jit(solution)/shard_map/ppermute | solution.py:21
  151.5 6.3 %collective-permute-start.13 = (bf16[512,1024]{0,1:T(8,128)(2,1)S(1)}, bf16[512,1024]{0,1:T(8,128)(2,1)}, u32[]{:S(2)}, u32[]{:S(2)}) collective-permute-start(bf16[512,1024]{0,1:T(8,128)(2,1)S(1)} %bitcast.119), channel_id=1, source_target_pairs={{0,1},{1,0},{2,3},{3,2},{4,5},{5,4},{6,7},{7,6},{8,9},{9,8},{10,11... | collective-permute-start | bytes 3145736 | tf_op jit(solution)/shard_map/ppermute | solution.py:21
  157.8 30.4 %collective-permute-start.17 = (bf16[256,2048]{1,0:T(8,128)(2,1)S(1)}, bf16[256,2048]{1,0:T(8,128)(2,1)S(1)}, u32[]{:S(2)}, u32[]{:S(2)}) collective-permute-start(bf16[256,2048]{1,0:T(8,128)(2,1)S(1)} %copy-done.19), channel_id=1, source_target_pairs={{0,2},{2,0},{1,3},{3,1},{4,6},{6,4},{5,7},{7,5},{8,10},{10,8},{9,1... | collective-permute-start | bytes 3145736 | tf_op jit(solution)/shard_map/ppermute | solution.py:21
  160.1 50.5 %collective-permute-start.14 = (bf16[512,1024]{1,0:T(8,128)(2,1)S(1)}, bf16[512,1024]{1,0:T(8,128)(2,1)S(1)}, u32[]{:S(2)}, u32[]{:S(2)}) collective-permute-start(bf16[512,1024]{1,0:T(8,128)(2,1)S(1)} %multiply_convert_fusion), channel_id=1, source_target_pairs={{0,2},{2,0},{1,3},{3,1},{4,6},{6,4},{5,7},{7,5},{8,10},{10,8},{9,1... | collective-permute-start | bytes 3145736 | tf_op jit(solution)/shard_map/ppermute | solution.py:21
  164.0 24.2 %copy-start.17 = (bf16[1,256,2048]{2,1,0:T(8,128)(2,1)S(1)}, bf16[1,256,2048]{2,1,0:T(8,128)(2,1)}, u32[]{:S(2)}) copy-start(bf16[1,256,2048]{2,1,0:T(8,128)(2,1)} %param.15) | copy-start | bytes 3145732
  166.3 44.3 %copy-start.13 = (bf16[1,512,1024]{2,1,0:T(8,128)(2,1)S(1)}, bf16[1,512,1024]{2,1,0:T(8,128)(2,1)}, u32[]{:S(2)}) copy-start(bf16[1,512,1024]{2,1,0:T(8,128)(2,1)} %param.14) | copy-start | bytes 3145732
  (20 other events, 151.6 us)

commit v4 on v3

--- a/solution.py
+++ b/solution.py
@@ -10,6 +10,7 @@
 
 learning_rate = 0.25
 norm_eps = 1e-06
+
 
 ACROSS = [(0, 2), (2, 0), (1, 3), (3, 1)]
 TWIN = [(0, 1), (1, 0), (2, 3), (3, 2)]
@@ -107,9 +108,11 @@
     states = jnp.einsum("the,thf->hef", key_heads, value_heads, preferred_element_type=f32)
     states = states.astype(bf16)
     prior = state_sums(states, BEFORE)
-    across_o = sent(weight_o, ACROSS)
+    across_oa = sent(weight_o[: rows_o // 2], ACROSS)
+    across_ob = sent(weight_o[rows_o // 2 :], ACROSS)
     twin_o = sent(weight_o, TWIN)
-    both_o = sent(across_o, TWIN)
+    both_oa = sent(across_oa, TWIN)
+    both_ob = sent(across_ob, TWIN)
     causal = jnp.arange(positions)[:, None] >= jnp.arange(positions)[None, :]
     scores = jnp.einsum("the,she->hts", query_heads, key_heads, preferred_element_type=f32)
     scores = jnp.where(causal[None], scores, f32(0.0)).astype(bf16)
@@ -120,11 +123,19 @@
     normed = unit.astype(bf16).reshape(positions, width)
 
     upstream = jnp.zeros((positions, width), f32)
-    for step, block in ((0, weight_o), (1, twin_o), (2, across_o), (3, both_o)):
+    for step, start, block in (
+        (0, 0, weight_o),
+        (1, 0, twin_o),
+        (2, 0, across_oa),
+        (3, 0, both_oa),
+        (2, rows_o // 2, across_ob),
+        (3, rows_o // 2, both_ob),
+    ):
         part = lax.dot_general(
             upstream_rows, block, (((1,), (1,)), ((), ())), preferred_element_type=f32
         )
-        upstream = lax.dynamic_update_slice(upstream, part, (0, (rank ^ step) * rows_o))
+        upstream = lax.dynamic_update_slice(upstream, part, (0, (rank ^ step) * rows_o + start))
+    upstream = after(upstream, normed)
     upstream = (upstream * scale_output).reshape(positions, HEADS, HEAD)
     d_attn = inverse * (upstream - unit * jnp.mean(unit * upstream, axis=-1, keepdims=True))
     d_attn = d_attn.astype(bf16)
@@ -163,10 +174,9 @@
         mode="promise_in_bounds", unique_indices=True
     )
     fetched = swap(picked)
-    _, back_v, own_v = rows_grad(
+    _, back_v, grad_value = rows_grad(
         features, d_values, twin_features, sent(d_values, TWIN), rows_v, scale_value
     )
-    grad_value = own_v + back_v.astype(f32)
     replica = lax.axis_index("rep")
     own_count = step_counts[replica].astype(f32)
     mate_count = step_counts[partner[replica]].astype(f32)
@@ -177,7 +187,9 @@
         (value_pieces(kept_value, replicas), output_pieces(kept_output, replicas))
     )
     half = kept_value.shape[1]
-    new_value = (kept_value + mix * fetched[:, :half].astype(f32)).astype(bf16)
+    back_v = value_pieces(back_v, replicas).astype(f32)
+    new_value = kept_value - learning_rate * back_v + mix * fetched[:, :half].astype(f32)
+    new_value = new_value.astype(bf16)
     new_output = (kept_output + mix * fetched[:, half:].astype(f32)).astype(bf16)
     return new_value.reshape(value_weight.shape), output_rows(new_output)[None]
 

time: 218 us -> 230 us (1.055)
  waiting for transfers between devices: 83.2 us -> 71 us
  matrix products: 47.8 us -> 58.8 us
  starting transfers between devices: 54.2 us -> 64.6 us
    ppermute x18 -> x20, waiting for transfers between devices: 83.2 us -> 71 us  [sent(): return lax.ppermute(x, 'seq', pairs)]
    ppermute x18 -> x20, starting transfers between devices: 26.7 us -> 36.1 us  [sent(): return lax.ppermute(x, 'seq', pairs)]
    dot_general x4 -> x6, matrix products: 7.04 us -> 12.6 us  [on_device(): lax.dot_general(upstream_rows, block, (((1,), (1,)), ((), ())), preferred...]
    dot_general x4, matrix products: 6.44 us -> 9.01 us  [on_device(): jnp.dot(column_block(features, rank ^ step, rows_v), block, preferred_ele...]
    unnamed x50 -> x42, local copies, waits for them, and re-layouts: 6.9 us -> 5.28 us
  transfers between devices with their start and end apart: 20 -> 22, of which waited for: 7 -> 7; matrix products, arithmetic and copies ran while one was open for 29% -> 34% of each run, Pallas kernels for 0% -> 0%
where the time goes in v4:
time: 230 us; the launch traced here: 229 us
  waiting for transfers between devices  71 us (31%)
  starting transfers between devices  64.6 us (28%)
  matrix products  58.8 us (26%)
  local copies, waits for them, and re-layouts  17.6 us (8%)
  other arithmetic  12.3 us (5%)
  between operations  4.36 us (2%)
    ppermute x20, waiting for transfers between devices, sent(): return lax.ppermute(x, 'seq', pairs)  71 us
    ppermute x20, starting transfers between devices, sent(): return lax.ppermute(x, 'seq', pairs)  36.1 us
    all_to_all x2, starting transfers between devices, swap(): return lax.all_to_all(x, 'rep', split_axis=0, concat_axis=0, tiled=True)  28.5 us
    dot_general x6, matrix products, on_device(): lax.dot_general(upstream_rows, block, (((1,), (1,)), ((), ())), preferred...  12.6 us
    dot_general x4, matrix products, term(): both += lax.dot_general(other, twin_right, dims, preferred_element_type=f32)  11.9 us
    dot_general x4, matrix products, on_device(): jnp.dot(column_block(features, rank ^ step, rows_v), block, preferred_ele...  9.01 us
    dot_general x1, matrix products, on_device(): jnp.einsum('the,she->hts', query_heads, key_heads, preferred_element_type...  7.26 us
    dot_general x1, matrix products, on_device(): jnp.einsum('hts,shf->thf', scores, value_heads, preferred_element_type=f32)  6 us
  transfers between devices with their start and end apart: 22, of which 7 were waited for; matrix products, arithmetic and copies ran while one was open for 34% of the time, Pallas kernels for 0%

profile of v4, /device:TPU:1, one launch (start us, length us, event | category | flops | bytes accessed | tf_op | source)
XLA Modules:
  0.0 228.5 jit_solution(15847195484674325523)
XLA Ops:
  9.5 13.9 %all-to-all-start = ((bf16[64,16,1024]{2,1,0:T(8,128)(2,1)}), bf16[64,16,1024]{2,1,0:T(8,128)(2,1)}, u32[]{:S(2)}, u32[]{:S(2)}) async-start(bf16[64,16,1024]{2,1,0:T(8,128)(2,1)} %pad_maximum_fusion), calls=%async_computation | async-start | bytes 4194304 | tf_op jit(solution)/shard_map/all_to_all | solution.py:46
  23.5 3.1 %fusion.22 = f32[512,1024]{1,0:T(8,128)} fusion(bf16[1,512,2048]{2,1,0:T(8,128)(2,1)} %param.10, s32[]{:T(128)S(6)} %select_n.90, bf16[1,512,1024]{2,1,0:T(8,128)(2,1)S(1)} %copy-done.11), kind=kOutput, calls=%fused_computation.50 | convolution fusion | flops 536870912 | bytes 3670020 | tf_op jit(solution)/shard_map/dot_general | solution.py:100
  34.3 7.3 %select_convert_fusion = bf16[16,512,512]{2,1,0:T(8,128)(2,1)} fusion(bf16[512,16,64]{0,2,1:T(8,128)(2,1)} %bitcast.135, bf16[512,16,64]{0,2,1:T(8,128)(2,1)S(1)} %bitcast.132, pred[512,512]{1,0:T(8,128)(4,1)S(1)} %iota_compare_fusion), kind=kOutput, calls=%fused_computation.1 | convolution fusion | flops 545259520 | bytes 10747904 | tf_op jit(solution)/shard_map/the,she->hts/dot_general | solution.py:117
  41.6 3.6 %collective-permute-done.7 = bf16[128,2048]{1,0:T(8,128)(2,1)} collective-permute-done((bf16[128,2048]{1,0:T(8,128)(2,1)}, bf16[128,2048]{1,0:T(8,128)(2,1)}, u32[]{:S(2)}, u32[]{:S(2)}) %collective-permute-start.7) | collective-permute-done | bytes 524320 | tf_op jit(solution)/shard_map/ppermute | solution.py:22
  45.2 9.2 %collective-permute-start.17 = (bf16[512,2048]{1,0:T(8,128)(2,1)S(1)}, bf16[512,2048]{1,0:T(8,128)(2,1)}, u32[]{:S(2)}, u32[]{:S(2)}) collective-permute-start(bf16[512,2048]{1,0:T(8,128)(2,1)S(1)} %bitcast.131), channel_id=1, source_target_pairs={{0,1},{1,0},{2,3},{3,2},{4,5},{5,4},{6,7},{7,6},{8,9},{9,8},{10,11... | collective-permute-start | bytes 6291464 | tf_op jit(solution)/shard_map/ppermute | solution.py:22
  54.4 9.1 %collective-permute-done.9 = bf16[128,2048]{1,0:T(8,128)(2,1)} collective-permute-done((bf16[128,2048]{1,0:T(8,128)(2,1)}, bf16[128,2048]{1,0:T(8,128)(2,1)}, u32[]{:S(2)}, u32[]{:S(2)}) %collective-permute-start.9) | collective-permute-done | bytes 524320 | tf_op jit(solution)/shard_map/ppermute | solution.py:22
  63.4 6.9 %collective-permute-start.8 = (bf16[128,2048]{1,0:T(8,128)(2,1)}, bf16[128,2048]{1,0:T(8,128)(2,1)S(1)}, u32[]{:S(2)}, u32[]{:S(2)}) collective-permute-start(bf16[128,2048]{1,0:T(8,128)(2,1)} %collective-permute-done.7), channel_id=1, source_target_pairs={{0,1},{1,0},{2,3},{3,2},{4,5},{5,4},{6,7},{7,6},{8,9},{9,8},{10,11... | collective-permute-start | bytes 1572872 | tf_op jit(solution)/shard_map/ppermute | solution.py:22
  70.9 2.8 %convolution_dynamic-update-slice_fusion = f32[512,1024]{0,1:T(8,128)} fusion(f32[512,1024]{0,1:T(8,128)} %convolution_dynamic-update-slice_fusion.1, s32[]{:T(128)S(6)} %select_n.96, bf16[256,2048]{1,0:T(8,128)(2,1)} %collective-permute-done.6, bf16[1,512,2048]{2,1,0:T(8,128)(2,1)S(1)} %copy-done), kind=kOutput, calls=%fused_computation.26 | convolution fusion | flops 536870912 | bytes 3670020 | tf_op jit(solution)/shard_map/dot_general | solution.py:134
  73.7 2.6 %convolution_dynamic-update-slice_fusion.5 = f32[512,1024]{0,1:T(8,128)} fusion(f32[512,1024]{0,1:T(8,128)} %convolution_dynamic-update-slice_fusion, s32[]{:T(128)S(6)} %select_n.97, bf16[128,2048]{1,0:T(8,128)(2,1)} %collective-permute-done.7, bf16[1,512,2048]{2,1,0:T(8,128)(2,1)S(1)} %copy-done), kind=kOutput, calls=%fused_computation.33 | convolution fusion | flops 268435456 | bytes 2883588 | tf_op jit(solution)/shard_map/dot_general | solution.py:134
  77.8 2.6 %convolution_dynamic-update-slice_fusion.3 = f32[512,1024]{0,1:T(8,128)} fusion(f32[512,1024]{0,1:T(8,128)} %convolution_dynamic-update-slice_fusion.4, s32[]{:T(128)S(6)} %select_n.99, bf16[128,2048]{1,0:T(8,128)(2,1)} %collective-permute-done.9, bf16[1,512,2048]{2,1,0:T(8,128)(2,1)S(1)} %copy-done), kind=kOutput, calls=%fused_computation.31 | convolution fusion | flops 268435456 | bytes 2883588 | tf_op jit(solution)/shard_map/dot_general | solution.py:134
  91.9 3.6 %collective-permute-start.5 = (bf16[16,64,64]{1,2,0:T(8,128)(2,1)S(1)}, bf16[16,64,64]{1,2,0:T(8,128)(2,1)S(1)}, u32[]{:S(2)}, u32[]{:S(2)}) collective-permute-start(bf16[16,64,64]{1,2,0:T(8,128)(2,1)S(1)} %fusion.10), channel_id=1, source_target_pairs={{0,3},{1,2},{4,7},{5,6},{8,11},{9,10},{12,15},{13,14},{16,19},{17,... | collective-permute-start | bytes 393224 | tf_op jit(solution)/shard_map/ppermute | solution.py:22
  98.2 6.0 %fusion.61 = f32[16,64,512]{2,1,0:T(8,128)S(1)} fusion(bf16[512,16,64]{0,2,1:T(8,128)(2,1)S(1)} %bitcast.142, bf16[16,512,512]{2,1,0:T(8,128)(2,1)} %select_convert_fusion), kind=kOutput, calls=%fused_computation.101 | convolution fusion | flops 536870912 | bytes 11534336 | tf_op jit(solution)/shard_map/hts,shf->thf/dot_general | solution.py:119
  104.2 2.7 %collective-permute-done.4 = bf16[16,64,64]{1,2,0:T(8,128)(2,1)S(1)} collective-permute-done((bf16[16,64,64]{1,2,0:T(8,128)(2,1)S(1)}, bf16[16,64,64]{1,2,0:T(8,128)(2,1)S(1)}, u32[]{:S(2)}, u32[]{:S(2)}) %collective-permute-start.4) | collective-permute-done | bytes 131104 | tf_op jit(solution)/shard_map/ppermute | solution.py:22
  115.1 3.4 %fusion.5 = bf16[256,2048]{1,0:T(8,128)(2,1)} fusion(f32[256,2048]{1,0:T(8,128)S(1)} %fusion.33, bf16[512,2048]{1,0:T(8,128)(2,1)} %collective-permute-done.17, bf16[512,512]{0,1:T(8,128)(2,1)S(1)} %collective-permute-done.16, s32[]{:T(128)S(6)} %select_n.110), kind=kOutput, calls=%fused_computation.9 | convolution fusion | flops 538443776 | bytes 5505028 | tf_op jit(solution)/shard_map/dot_general | solution.py:155
  118.5 3.6 %gather_fusion = bf16[64,16,1024]{2,1,0:T(8,128)(2,1)} fusion(bf16[64,16,1024]{2,1,0:T(8,128)(2,1)} %all-to-all-done, s32[1024]{0:T(1024)S(1)} %pad_clamp_fusion), kind=kCustom, calls=%fused_computation | custom fusion | bytes 4194560 | tf_op jit(solution)/shard_map/gather | solution.py:173
  122.0 14.6 %all-to-all-start.1 = ((bf16[64,16,1024]{2,1,0:T(8,128)(2,1)}), bf16[64,16,1024]{2,1,0:T(8,128)(2,1)}, u32[]{:S(2)}, u32[]{:S(2)}) async-start(bf16[64,16,1024]{2,1,0:T(8,128)(2,1)} %gather_fusion), calls=%async_computation.1 | async-start | bytes 4194304 | tf_op jit(solution)/shard_map/all_to_all | solution.py:46
  144.2 4.9 %fusion.62 = f32[16,64,512]{2,1,0:T(8,128)S(1)} fusion(bf16[512,16,64]{0,2,1:T(8,128)(2,1)S(1)} %multiply_convert_fusion.1, bf16[16,512,512]{2,1,0:T(8,128)(2,1)} %select_convert_fusion), kind=kOutput, calls=%fused_computation.102 | convolution fusion | flops 536870912 | bytes 11534336 | tf_op jit(solution)/shard_map/hts,thf->shf/dot_general | solution.py:145
  149.2 6.5 %collective-permute-done.13 = bf16[16,64,64]{1,2,0:T(8,128)(2,1)S(1)} collective-permute-done((bf16[16,64,64]{1,2,0:T(8,128)(2,1)S(1)}, bf16[16,64,64]{1,2,0:T(8,128)(2,1)S(1)}, u32[]{:S(2)}, u32[]{:S(2)}) %collective-permute-start.13) | collective-permute-done | bytes 131104 | tf_op jit(solution)/shard_map/ppermute | solution.py:22
  155.7 9.2 %collective-permute-done.12 = bf16[16,64,64]{1,2,0:T(8,128)(2,1)S(1)} collective-permute-done((bf16[16,64,64]{1,2,0:T(8,128)(2,1)S(1)}, bf16[16,64,64]{1,2,0:T(8,128)(2,1)S(1)}, u32[]{:S(2)}, u32[]{:S(2)}) %collective-permute-start.12) | collective-permute-done | bytes 131104 | tf_op jit(solution)/shard_map/ppermute | solution.py:22
  177.6 3.7 %subtract_bitcast_fusion = f32[64,8,1024]{2,1,0:T(8,128)} fusion(f32[512,1024]{1,0:T(8,128)S(1)} %fusion.20, bf16[512,1024]{0,1:T(8,128)(2,1)} %collective-permute-done.15, f32[]{:T(128)S(6)} %sub.33, bf16[512,1024]{1,0:T(8,128)(2,1)} %collective-permute-done.14, s32[]{:T(128)S(6)} %select_n.105, bf16[1,512,1024]{2,1,0:T(8,128)(2,1)S(1)} %copy-done.12), kind=kOutput, calls=%fused_computation.19 | convolution fusion | flops 539492352 | bytes 6815752 | tf_op jit(solution)/shard_map/dot_general | solution.py:155
  181.3 19.9 %collective-permute-done.18 = bf16[256,2048]{1,0:T(8,128)(2,1)S(1)} collective-permute-done((bf16[256,2048]{1,0:T(8,128)(2,1)S(1)}, bf16[256,2048]{1,0:T(8,128)(2,1)S(1)}, u32[]{:S(2)}, u32[]{:S(2)}) %collective-permute-start.18) | collective-permute-done | bytes 1048608 | tf_op jit(solution)/shard_map/ppermute | solution.py:22
  201.2 2.7 %fusion.4 = f32[256,2048]{1,0:T(8,128)S(1)} fusion(f32[256,2048]{1,0:T(8,128)S(1)} %fusion.36, bf16[512,2048]{1,0:T(8,128)(2,1)} %collective-permute-done.17, bf16[256,2048]{1,0:T(8,128)(2,1)S(1)} %collective-permute-done.18, f32[]{:T(128)S(6)} %sub.33, bf16[512,512]{0,1:T(8,128)(2,1)S(1)} %copy-done.17, s32[]{:T(128)S(6)} %select_n.108, ...), kind=kOutput, calls=%fused_computation.8 | convolution fusion | flops 541065216 | bytes 8650760 | tf_op jit(solution)/shard_map/dot_general | solution.py:155
  203.9 19.9 %collective-permute-done.19 = bf16[512,1024]{1,0:T(8,128)(2,1)} collective-permute-done((bf16[512,1024]{1,0:T(8,128)(2,1)S(1)}, bf16[512,1024]{1,0:T(8,128)(2,1)}, u32[]{:S(2)}, u32[]{:S(2)}) %collective-permute-start.19) | collective-permute-done | bytes 1048608 | tf_op jit(solution)/shard_map/ppermute | solution.py:22
  223.8 4.8 %add_convert_fusion = (bf16[64,8,1024]{2,1,0:T(8,128)(2,1)}, bf16[1,512,1024]{2,1,0:T(8,128)(2,1)}) fusion(f32[64,8,1024]{2,1,0:T(8,128)S(1)} %bitcast.143, bf16[64,16,1024]{2,1,0:T(8,128)(2,1)} %all-to-all-done.1, f32[]{:T(128)S(6)} %div.26, f32[64,8,1024]{2,1,0:T(8,128)} %subtract_bitcast_fusion, bf16[512,1024]{1,0:T(8,128)(2,1)} %collective-permute-done.19), kind=kLoop, calls=%fused_computation.17 | loop fusion | flops 5767168 | bytes 9437188 | tf_op jit(solution)/shard_map/convert_element_type | solution.py:193
  (107 shorter events, 57.7 us)
Async XLA Ops:
  0.6 69.7 %collective-permute-start.1 = (bf16[512,1024]{1,0:T(8,128)(2,1)}, bf16[512,1024]{1,0:T(8,128)(2,1)}, u32[]{:S(2)}, u32[]{:S(2)}) collective-permute-start(bf16[512,1024]{1,0:T(8,128)(2,1)} %bitcast.148), channel_id=1, source_target_pairs={{0,2},{2,0},{1,3},{3,1},{4,6},{6,4},{5,7},{7,5},{8,10},{10,8},{9,1... | collective-permute-start | bytes 3145736 | tf_op jit(solution)/shard_map/ppermute | solution.py:22
  2.8 81.1 %collective-permute-start = (bf16[512,1024]{1,0:T(8,128)(2,1)}, bf16[512,1024]{1,0:T(8,128)(2,1)}, u32[]{:S(2)}, u32[]{:S(2)}) collective-permute-start(bf16[512,1024]{1,0:T(8,128)(2,1)} %bitcast.149), channel_id=1, source_target_pairs={{0,1},{1,0},{2,3},{3,2},{4,5},{5,4},{6,7},{7,6},{8,9},{9,8},{10,11... | collective-permute-start | bytes 3145736 | tf_op jit(solution)/shard_map/ppermute | solution.py:22
  4.0 66.4 %collective-permute-start.6 = (bf16[256,2048]{1,0:T(8,128)(2,1)}, bf16[256,2048]{1,0:T(8,128)(2,1)}, u32[]{:S(2)}, u32[]{:S(2)}) collective-permute-start(bf16[256,2048]{1,0:T(8,128)(2,1)} %bitcast.147), channel_id=1, source_target_pairs={{0,1},{1,0},{2,3},{3,2},{4,5},{5,4},{6,7},{7,6},{8,9},{9,8},{10,11... | collective-permute-start | bytes 3145736 | tf_op jit(solution)/shard_map/ppermute | solution.py:22
  6.4 38.8 %collective-permute-start.7 = (bf16[128,2048]{1,0:T(8,128)(2,1)}, bf16[128,2048]{1,0:T(8,128)(2,1)}, u32[]{:S(2)}, u32[]{:S(2)}) collective-permute-start(bf16[128,2048]{1,0:T(8,128)(2,1)} %get-tuple-element.17), channel_id=1, source_target_pairs={{0,2},{2,0},{1,3},{3,1},{4,6},{6,4},{5,7},{7,5},{8,10},{10,8},{9,1... | collective-permute-start | bytes 1572872 | tf_op jit(solution)/shard_map/ppermute | solution.py:22
  8.0 55.5 %collective-permute-start.9 = (bf16[128,2048]{1,0:T(8,128)(2,1)}, bf16[128,2048]{1,0:T(8,128)(2,1)}, u32[]{:S(2)}, u32[]{:S(2)}) collective-permute-start(bf16[128,2048]{1,0:T(8,128)(2,1)} %get-tuple-element.16), channel_id=1, source_target_pairs={{0,2},{2,0},{1,3},{3,1},{4,6},{6,4},{5,7},{7,5},{8,10},{10,8},{9,1... | collective-permute-start | bytes 1572872 | tf_op jit(solution)/shard_map/ppermute | solution.py:22
  9.5 108.9 %all-to-all-start = ((bf16[64,16,1024]{2,1,0:T(8,128)(2,1)}), bf16[64,16,1024]{2,1,0:T(8,128)(2,1)}, u32[]{:S(2)}, u32[]{:S(2)}) async-start(bf16[64,16,1024]{2,1,0:T(8,128)(2,1)} %pad_maximum_fusion), calls=%async_computation | async-start | bytes 4194304 | tf_op jit(solution)/shard_map/all_to_all | solution.py:46
  34.2 55.9 %copy-start.1 = (bf16[1,512,1024]{1,2,0:T(8,128)(2,1)}, bf16[1,512,1024]{1,2,0:T(8,128)(2,1)S(1)}, u32[]{:S(2)}) copy-start(bf16[1,512,1024]{1,2,0:T(8,128)(2,1)S(1)} %copy.28) | copy-start | bytes 3145732
  45.2 69.1 %collective-permute-start.17 = (bf16[512,2048]{1,0:T(8,128)(2,1)S(1)}, bf16[512,2048]{1,0:T(8,128)(2,1)}, u32[]{:S(2)}, u32[]{:S(2)}) collective-permute-start(bf16[512,2048]{1,0:T(8,128)(2,1)S(1)} %bitcast.131), channel_id=1, source_target_pairs={{0,1},{1,0},{2,3},{3,2},{4,5},{5,4},{6,7},{7,6},{8,9},{9,8},{10,11... | collective-permute-start | bytes 6291464 | tf_op jit(solution)/shard_map/ppermute | solution.py:22
  63.4 12.8 %collective-permute-start.8 = (bf16[128,2048]{1,0:T(8,128)(2,1)}, bf16[128,2048]{1,0:T(8,128)(2,1)S(1)}, u32[]{:S(2)}, u32[]{:S(2)}) collective-permute-start(bf16[128,2048]{1,0:T(8,128)(2,1)} %collective-permute-done.7), channel_id=1, source_target_pairs={{0,1},{1,0},{2,3},{3,2},{4,5},{5,4},{6,7},{7,6},{8,9},{9,8},{10,11... | collective-permute-start | bytes 1572872 | tf_op jit(solution)/shard_map/ppermute | solution.py:22
  70.4 10.0 %collective-permute-start.10 = (bf16[128,2048]{1,0:T(8,128)(2,1)}, bf16[128,2048]{1,0:T(8,128)(2,1)S(1)}, u32[]{:S(2)}, u32[]{:S(2)}) collective-permute-start(bf16[128,2048]{1,0:T(8,128)(2,1)} %collective-permute-done.9), channel_id=1, source_target_pairs={{0,1},{1,0},{2,3},{3,2},{4,5},{5,4},{6,7},{7,6},{8,9},{9,8},{10,11... | collective-permute-start | bytes 1572872 | tf_op jit(solution)/shard_map/ppermute | solution.py:22
  70.4 15.6 %collective-permute-start.2 = (bf16[512,1024]{1,0:T(8,128)(2,1)}, bf16[512,1024]{1,0:T(8,128)(2,1)S(1)}, u32[]{:S(2)}, u32[]{:S(2)}) collective-permute-start(bf16[512,1024]{1,0:T(8,128)(2,1)} %collective-permute-done.1), channel_id=1, source_target_pairs={{0,1},{1,0},{2,3},{3,2},{4,5},{5,4},{6,7},{7,6},{8,9},{9,8},{10,11... | collective-permute-start | bytes 3145736 | tf_op jit(solution)/shard_map/ppermute | solution.py:22
  91.9 12.3 %collective-permute-start.5 = (bf16[16,64,64]{1,2,0:T(8,128)(2,1)S(1)}, bf16[16,64,64]{1,2,0:T(8,128)(2,1)S(1)}, u32[]{:S(2)}, u32[]{:S(2)}) collective-permute-start(bf16[16,64,64]{1,2,0:T(8,128)(2,1)S(1)} %fusion.10), channel_id=1, source_target_pairs={{0,3},{1,2},{4,7},{5,6},{8,11},{9,10},{12,15},{13,14},{16,19},{17,... | collective-permute-start | bytes 393224 | tf_op jit(solution)/shard_map/ppermute | solution.py:22
  95.5 11.3 %collective-permute-start.4 = (bf16[16,64,64]{1,2,0:T(8,128)(2,1)S(1)}, bf16[16,64,64]{1,2,0:T(8,128)(2,1)S(1)}, u32[]{:S(2)}, u32[]{:S(2)}) collective-permute-start(bf16[16,64,64]{1,2,0:T(8,128)(2,1)S(1)} %fusion.10), channel_id=1, source_target_pairs={{0,2},{1,3},{4,6},{5,7},{8,10},{9,11},{12,14},{13,15},{16,18},{17,... | collective-permute-start | bytes 393224 | tf_op jit(solution)/shard_map/ppermute | solution.py:22
  96.8 10.0 %collective-permute-start.3 = (bf16[16,64,64]{1,2,0:T(8,128)(2,1)S(1)}, bf16[16,64,64]{1,2,0:T(8,128)(2,1)S(1)}, u32[]{:S(2)}, u32[]{:S(2)}) collective-permute-start(bf16[16,64,64]{1,2,0:T(8,128)(2,1)S(1)} %fusion.10), channel_id=1, source_target_pairs={{0,1},{2,3},{4,5},{6,7},{8,9},{10,11},{12,13},{14,15},{16,17},{18,... | collective-permute-start | bytes 393224 | tf_op jit(solution)/shard_map/ppermute | solution.py:22
  107.8 6.5 %collective-permute-start.16 = (bf16[512,512]{0,1:T(8,128)(2,1)S(1)}, bf16[512,512]{0,1:T(8,128)(2,1)S(1)}, u32[]{:S(2)}, u32[]{:S(2)}) collective-permute-start(bf16[512,512]{0,1:T(8,128)(2,1)S(1)} %pad_maximum_fusion.2), channel_id=1, source_target_pairs={{0,1},{1,0},{2,3},{3,2},{4,5},{5,4},{6,7},{7,6},{8,9},{9,8},{10,11... | collective-permute-start | bytes 1572872 | tf_op jit(solution)/shard_map/ppermute | solution.py:22
  122.0 101.8 %all-to-all-start.1 = ((bf16[64,16,1024]{2,1,0:T(8,128)(2,1)}), bf16[64,16,1024]{2,1,0:T(8,128)(2,1)}, u32[]{:S(2)}, u32[]{:S(2)}) async-start(bf16[64,16,1024]{2,1,0:T(8,128)(2,1)} %gather_fusion), calls=%async_computation.1 | async-start | bytes 4194304 | tf_op jit(solution)/shard_map/all_to_all | solution.py:46
  139.1 25.9 %copy-start.2 = (bf16[1,512,1024]{1,2,0:T(8,128)(2,1)S(1)}, bf16[1,512,1024]{1,2,0:T(8,128)(2,1)}, u32[]{:S(2)}) copy-start(bf16[1,512,1024]{1,2,0:T(8,128)(2,1)} %copy-done.1) | copy-start | bytes 3145732
  139.1 34.0 %collective-permute-start.14 = (bf16[512,1024]{1,0:T(8,128)(2,1)}, bf16[512,1024]{1,0:T(8,128)(2,1)}, u32[]{:S(2)}, u32[]{:S(2)}) collective-permute-start(bf16[512,1024]{1,0:T(8,128)(2,1)} %pad_maximum_fusion.1), channel_id=1, source_target_pairs={{0,1},{1,0},{2,3},{3,2},{4,5},{5,4},{6,7},{7,6},{8,9},{9,8},{10,11... | collective-permute-start | bytes 3145736 | tf_op jit(solution)/shard_map/ppermute | solution.py:22
  139.5 16.2 %collective-permute-start.13 = (bf16[16,64,64]{1,2,0:T(8,128)(2,1)S(1)}, bf16[16,64,64]{1,2,0:T(8,128)(2,1)S(1)}, u32[]{:S(2)}, u32[]{:S(2)}) collective-permute-start(bf16[16,64,64]{1,2,0:T(8,128)(2,1)S(1)} %fusion.11), channel_id=1, source_target_pairs={{3,0},{2,1},{7,4},{6,5},{11,8},{10,9},{15,12},{14,13},{19,16},{18,... | collective-permute-start | bytes 393224 | tf_op jit(solution)/shard_map/ppermute | solution.py:22
  140.8 24.1 %collective-permute-start.12 = (bf16[16,64,64]{1,2,0:T(8,128)(2,1)S(1)}, bf16[16,64,64]{1,2,0:T(8,128)(2,1)S(1)}, u32[]{:S(2)}, u32[]{:S(2)}) collective-permute-start(bf16[16,64,64]{1,2,0:T(8,128)(2,1)S(1)} %fusion.11), channel_id=1, source_target_pairs={{2,0},{3,1},{6,4},{7,5},{10,8},{11,9},{14,12},{15,13},{18,16},{19,... | collective-permute-start | bytes 393224 | tf_op jit(solution)/shard_map/ppermute | solution.py:22
  142.1 22.8 %collective-permute-start.11 = (bf16[16,64,64]{1,2,0:T(8,128)(2,1)S(1)}, bf16[16,64,64]{1,2,0:T(8,128)(2,1)S(1)}, u32[]{:S(2)}, u32[]{:S(2)}) collective-permute-start(bf16[16,64,64]{1,2,0:T(8,128)(2,1)S(1)} %fusion.11), channel_id=1, source_target_pairs={{1,0},{3,2},{5,4},{7,6},{9,8},{11,10},{13,12},{15,14},{17,16},{19,... | collective-permute-start | bytes 393224 | tf_op jit(solution)/shard_map/ppermute | solution.py:22
  165.3 7.8 %collective-permute-start.15 = (bf16[512,1024]{0,1:T(8,128)(2,1)S(1)}, bf16[512,1024]{0,1:T(8,128)(2,1)}, u32[]{:S(2)}, u32[]{:S(2)}) collective-permute-start(bf16[512,1024]{0,1:T(8,128)(2,1)S(1)} %bitcast.138), channel_id=1, source_target_pairs={{0,1},{1,0},{2,3},{3,2},{4,5},{5,4},{6,7},{7,6},{8,9},{9,8},{10,11... | collective-permute-start | bytes 3145736 | tf_op jit(solution)/shard_map/ppermute | solution.py:22
  172.2 29.0 %collective-permute-start.18 = (bf16[256,2048]{1,0:T(8,128)(2,1)S(1)}, bf16[256,2048]{1,0:T(8,128)(2,1)S(1)}, u32[]{:S(2)}, u32[]{:S(2)}) collective-permute-start(bf16[256,2048]{1,0:T(8,128)(2,1)S(1)} %copy-done.15), channel_id=1, source_target_pairs={{0,2},{2,0},{1,3},{3,1},{4,6},{6,4},{5,7},{7,5},{8,10},{10,8},{9,1... | collective-permute-start | bytes 3145736 | tf_op jit(solution)/shard_map/ppermute | solution.py:22
  175.3 48.5 %collective-permute-start.19 = (bf16[512,1024]{1,0:T(8,128)(2,1)S(1)}, bf16[512,1024]{1,0:T(8,128)(2,1)}, u32[]{:S(2)}, u32[]{:S(2)}) collective-permute-start(bf16[512,1024]{1,0:T(8,128)(2,1)S(1)} %multiply_convert_fusion), channel_id=1, source_target_pairs={{0,2},{2,0},{1,3},{3,1},{4,6},{6,4},{5,7},{7,5},{8,10},{10,8},{9,1... | collective-permute-start | bytes 3145736 | tf_op jit(solution)/shard_map/ppermute | solution.py:22
  (18 other events, 155.5 us)

commit v5 on v4

--- a/solution.py
+++ b/solution.py
@@ -109,7 +109,7 @@
     states = states.astype(bf16)
     prior = state_sums(states, BEFORE)
     across_oa = sent(weight_o[: rows_o // 2], ACROSS)
-    across_ob = sent(weight_o[rows_o // 2 :], ACROSS)
+    across_ob = sent(after(weight_o, across_v)[rows_o // 2 :], ACROSS)
     twin_o = sent(weight_o, TWIN)
     both_oa = sent(across_oa, TWIN)
     both_ob = sent(across_ob, TWIN)
@@ -134,7 +134,8 @@
         part = lax.dot_general(
             upstream_rows, block, (((1,), (1,)), ((), ())), preferred_element_type=f32
         )
-        upstream = lax.dynamic_update_slice(upstream, part, (0, (rank ^ step) * rows_o + start))
+        column = (rank ^ step) * rows_o + start
+        upstream = lax.dynamic_update_slice(upstream, part, (0, column))
     upstream = after(upstream, normed)
     upstream = (upstream * scale_output).reshape(positions, HEADS, HEAD)
     d_attn = inverse * (upstream - unit * jnp.mean(unit * upstream, axis=-1, keepdims=True))

time: 230 us -> 218 us (0.948)
  starting transfers between devices: 64.6 us -> 55.9 us
  waiting for transfers between devices: 71 us -> 65.7 us
    ppermute x20, starting transfers between devices: 36.1 us -> 29.4 us  [sent(): return lax.ppermute(x, 'seq', pairs)]
    ppermute x20, waiting for transfers between devices: 71 us -> 65.7 us  [sent(): return lax.ppermute(x, 'seq', pairs)]
    unnamed x42 -> x40, local copies, waits for them, and re-layouts: 5.28 us -> 5.23 us
  transfers between devices with their start and end apart: 22 -> 22, of which waited for: 7 -> 6; matrix products, arithmetic and copies ran while one was open for 34% -> 37% of each run, Pallas kernels for 0% -> 0%
where the time goes in v5:
time: 218 us; the launch traced here: 217 us
  waiting for transfers between devices  65.7 us (30%)
  matrix products  59.9 us (27%)
  starting transfers between devices  55.9 us (26%)
  local copies, waits for them, and re-layouts  17.2 us (8%)
  other arithmetic  13.8 us (6%)
  between operations  4.25 us (2%)
    ppermute x20, waiting for transfers between devices, sent(): return lax.ppermute(x, 'seq', pairs)  65.7 us
    ppermute x20, starting transfers between devices, sent(): return lax.ppermute(x, 'seq', pairs)  29.4 us
    all_to_all x2, starting transfers between devices, swap(): return lax.all_to_all(x, 'rep', split_axis=0, concat_axis=0, tiled=True)  26.5 us
    dot_general x6, matrix products, on_device(): lax.dot_general(upstream_rows, block, (((1,), (1,)), ((), ())), preferred...  13.7 us
    dot_general x4, matrix products, term(): both += lax.dot_general(other, twin_right, dims, preferred_element_type=f32)  11.9 us
    dot_general x4, matrix products, on_device(): jnp.dot(column_block(features, rank ^ step, rows_v), block, preferred_ele...  8.86 us
    dot_general x1, matrix products, on_device(): jnp.einsum('the,she->hts', query_heads, key_heads, preferred_element_type...  7.29 us
    dot_general x1, matrix products, on_device(): jnp.einsum('hts,shf->thf', scores, value_heads, preferred_element_type=f32)  6 us
  transfers between devices with their start and end apart: 22, of which 6 were waited for; matrix products, arithmetic and copies ran while one was open for 37% of the time, Pallas kernels for 0%

profile of v5, /device:TPU:1, one launch (start us, length us, event | category | flops | bytes accessed | tf_op | source)
XLA Modules:
  0.0 216.7 jit_solution(8266183054118706035)
XLA Ops:
  8.3 3.1 %pad_maximum_fusion = bf16[64,16,1024]{2,1,0:T(8,128)(2,1)} fusion(bf16[64,8,1024]{2,1,0:T(8,128)(2,1)} %bitcast.158, bf16[64,8,1024]{2,1,0:T(8,128)(2,1)} %bitcast.159), kind=kLoop, calls=%fused_computation.10 | loop fusion | flops 4194304 | bytes 4194304 | tf_op jit(solution)/shard_map/concatenate | solution.py:87
  11.4 13.0 %all-to-all-start = ((bf16[64,16,1024]{2,1,0:T(8,128)(2,1)}), bf16[64,16,1024]{2,1,0:T(8,128)(2,1)}, u32[]{:S(2)}, u32[]{:S(2)}) async-start(bf16[64,16,1024]{2,1,0:T(8,128)(2,1)} %pad_maximum_fusion), calls=%async_computation | async-start | bytes 4194304 | tf_op jit(solution)/shard_map/all_to_all | solution.py:46
  24.5 3.2 %fusion.24 = f32[512,1024]{1,0:T(8,128)} fusion(bf16[1,512,2048]{2,1,0:T(8,128)(2,1)} %param.10, s32[]{:T(128)S(6)} %select_n.90, bf16[1,512,1024]{2,1,0:T(8,128)(2,1)S(1)} %copy-done.12), kind=kOutput, calls=%fused_computation.52 | convolution fusion | flops 536870912 | bytes 3670020 | tf_op jit(solution)/shard_map/dot_general | solution.py:100
  31.5 2.3 %copy.25 = bf16[1,512,1024]{1,2,0:T(8,128)(2,1)} copy(bf16[1,512,1024]{2,1,0:T(8,128)(2,1)} %param.11) | data formatting | bytes 2097152 | tf_op args[1]
  35.3 7.3 %select_convert_fusion = bf16[16,512,512]{2,1,0:T(8,128)(2,1)} fusion(bf16[512,16,64]{0,2,1:T(8,128)(2,1)} %bitcast.141, bf16[512,16,64]{0,2,1:T(8,128)(2,1)S(1)} %bitcast.138, pred[512,512]{1,0:T(8,128)(4,1)S(1)} %iota_compare_fusion), kind=kOutput, calls=%fused_computation.1 | convolution fusion | flops 545259520 | bytes 10747904 | tf_op jit(solution)/shard_map/the,she->hts/dot_general | solution.py:117
  43.4 6.7 %collective-permute-start.8 = (bf16[128,2048]{1,0:T(8,128)(2,1)}, bf16[128,2048]{1,0:T(8,128)(2,1)S(1)}, u32[]{:S(2)}, u32[]{:S(2)}) collective-permute-start(bf16[128,2048]{1,0:T(8,128)(2,1)} %collective-permute-done.7), channel_id=1, source_target_pairs={{0,1},{1,0},{2,3},{3,2},{4,5},{5,4},{6,7},{7,6},{8,9},{9,8},{10,11... | collective-permute-start | bytes 1572872 | tf_op jit(solution)/shard_map/ppermute | solution.py:22
  52.1 2.8 %convolution_dynamic-update-slice_fusion = f32[512,1024]{0,1:T(8,128)} fusion(f32[512,1024]{0,1:T(8,128)} %convolution_dynamic-update-slice_fusion.1, s32[]{:T(128)S(6)} %select_n.96, bf16[256,2048]{1,0:T(8,128)(2,1)} %collective-permute-done.6, bf16[1,512,2048]{2,1,0:T(8,128)(2,1)S(1)} %copy-done), kind=kOutput, calls=%fused_computation.26 | convolution fusion | flops 536870912 | bytes 3670020 | tf_op jit(solution)/shard_map/dot_general | solution.py:134
  56.8 2.6 %convolution_dynamic-update-slice_fusion.3 = f32[512,1024]{0,1:T(8,128)} fusion(f32[512,1024]{0,1:T(8,128)} %convolution_dynamic-update-slice_fusion, s32[]{:T(128)S(6)} %select_n.97, bf16[128,2048]{1,0:T(8,128)(2,1)} %collective-permute-done.7, bf16[1,512,2048]{2,1,0:T(8,128)(2,1)S(1)} %copy-done), kind=kOutput, calls=%fused_computation.31 | convolution fusion | flops 268435456 | bytes 2883588 | tf_op jit(solution)/shard_map/dot_general | solution.py:134
  62.9 9.6 %collective-permute-done.9 = bf16[128,2048]{1,0:T(8,128)(2,1)} collective-permute-done((bf16[128,2048]{1,0:T(8,128)(2,1)S(1)}, bf16[128,2048]{1,0:T(8,128)(2,1)}, u32[]{:S(2)}, u32[]{:S(2)}) %collective-permute-start.9) | collective-permute-done | bytes 524320 | tf_op jit(solution)/shard_map/ppermute | solution.py:22
  73.1 2.6 %fusion.11 = f32[512,1024]{0,1:T(8,128)} fusion(f32[512,1024]{0,1:T(8,128)} %convolution_dynamic-update-slice_fusion.2, s32[]{:T(128)S(6)} %select_n.99, bf16[128,2048]{1,0:T(8,128)(2,1)} %collective-permute-done.9, bf16[1,512,2048]{2,1,0:T(8,128)(2,1)S(1)} %copy-done), kind=kOutput, calls=%fused_computation.35 | convolution fusion | flops 268435456 | bytes 2883588 | tf_op jit(solution)/shard_map/dot_general | solution.py:134
  81.5 3.1 %collective-permute-start.5 = (bf16[16,64,64]{1,2,0:T(8,128)(2,1)S(1)}, bf16[16,64,64]{1,2,0:T(8,128)(2,1)S(1)}, u32[]{:S(2)}, u32[]{:S(2)}) collective-permute-start(bf16[16,64,64]{1,2,0:T(8,128)(2,1)S(1)} %fusion.12), channel_id=1, source_target_pairs={{0,3},{1,2},{4,7},{5,6},{8,11},{9,10},{12,15},{13,14},{16,19},{17,... | collective-permute-start | bytes 393224 | tf_op jit(solution)/shard_map/ppermute | solution.py:22
  87.3 6.0 %fusion.63 = f32[16,64,512]{2,1,0:T(8,128)S(1)} fusion(bf16[512,16,64]{0,2,1:T(8,128)(2,1)S(1)} %bitcast.148, bf16[16,512,512]{2,1,0:T(8,128)(2,1)} %select_convert_fusion), kind=kOutput, calls=%fused_computation.102 | convolution fusion | flops 536870912 | bytes 11534336 | tf_op jit(solution)/shard_map/hts,shf->thf/dot_general | solution.py:119
  93.3 2.7 %fusion.10 = f32[512,1024]{0,1:T(8,128)} fusion(f32[512,1024]{0,1:T(8,128)} %fusion.11, s32[]{:T(128)S(6)} %select_n.100, bf16[128,2048]{1,0:T(8,128)(2,1)} %collective-permute-done.10, bf16[1,512,2048]{2,1,0:T(8,128)(2,1)S(1)} %copy-done), kind=kOutput, calls=%fused_computation.33 | convolution fusion | flops 268435456 | bytes 2883588 | tf_op jit(solution)/shard_map/dot_general | solution.py:134
  104.6 3.4 %fusion.5 = bf16[256,2048]{1,0:T(8,128)(2,1)} fusion(f32[256,2048]{1,0:T(8,128)S(1)} %fusion.35, bf16[512,2048]{1,0:T(8,128)(2,1)} %collective-permute-done.17, bf16[512,512]{0,1:T(8,128)(2,1)S(1)} %collective-permute-done.16, s32[]{:T(128)S(6)} %select_n.110), kind=kOutput, calls=%fused_computation.9 | convolution fusion | flops 538443776 | bytes 5505028 | tf_op jit(solution)/shard_map/dot_general | solution.py:156
  108.0 3.6 %gather_fusion = bf16[64,16,1024]{2,1,0:T(8,128)(2,1)} fusion(bf16[64,16,1024]{2,1,0:T(8,128)(2,1)} %all-to-all-done, s32[1024]{0:T(1024)S(1)} %pad_clamp_fusion), kind=kCustom, calls=%fused_computation | custom fusion | bytes 4194560 | tf_op jit(solution)/shard_map/gather | solution.py:174
  111.6 13.5 %all-to-all-start.1 = ((bf16[64,16,1024]{2,1,0:T(8,128)(2,1)}), bf16[64,16,1024]{2,1,0:T(8,128)(2,1)}, u32[]{:S(2)}, u32[]{:S(2)}) async-start(bf16[64,16,1024]{2,1,0:T(8,128)(2,1)} %gather_fusion), calls=%async_computation.1 | async-start | bytes 4194304 | tf_op jit(solution)/shard_map/all_to_all | solution.py:46
  132.7 4.9 %fusion.64 = f32[16,64,512]{2,1,0:T(8,128)S(1)} fusion(bf16[512,16,64]{0,2,1:T(8,128)(2,1)S(1)} %multiply_convert_fusion.1, bf16[16,512,512]{2,1,0:T(8,128)(2,1)} %select_convert_fusion), kind=kOutput, calls=%fused_computation.103 | convolution fusion | flops 536870912 | bytes 11534336 | tf_op jit(solution)/shard_map/hts,thf->shf/dot_general | solution.py:146
  137.6 6.2 %collective-permute-done.13 = bf16[16,64,64]{1,2,0:T(8,128)(2,1)S(1)} collective-permute-done((bf16[16,64,64]{1,2,0:T(8,128)(2,1)S(1)}, bf16[16,64,64]{1,2,0:T(8,128)(2,1)S(1)}, u32[]{:S(2)}, u32[]{:S(2)}) %collective-permute-start.13) | collective-permute-done | bytes 131104 | tf_op jit(solution)/shard_map/ppermute | solution.py:22
  143.8 9.1 %collective-permute-done.12 = bf16[16,64,64]{1,2,0:T(8,128)(2,1)S(1)} collective-permute-done((bf16[16,64,64]{1,2,0:T(8,128)(2,1)S(1)}, bf16[16,64,64]{1,2,0:T(8,128)(2,1)S(1)}, u32[]{:S(2)}, u32[]{:S(2)}) %collective-permute-start.12) | collective-permute-done | bytes 131104 | tf_op jit(solution)/shard_map/ppermute | solution.py:22
  165.5 3.7 %subtract_bitcast_fusion = f32[64,8,1024]{2,1,0:T(8,128)} fusion(f32[512,1024]{1,0:T(8,128)S(1)} %fusion.22, bf16[512,1024]{0,1:T(8,128)(2,1)} %collective-permute-done.15, f32[]{:T(128)S(6)} %sub.33, bf16[512,1024]{1,0:T(8,128)(2,1)} %collective-permute-done.14, s32[]{:T(128)S(6)} %select_n.105, bf16[1,512,1024]{2,1,0:T(8,128)(2,1)S(1)} %copy-done.13), kind=kOutput, calls=%fused_computation.19 | convolution fusion | flops 539492352 | bytes 6815752 | tf_op jit(solution)/shard_map/dot_general | solution.py:156
  169.2 20.1 %collective-permute-done.18 = bf16[256,2048]{1,0:T(8,128)(2,1)S(1)} collective-permute-done((bf16[256,2048]{1,0:T(8,128)(2,1)S(1)}, bf16[256,2048]{1,0:T(8,128)(2,1)S(1)}, u32[]{:S(2)}, u32[]{:S(2)}) %collective-permute-start.18) | collective-permute-done | bytes 1048608 | tf_op jit(solution)/shard_map/ppermute | solution.py:22
  189.3 2.7 %fusion.4 = f32[256,2048]{1,0:T(8,128)S(1)} fusion(f32[256,2048]{1,0:T(8,128)S(1)} %fusion.38, bf16[512,2048]{1,0:T(8,128)(2,1)} %collective-permute-done.17, bf16[256,2048]{1,0:T(8,128)(2,1)S(1)} %collective-permute-done.18, f32[]{:T(128)S(6)} %sub.33, bf16[512,512]{0,1:T(8,128)(2,1)S(1)} %copy-done.16, s32[]{:T(128)S(6)} %select_n.108, ...), kind=kOutput, calls=%fused_computation.8 | convolution fusion | flops 541065216 | bytes 8650760 | tf_op jit(solution)/shard_map/dot_general | solution.py:156
  192.0 19.9 %collective-permute-done.19 = bf16[512,1024]{1,0:T(8,128)(2,1)} collective-permute-done((bf16[512,1024]{1,0:T(8,128)(2,1)S(1)}, bf16[512,1024]{1,0:T(8,128)(2,1)}, u32[]{:S(2)}, u32[]{:S(2)}) %collective-permute-start.19) | collective-permute-done | bytes 1048608 | tf_op jit(solution)/shard_map/ppermute | solution.py:22
  211.9 4.8 %add_convert_fusion = (bf16[64,8,1024]{2,1,0:T(8,128)(2,1)}, bf16[1,512,1024]{2,1,0:T(8,128)(2,1)}) fusion(f32[64,8,1024]{2,1,0:T(8,128)S(1)} %bitcast.149, bf16[64,16,1024]{2,1,0:T(8,128)(2,1)} %all-to-all-done.1, f32[]{:T(128)S(6)} %div.26, f32[64,8,1024]{2,1,0:T(8,128)} %subtract_bitcast_fusion, bf16[512,1024]{1,0:T(8,128)(2,1)} %collective-permute-done.19), kind=kLoop, calls=%fused_computation.17 | loop fusion | flops 5767168 | bytes 9437188 | tf_op jit(solution)/shard_map/convert_element_type | solution.py:194
  (106 shorter events, 55.8 us)
Async XLA Ops:
  0.6 49.4 %collective-permute-start.1 = (bf16[512,1024]{1,0:T(8,128)(2,1)}, bf16[512,1024]{1,0:T(8,128)(2,1)}, u32[]{:S(2)}, u32[]{:S(2)}) collective-permute-start(bf16[512,1024]{1,0:T(8,128)(2,1)} %bitcast.155), channel_id=1, source_target_pairs={{0,2},{2,0},{1,3},{3,1},{4,6},{6,4},{5,7},{7,5},{8,10},{10,8},{9,1... | collective-permute-start | bytes 3145736 | tf_op jit(solution)/shard_map/ppermute | solution.py:22
  2.7 58.2 %collective-permute-start = (bf16[512,1024]{1,0:T(8,128)(2,1)}, bf16[512,1024]{1,0:T(8,128)(2,1)}, u32[]{:S(2)}, u32[]{:S(2)}) collective-permute-start(bf16[512,1024]{1,0:T(8,128)(2,1)} %bitcast.156), channel_id=1, source_target_pairs={{0,1},{1,0},{2,3},{3,2},{4,5},{5,4},{6,7},{7,6},{8,9},{9,8},{10,11... | collective-permute-start | bytes 3145736 | tf_op jit(solution)/shard_map/ppermute | solution.py:22
  4.0 47.8 %collective-permute-start.6 = (bf16[256,2048]{1,0:T(8,128)(2,1)}, bf16[256,2048]{1,0:T(8,128)(2,1)}, u32[]{:S(2)}, u32[]{:S(2)}) collective-permute-start(bf16[256,2048]{1,0:T(8,128)(2,1)} %bitcast.153), channel_id=1, source_target_pairs={{0,1},{1,0},{2,3},{3,2},{4,5},{5,4},{6,7},{7,6},{8,9},{9,8},{10,11... | collective-permute-start | bytes 3145736 | tf_op jit(solution)/shard_map/ppermute | solution.py:22
  6.0 37.3 %collective-permute-start.7 = (bf16[128,2048]{1,0:T(8,128)(2,1)}, bf16[128,2048]{1,0:T(8,128)(2,1)}, u32[]{:S(2)}, u32[]{:S(2)}) collective-permute-start(bf16[128,2048]{1,0:T(8,128)(2,1)} %slice_bitcast_fusion), channel_id=1, source_target_pairs={{0,2},{2,0},{1,3},{3,1},{4,6},{6,4},{5,7},{7,5},{8,10},{10,8},{9,1... | collective-permute-start | bytes 1572872 | tf_op jit(solution)/shard_map/ppermute | solution.py:22
  7.5 96.3 %collective-permute-start.17 = (bf16[512,2048]{1,0:T(8,128)(2,1)}, bf16[512,2048]{1,0:T(8,128)(2,1)}, u32[]{:S(2)}, u32[]{:S(2)}) collective-permute-start(bf16[512,2048]{1,0:T(8,128)(2,1)} %bitcast.137), channel_id=1, source_target_pairs={{0,1},{1,0},{2,3},{3,2},{4,5},{5,4},{6,7},{7,6},{8,9},{9,8},{10,11... | collective-permute-start | bytes 6291464 | tf_op jit(solution)/shard_map/ppermute | solution.py:22
  11.4 96.6 %all-to-all-start = ((bf16[64,16,1024]{2,1,0:T(8,128)(2,1)}), bf16[64,16,1024]{2,1,0:T(8,128)(2,1)}, u32[]{:S(2)}, u32[]{:S(2)}) async-start(bf16[64,16,1024]{2,1,0:T(8,128)(2,1)} %pad_maximum_fusion), calls=%async_computation | async-start | bytes 4194304 | tf_op jit(solution)/shard_map/all_to_all | solution.py:46
  35.3 44.5 %copy-start.1 = (bf16[1,512,1024]{1,2,0:T(8,128)(2,1)}, bf16[1,512,1024]{1,2,0:T(8,128)(2,1)S(1)}, u32[]{:S(2)}) copy-start(bf16[1,512,1024]{1,2,0:T(8,128)(2,1)S(1)} %copy.26) | copy-start | bytes 3145732
  43.4 16.0 %collective-permute-start.8 = (bf16[128,2048]{1,0:T(8,128)(2,1)}, bf16[128,2048]{1,0:T(8,128)(2,1)S(1)}, u32[]{:S(2)}, u32[]{:S(2)}) collective-permute-start(bf16[128,2048]{1,0:T(8,128)(2,1)} %collective-permute-done.7), channel_id=1, source_target_pairs={{0,1},{1,0},{2,3},{3,2},{4,5},{5,4},{6,7},{7,6},{8,9},{9,8},{10,11... | collective-permute-start | bytes 1572872 | tf_op jit(solution)/shard_map/ppermute | solution.py:22
  50.1 22.4 %collective-permute-start.9 = (bf16[128,2048]{1,0:T(8,128)(2,1)S(1)}, bf16[128,2048]{1,0:T(8,128)(2,1)}, u32[]{:S(2)}, u32[]{:S(2)}) collective-permute-start(bf16[128,2048]{1,0:T(8,128)(2,1)S(1)} %slice.17), channel_id=1, source_target_pairs={{0,2},{2,0},{1,3},{3,1},{4,6},{6,4},{5,7},{7,5},{8,10},{10,8},{9,1... | collective-permute-start | bytes 1572872 | tf_op jit(solution)/shard_map/ppermute | solution.py:22
  51.8 23.8 %collective-permute-start.2 = (bf16[512,1024]{1,0:T(8,128)(2,1)}, bf16[512,1024]{1,0:T(8,128)(2,1)S(1)}, u32[]{:S(2)}, u32[]{:S(2)}) collective-permute-start(bf16[512,1024]{1,0:T(8,128)(2,1)} %collective-permute-done.1), channel_id=1, source_target_pairs={{0,1},{1,0},{2,3},{3,2},{4,5},{5,4},{6,7},{7,6},{8,9},{9,8},{10,11... | collective-permute-start | bytes 3145736 | tf_op jit(solution)/shard_map/ppermute | solution.py:22
  72.5 20.8 %collective-permute-start.10 = (bf16[128,2048]{1,0:T(8,128)(2,1)}, bf16[128,2048]{1,0:T(8,128)(2,1)}, u32[]{:S(2)}, u32[]{:S(2)}) collective-permute-start(bf16[128,2048]{1,0:T(8,128)(2,1)} %collective-permute-done.9), channel_id=1, source_target_pairs={{0,1},{1,0},{2,3},{3,2},{4,5},{5,4},{6,7},{7,6},{8,9},{9,8},{10,11... | collective-permute-start | bytes 1572872 | tf_op jit(solution)/shard_map/ppermute | solution.py:22
  81.5 14.5 %collective-permute-start.5 = (bf16[16,64,64]{1,2,0:T(8,128)(2,1)S(1)}, bf16[16,64,64]{1,2,0:T(8,128)(2,1)S(1)}, u32[]{:S(2)}, u32[]{:S(2)}) collective-permute-start(bf16[16,64,64]{1,2,0:T(8,128)(2,1)S(1)} %fusion.12), channel_id=1, source_target_pairs={{0,3},{1,2},{4,7},{5,6},{8,11},{9,10},{12,15},{13,14},{16,19},{17,... | collective-permute-start | bytes 393224 | tf_op jit(solution)/shard_map/ppermute | solution.py:22
  84.6 11.4 %collective-permute-start.4 = (bf16[16,64,64]{1,2,0:T(8,128)(2,1)S(1)}, bf16[16,64,64]{1,2,0:T(8,128)(2,1)S(1)}, u32[]{:S(2)}, u32[]{:S(2)}) collective-permute-start(bf16[16,64,64]{1,2,0:T(8,128)(2,1)S(1)} %fusion.12), channel_id=1, source_target_pairs={{0,2},{1,3},{4,6},{5,7},{8,10},{9,11},{12,14},{13,15},{16,18},{17,... | collective-permute-start | bytes 393224 | tf_op jit(solution)/shard_map/ppermute | solution.py:22
  86.0 10.0 %collective-permute-start.3 = (bf16[16,64,64]{1,2,0:T(8,128)(2,1)S(1)}, bf16[16,64,64]{1,2,0:T(8,128)(2,1)S(1)}, u32[]{:S(2)}, u32[]{:S(2)}) collective-permute-start(bf16[16,64,64]{1,2,0:T(8,128)(2,1)S(1)} %fusion.12), channel_id=1, source_target_pairs={{0,1},{2,3},{4,5},{6,7},{8,9},{10,11},{12,13},{14,15},{16,17},{18,... | collective-permute-start | bytes 393224 | tf_op jit(solution)/shard_map/ppermute | solution.py:22
  97.0 6.9 %collective-permute-start.16 = (bf16[512,512]{0,1:T(8,128)(2,1)S(1)}, bf16[512,512]{0,1:T(8,128)(2,1)S(1)}, u32[]{:S(2)}, u32[]{:S(2)}) collective-permute-start(bf16[512,512]{0,1:T(8,128)(2,1)S(1)} %pad_maximum_fusion.2), channel_id=1, source_target_pairs={{0,1},{1,0},{2,3},{3,2},{4,5},{5,4},{6,7},{7,6},{8,9},{9,8},{10,11... | collective-permute-start | bytes 1572872 | tf_op jit(solution)/shard_map/ppermute | solution.py:22
  111.6 100.4 %all-to-all-start.1 = ((bf16[64,16,1024]{2,1,0:T(8,128)(2,1)}), bf16[64,16,1024]{2,1,0:T(8,128)(2,1)}, u32[]{:S(2)}, u32[]{:S(2)}) async-start(bf16[64,16,1024]{2,1,0:T(8,128)(2,1)} %gather_fusion), calls=%async_computation.1 | async-start | bytes 4194304 | tf_op jit(solution)/shard_map/all_to_all | solution.py:46
  127.5 25.4 %copy-start.2 = (bf16[1,512,1024]{1,2,0:T(8,128)(2,1)S(1)}, bf16[1,512,1024]{1,2,0:T(8,128)(2,1)}, u32[]{:S(2)}) copy-start(bf16[1,512,1024]{1,2,0:T(8,128)(2,1)} %copy-done.1) | copy-start | bytes 3145732
  127.5 33.5 %collective-permute-start.14 = (bf16[512,1024]{1,0:T(8,128)(2,1)}, bf16[512,1024]{1,0:T(8,128)(2,1)}, u32[]{:S(2)}, u32[]{:S(2)}) collective-permute-start(bf16[512,1024]{1,0:T(8,128)(2,1)} %pad_maximum_fusion.1), channel_id=1, source_target_pairs={{0,1},{1,0},{2,3},{3,2},{4,5},{5,4},{6,7},{7,6},{8,9},{9,8},{10,11... | collective-permute-start | bytes 3145736 | tf_op jit(solution)/shard_map/ppermute | solution.py:22
  128.0 15.8 %collective-permute-start.13 = (bf16[16,64,64]{1,2,0:T(8,128)(2,1)S(1)}, bf16[16,64,64]{1,2,0:T(8,128)(2,1)S(1)}, u32[]{:S(2)}, u32[]{:S(2)}) collective-permute-start(bf16[16,64,64]{1,2,0:T(8,128)(2,1)S(1)} %fusion.13), channel_id=1, source_target_pairs={{3,0},{2,1},{7,4},{6,5},{11,8},{10,9},{15,12},{14,13},{19,16},{18,... | collective-permute-start | bytes 393224 | tf_op jit(solution)/shard_map/ppermute | solution.py:22
  129.3 23.7 %collective-permute-start.12 = (bf16[16,64,64]{1,2,0:T(8,128)(2,1)S(1)}, bf16[16,64,64]{1,2,0:T(8,128)(2,1)S(1)}, u32[]{:S(2)}, u32[]{:S(2)}) collective-permute-start(bf16[16,64,64]{1,2,0:T(8,128)(2,1)S(1)} %fusion.13), channel_id=1, source_target_pairs={{2,0},{3,1},{6,4},{7,5},{10,8},{11,9},{14,12},{15,13},{18,16},{19,... | collective-permute-start | bytes 393224 | tf_op jit(solution)/shard_map/ppermute | solution.py:22
  130.6 22.4 %collective-permute-start.11 = (bf16[16,64,64]{1,2,0:T(8,128)(2,1)S(1)}, bf16[16,64,64]{1,2,0:T(8,128)(2,1)S(1)}, u32[]{:S(2)}, u32[]{:S(2)}) collective-permute-start(bf16[16,64,64]{1,2,0:T(8,128)(2,1)S(1)} %fusion.13), channel_id=1, source_target_pairs={{1,0},{3,2},{5,4},{7,6},{9,8},{11,10},{13,12},{15,14},{17,16},{19,... | collective-permute-start | bytes 393224 | tf_op jit(solution)/shard_map/ppermute | solution.py:22
  153.4 7.7 %collective-permute-start.15 = (bf16[512,1024]{0,1:T(8,128)(2,1)S(1)}, bf16[512,1024]{0,1:T(8,128)(2,1)}, u32[]{:S(2)}, u32[]{:S(2)}) collective-permute-start(bf16[512,1024]{0,1:T(8,128)(2,1)S(1)} %bitcast.144), channel_id=1, source_target_pairs={{0,1},{1,0},{2,3},{3,2},{4,5},{5,4},{6,7},{7,6},{8,9},{9,8},{10,11... | collective-permute-start | bytes 3145736 | tf_op jit(solution)/shard_map/ppermute | solution.py:22
  160.1 29.2 %collective-permute-start.18 = (bf16[256,2048]{1,0:T(8,128)(2,1)S(1)}, bf16[256,2048]{1,0:T(8,128)(2,1)S(1)}, u32[]{:S(2)}, u32[]{:S(2)}) collective-permute-start(bf16[256,2048]{1,0:T(8,128)(2,1)S(1)} %copy-done.14), channel_id=1, source_target_pairs={{0,2},{2,0},{1,3},{3,1},{4,6},{6,4},{5,7},{7,5},{8,10},{10,8},{9,1... | collective-permute-start | bytes 3145736 | tf_op jit(solution)/shard_map/ppermute | solution.py:22
  163.2 48.7 %collective-permute-start.19 = (bf16[512,1024]{1,0:T(8,128)(2,1)S(1)}, bf16[512,1024]{1,0:T(8,128)(2,1)}, u32[]{:S(2)}, u32[]{:S(2)}) collective-permute-start(bf16[512,1024]{1,0:T(8,128)(2,1)S(1)} %multiply_convert_fusion), channel_id=1, source_target_pairs={{0,2},{2,0},{1,3},{3,1},{4,6},{6,4},{5,7},{7,5},{8,10},{10,8},{9,1... | collective-permute-start | bytes 3145736 | tf_op jit(solution)/shard_map/ppermute | solution.py:22
  (17 other events, 155.1 us)

commit v6 on v5

--- a/solution.py
+++ b/solution.py
@@ -86,13 +86,11 @@
     published = [value_pieces(stale_value[0], replicas), output_pieces(stale_output[0], replicas)]
     spread = swap(jnp.concatenate(published, axis=1))
 
-    twin_features = sent(
-        jnp.concatenate(
-            [column_block(features, 1 - core, rows_v), column_block(features, 3 - core, rows_v)],
-            axis=1,
-        ),
-        TWIN,
-    )
+    away_features = jnp.concatenate(
+        [column_block(features, 1 - core, rows_v), column_block(features, 3 - core, rows_v)],
+        axis=1,
+    )
+    twin_features = sent(away_features, TWIN)
     twin_rows = sent(upstream_rows, TWIN)
 
     values = None
@@ -109,7 +107,7 @@
     states = states.astype(bf16)
     prior = state_sums(states, BEFORE)
     across_oa = sent(weight_o[: rows_o // 2], ACROSS)
-    across_ob = sent(after(weight_o, across_v)[rows_o // 2 :], ACROSS)
+    across_ob = sent(after(weight_o, away_features)[rows_o // 2 :], ACROSS)
     twin_o = sent(weight_o, TWIN)
     both_oa = sent(across_oa, TWIN)
     both_ob = sent(across_ob, TWIN)

time: 218 us -> 229 us (1.050)
  starting transfers between devices: 55.9 us -> 63.1 us
  waiting for transfers between devices: 65.7 us -> 70.7 us
    ppermute x20, waiting for transfers between devices: 65.7 us -> 70.7 us  [sent(): return lax.ppermute(x, 'seq', pairs)]
    all_to_all x2, starting transfers between devices: 26.5 us -> 31 us  [swap(): return lax.all_to_all(x, 'rep', split_axis=0, concat_axis=0, tiled=True)]
    ppermute x20, starting transfers between devices: 29.4 us -> 32.1 us  [sent(): return lax.ppermute(x, 'seq', pairs)]
    unnamed x40 -> x42, local copies, waits for them, and re-layouts: 5.23 us -> 5.25 us
  transfers between devices with their start and end apart: 22 -> 22, of which waited for: 6 -> 6; matrix products, arithmetic and copies ran while one was open for 37% -> 35% of each run, Pallas kernels for 0% -> 0%
where the time goes in v6:
time: 229 us; the launch traced here: 227 us
  waiting for transfers between devices  70.7 us (31%)
  starting transfers between devices  63.1 us (28%)
  matrix products  58.7 us (26%)
  local copies, waits for them, and re-layouts  18.1 us (8%)
  other arithmetic  12.3 us (5%)
  between operations  4.31 us (2%)
    ppermute x20, waiting for transfers between devices, sent(): return lax.ppermute(x, 'seq', pairs)  70.7 us
    ppermute x20, starting transfers between devices, sent(): return lax.ppermute(x, 'seq', pairs)  32.1 us
    all_to_all x2, starting transfers between devices, swap(): return lax.all_to_all(x, 'rep', split_axis=0, concat_axis=0, tiled=True)  31 us
    dot_general x6, matrix products, on_device(): lax.dot_general(upstream_rows, block, (((1,), (1,)), ((), ())), preferred...  12.5 us
    dot_general x4, matrix products, term(): both += lax.dot_general(other, twin_right, dims, preferred_element_type=f32)  11.9 us
    dot_general x4, matrix products, on_device(): jnp.dot(column_block(features, rank ^ step, rows_v), block, preferred_ele...  8.93 us
    dot_general x1, matrix products, on_device(): jnp.einsum('the,she->hts', query_heads, key_heads, preferred_element_type...  7.27 us
    dot_general x1, matrix products, on_device(): jnp.einsum('hts,shf->thf', scores, value_heads, preferred_element_type=f32)  6 us
  transfers between devices with their start and end apart: 22, of which 6 were waited for; matrix products, arithmetic and copies ran while one was open for 35% of the time, Pallas kernels for 0%

profile of v6, /device:TPU:1, one launch (start us, length us, event | category | flops | bytes accessed | tf_op | source)
XLA Modules:
  0.0 227.2 jit_solution(10689298452300285502)
XLA Ops:
  12.5 13.9 %all-to-all-start = ((bf16[64,16,1024]{2,1,0:T(8,128)(2,1)}), bf16[64,16,1024]{2,1,0:T(8,128)(2,1)}, u32[]{:S(2)}, u32[]{:S(2)}) async-start(bf16[64,16,1024]{2,1,0:T(8,128)(2,1)} %pad_maximum_fusion), calls=%async_computation | async-start | bytes 4194304 | tf_op jit(solution)/shard_map/all_to_all | solution.py:46
  26.4 3.1 %fusion.24 = f32[512,1024]{1,0:T(8,128)} fusion(bf16[1,512,2048]{2,1,0:T(8,128)(2,1)} %param.10, s32[]{:T(128)S(6)} %select_n.90, bf16[1,512,1024]{2,1,0:T(8,128)(2,1)S(1)} %copy-done.11), kind=kOutput, calls=%fused_computation.52 | convolution fusion | flops 536870912 | bytes 3670020 | tf_op jit(solution)/shard_map/dot_general | solution.py:98
  37.1 7.3 %select_convert_fusion = bf16[16,512,512]{2,1,0:T(8,128)(2,1)} fusion(bf16[512,16,64]{0,2,1:T(8,128)(2,1)} %bitcast.141, bf16[512,16,64]{0,2,1:T(8,128)(2,1)S(1)} %bitcast.138, pred[512,512]{1,0:T(8,128)(4,1)S(1)} %iota_compare_fusion), kind=kOutput, calls=%fused_computation.1 | convolution fusion | flops 545259520 | bytes 10747904 | tf_op jit(solution)/shard_map/the,she->hts/dot_general | solution.py:115
  44.4 7.0 %collective-permute-start.17 = (bf16[512,2048]{1,0:T(8,128)(2,1)S(1)}, bf16[512,2048]{1,0:T(8,128)(2,1)}, u32[]{:S(2)}, u32[]{:S(2)}) collective-permute-start(bf16[512,2048]{1,0:T(8,128)(2,1)S(1)} %bitcast.137), channel_id=1, source_target_pairs={{0,1},{1,0},{2,3},{3,2},{4,5},{5,4},{6,7},{7,6},{8,9},{9,8},{10,11... | collective-permute-start | bytes 6291464 | tf_op jit(solution)/shard_map/ppermute | solution.py:22
  51.3 11.5 %collective-permute-done.9 = bf16[128,2048]{1,0:T(8,128)(2,1)} collective-permute-done((bf16[128,2048]{1,0:T(8,128)(2,1)}, bf16[128,2048]{1,0:T(8,128)(2,1)}, u32[]{:S(2)}, u32[]{:S(2)}) %collective-permute-start.9) | collective-permute-done | bytes 524320 | tf_op jit(solution)/shard_map/ppermute | solution.py:22
  62.8 4.7 %collective-permute-start.8 = (bf16[128,2048]{1,0:T(8,128)(2,1)}, bf16[128,2048]{1,0:T(8,128)(2,1)S(1)}, u32[]{:S(2)}, u32[]{:S(2)}) collective-permute-start(bf16[128,2048]{1,0:T(8,128)(2,1)} %collective-permute-done.7), channel_id=1, source_target_pairs={{0,1},{1,0},{2,3},{3,2},{4,5},{5,4},{6,7},{7,6},{8,9},{9,8},{10,11... | collective-permute-start | bytes 1572872 | tf_op jit(solution)/shard_map/ppermute | solution.py:22
  68.0 2.8 %convolution_dynamic-update-slice_fusion = f32[512,1024]{0,1:T(8,128)} fusion(f32[512,1024]{0,1:T(8,128)} %convolution_dynamic-update-slice_fusion.1, s32[]{:T(128)S(6)} %select_n.96, bf16[256,2048]{1,0:T(8,128)(2,1)} %collective-permute-done.6, bf16[1,512,2048]{2,1,0:T(8,128)(2,1)S(1)} %copy-done), kind=kOutput, calls=%fused_computation.26 | convolution fusion | flops 536870912 | bytes 3670020 | tf_op jit(solution)/shard_map/dot_general | solution.py:132
  70.8 2.6 %convolution_dynamic-update-slice_fusion.3 = f32[512,1024]{0,1:T(8,128)} fusion(f32[512,1024]{0,1:T(8,128)} %convolution_dynamic-update-slice_fusion, s32[]{:T(128)S(6)} %select_n.97, bf16[128,2048]{1,0:T(8,128)(2,1)} %collective-permute-done.7, bf16[1,512,2048]{2,1,0:T(8,128)(2,1)S(1)} %copy-done), kind=kOutput, calls=%fused_computation.31 | convolution fusion | flops 268435456 | bytes 2883588 | tf_op jit(solution)/shard_map/dot_general | solution.py:132
  74.9 2.6 %fusion.11 = f32[512,1024]{0,1:T(8,128)} fusion(f32[512,1024]{0,1:T(8,128)} %convolution_dynamic-update-slice_fusion.2, s32[]{:T(128)S(6)} %select_n.102, bf16[128,2048]{1,0:T(8,128)(2,1)} %collective-permute-done.9, bf16[1,512,2048]{2,1,0:T(8,128)(2,1)S(1)} %copy-done), kind=kOutput, calls=%fused_computation.35 | convolution fusion | flops 268435456 | bytes 2883588 | tf_op jit(solution)/shard_map/dot_general | solution.py:132
  85.0 2.3 %copy.24 = bf16[512,1024]{0,1:T(8,128)(2,1)} copy(bf16[512,1024]{1,0:T(8,128)(2,1)} %multiply_convert_fusion.2) | data formatting | bytes 2097152 | tf_op jit(solution)/shard_map/convert_element_type | solution.py:102
  89.0 3.6 %collective-permute-start.5 = (bf16[16,64,64]{1,2,0:T(8,128)(2,1)S(1)}, bf16[16,64,64]{1,2,0:T(8,128)(2,1)S(1)}, u32[]{:S(2)}, u32[]{:S(2)}) collective-permute-start(bf16[16,64,64]{1,2,0:T(8,128)(2,1)S(1)} %fusion.12), channel_id=1, source_target_pairs={{0,3},{1,2},{4,7},{5,6},{8,11},{9,10},{12,15},{13,14},{16,19},{17,... | collective-permute-start | bytes 393224 | tf_op jit(solution)/shard_map/ppermute | solution.py:22
  95.2 6.0 %fusion.63 = f32[16,64,512]{2,1,0:T(8,128)S(1)} fusion(bf16[512,16,64]{0,2,1:T(8,128)(2,1)S(1)} %bitcast.148, bf16[16,512,512]{2,1,0:T(8,128)(2,1)} %select_convert_fusion), kind=kOutput, calls=%fused_computation.102 | convolution fusion | flops 536870912 | bytes 11534336 | tf_op jit(solution)/shard_map/hts,shf->thf/dot_general | solution.py:117
  101.3 2.7 %collective-permute-done.4 = bf16[16,64,64]{1,2,0:T(8,128)(2,1)S(1)} collective-permute-done((bf16[16,64,64]{1,2,0:T(8,128)(2,1)S(1)}, bf16[16,64,64]{1,2,0:T(8,128)(2,1)S(1)}, u32[]{:S(2)}, u32[]{:S(2)}) %collective-permute-start.4) | collective-permute-done | bytes 131104 | tf_op jit(solution)/shard_map/ppermute | solution.py:22
  112.2 3.4 %fusion.5 = bf16[256,2048]{1,0:T(8,128)(2,1)} fusion(f32[256,2048]{1,0:T(8,128)S(1)} %fusion.35, bf16[512,2048]{1,0:T(8,128)(2,1)} %collective-permute-done.17, bf16[512,512]{0,1:T(8,128)(2,1)S(1)} %collective-permute-done.16, s32[]{:T(128)S(6)} %select_n.110), kind=kOutput, calls=%fused_computation.9 | convolution fusion | flops 538443776 | bytes 5505028 | tf_op jit(solution)/shard_map/dot_general | solution.py:154
  115.6 3.6 %gather_fusion = bf16[64,16,1024]{2,1,0:T(8,128)(2,1)} fusion(bf16[64,16,1024]{2,1,0:T(8,128)(2,1)} %all-to-all-done, s32[1024]{0:T(1024)S(1)} %pad_clamp_fusion), kind=kCustom, calls=%fused_computation | custom fusion | bytes 4194560 | tf_op jit(solution)/shard_map/gather | solution.py:172
  119.1 17.1 %all-to-all-start.1 = ((bf16[64,16,1024]{2,1,0:T(8,128)(2,1)}), bf16[64,16,1024]{2,1,0:T(8,128)(2,1)}, u32[]{:S(2)}, u32[]{:S(2)}) async-start(bf16[64,16,1024]{2,1,0:T(8,128)(2,1)} %gather_fusion), calls=%async_computation.1 | async-start | bytes 4194304 | tf_op jit(solution)/shard_map/all_to_all | solution.py:46
  141.6 4.9 %fusion.64 = f32[16,64,512]{2,1,0:T(8,128)S(1)} fusion(bf16[512,16,64]{0,2,1:T(8,128)(2,1)S(1)} %multiply_convert_fusion.1, bf16[16,512,512]{2,1,0:T(8,128)(2,1)} %select_convert_fusion), kind=kOutput, calls=%fused_computation.103 | convolution fusion | flops 536870912 | bytes 11534336 | tf_op jit(solution)/shard_map/hts,thf->shf/dot_general | solution.py:144
  146.5 7.3 %collective-permute-done.13 = bf16[16,64,64]{1,2,0:T(8,128)(2,1)S(1)} collective-permute-done((bf16[16,64,64]{1,2,0:T(8,128)(2,1)S(1)}, bf16[16,64,64]{1,2,0:T(8,128)(2,1)S(1)}, u32[]{:S(2)}, u32[]{:S(2)}) %collective-permute-start.13) | collective-permute-done | bytes 131104 | tf_op jit(solution)/shard_map/ppermute | solution.py:22
  153.8 8.3 %collective-permute-done.12 = bf16[16,64,64]{1,2,0:T(8,128)(2,1)S(1)} collective-permute-done((bf16[16,64,64]{1,2,0:T(8,128)(2,1)S(1)}, bf16[16,64,64]{1,2,0:T(8,128)(2,1)S(1)}, u32[]{:S(2)}, u32[]{:S(2)}) %collective-permute-start.12) | collective-permute-done | bytes 131104 | tf_op jit(solution)/shard_map/ppermute | solution.py:22
  175.2 3.7 %subtract_bitcast_fusion = f32[64,8,1024]{2,1,0:T(8,128)} fusion(f32[512,1024]{1,0:T(8,128)S(1)} %fusion.22, bf16[512,1024]{0,1:T(8,128)(2,1)} %collective-permute-done.15, f32[]{:T(128)S(6)} %sub.33, bf16[512,1024]{1,0:T(8,128)(2,1)} %collective-permute-done.14, s32[]{:T(128)S(6)} %select_n.105, bf16[1,512,1024]{2,1,0:T(8,128)(2,1)S(1)} %copy-done.12), kind=kOutput, calls=%fused_computation.19 | convolution fusion | flops 539492352 | bytes 6815752 | tf_op jit(solution)/shard_map/dot_general | solution.py:154
  178.8 21.0 %collective-permute-done.18 = bf16[256,2048]{1,0:T(8,128)(2,1)S(1)} collective-permute-done((bf16[256,2048]{1,0:T(8,128)(2,1)S(1)}, bf16[256,2048]{1,0:T(8,128)(2,1)S(1)}, u32[]{:S(2)}, u32[]{:S(2)}) %collective-permute-start.18) | collective-permute-done | bytes 1048608 | tf_op jit(solution)/shard_map/ppermute | solution.py:22
  199.9 2.7 %fusion.4 = f32[256,2048]{1,0:T(8,128)S(1)} fusion(f32[256,2048]{1,0:T(8,128)S(1)} %fusion.38, bf16[512,2048]{1,0:T(8,128)(2,1)} %collective-permute-done.17, bf16[256,2048]{1,0:T(8,128)(2,1)S(1)} %collective-permute-done.18, f32[]{:T(128)S(6)} %sub.33, bf16[512,512]{0,1:T(8,128)(2,1)S(1)} %copy-done.17, s32[]{:T(128)S(6)} %select_n.108, ...), kind=kOutput, calls=%fused_computation.8 | convolution fusion | flops 541065216 | bytes 8650760 | tf_op jit(solution)/shard_map/dot_general | solution.py:154
  202.5 19.9 %collective-permute-done.19 = bf16[512,1024]{1,0:T(8,128)(2,1)} collective-permute-done((bf16[512,1024]{1,0:T(8,128)(2,1)S(1)}, bf16[512,1024]{1,0:T(8,128)(2,1)}, u32[]{:S(2)}, u32[]{:S(2)}) %collective-permute-start.19) | collective-permute-done | bytes 1048608 | tf_op jit(solution)/shard_map/ppermute | solution.py:22
  222.4 4.8 %add_convert_fusion = (bf16[64,8,1024]{2,1,0:T(8,128)(2,1)}, bf16[1,512,1024]{2,1,0:T(8,128)(2,1)}) fusion(f32[64,8,1024]{2,1,0:T(8,128)S(1)} %bitcast.149, bf16[64,16,1024]{2,1,0:T(8,128)(2,1)} %all-to-all-done.1, f32[]{:T(128)S(6)} %div.26, f32[64,8,1024]{2,1,0:T(8,128)} %subtract_bitcast_fusion, bf16[512,1024]{1,0:T(8,128)(2,1)} %collective-permute-done.19), kind=kLoop, calls=%fused_computation.17 | loop fusion | flops 5767168 | bytes 9437188 | tf_op jit(solution)/shard_map/convert_element_type | solution.py:192
  (108 shorter events, 56.5 us)
Async XLA Ops:
  0.6 66.9 %collective-permute-start.1 = (bf16[512,1024]{1,0:T(8,128)(2,1)}, bf16[512,1024]{1,0:T(8,128)(2,1)}, u32[]{:S(2)}, u32[]{:S(2)}) collective-permute-start(bf16[512,1024]{1,0:T(8,128)(2,1)} %bitcast.155), channel_id=1, source_target_pairs={{0,2},{2,0},{1,3},{3,1},{4,6},{6,4},{5,7},{7,5},{8,10},{10,8},{9,1... | collective-permute-start | bytes 3145736 | tf_op jit(solution)/shard_map/ppermute | solution.py:22
  2.7 78.2 %collective-permute-start = (bf16[512,1024]{1,0:T(8,128)(2,1)}, bf16[512,1024]{1,0:T(8,128)(2,1)}, u32[]{:S(2)}, u32[]{:S(2)}) collective-permute-start(bf16[512,1024]{1,0:T(8,128)(2,1)} %bitcast.156), channel_id=1, source_target_pairs={{0,1},{1,0},{2,3},{3,2},{4,5},{5,4},{6,7},{7,6},{8,9},{9,8},{10,11... | collective-permute-start | bytes 3145736 | tf_op jit(solution)/shard_map/ppermute | solution.py:22
  4.0 63.5 %collective-permute-start.6 = (bf16[256,2048]{1,0:T(8,128)(2,1)}, bf16[256,2048]{1,0:T(8,128)(2,1)}, u32[]{:S(2)}, u32[]{:S(2)}) collective-permute-start(bf16[256,2048]{1,0:T(8,128)(2,1)} %bitcast.153), channel_id=1, source_target_pairs={{0,1},{1,0},{2,3},{3,2},{4,5},{5,4},{6,7},{7,6},{8,9},{9,8},{10,11... | collective-permute-start | bytes 3145736 | tf_op jit(solution)/shard_map/ppermute | solution.py:22
  6.0 38.4 %collective-permute-start.7 = (bf16[128,2048]{1,0:T(8,128)(2,1)}, bf16[128,2048]{1,0:T(8,128)(2,1)}, u32[]{:S(2)}, u32[]{:S(2)}) collective-permute-start(bf16[128,2048]{1,0:T(8,128)(2,1)} %slice_bitcast_fusion), channel_id=1, source_target_pairs={{0,2},{2,0},{1,3},{3,1},{4,6},{6,4},{5,7},{7,5},{8,10},{10,8},{9,1... | collective-permute-start | bytes 1572872 | tf_op jit(solution)/shard_map/ppermute | solution.py:22
  10.9 51.9 %collective-permute-start.9 = (bf16[128,2048]{1,0:T(8,128)(2,1)}, bf16[128,2048]{1,0:T(8,128)(2,1)}, u32[]{:S(2)}, u32[]{:S(2)}) collective-permute-start(bf16[128,2048]{1,0:T(8,128)(2,1)} %slice.17), channel_id=1, source_target_pairs={{0,2},{2,0},{1,3},{3,1},{4,6},{6,4},{5,7},{7,5},{8,10},{10,8},{9,1... | collective-permute-start | bytes 1572872 | tf_op jit(solution)/shard_map/ppermute | solution.py:22
  12.5 103.1 %all-to-all-start = ((bf16[64,16,1024]{2,1,0:T(8,128)(2,1)}), bf16[64,16,1024]{2,1,0:T(8,128)(2,1)}, u32[]{:S(2)}, u32[]{:S(2)}) async-start(bf16[64,16,1024]{2,1,0:T(8,128)(2,1)} %pad_maximum_fusion), calls=%async_computation | async-start | bytes 4194304 | tf_op jit(solution)/shard_map/all_to_all | solution.py:46
  37.0 50.2 %copy-start.1 = (bf16[1,512,1024]{1,2,0:T(8,128)(2,1)}, bf16[1,512,1024]{1,2,0:T(8,128)(2,1)S(1)}, u32[]{:S(2)}) copy-start(bf16[1,512,1024]{1,2,0:T(8,128)(2,1)S(1)} %copy.26) | copy-start | bytes 3145732
  44.4 67.0 %collective-permute-start.17 = (bf16[512,2048]{1,0:T(8,128)(2,1)S(1)}, bf16[512,2048]{1,0:T(8,128)(2,1)}, u32[]{:S(2)}, u32[]{:S(2)}) collective-permute-start(bf16[512,2048]{1,0:T(8,128)(2,1)S(1)} %bitcast.137), channel_id=1, source_target_pairs={{0,1},{1,0},{2,3},{3,2},{4,5},{5,4},{6,7},{7,6},{8,9},{9,8},{10,11... | collective-permute-start | bytes 6291464 | tf_op jit(solution)/shard_map/ppermute | solution.py:22
  62.8 10.5 %collective-permute-start.8 = (bf16[128,2048]{1,0:T(8,128)(2,1)}, bf16[128,2048]{1,0:T(8,128)(2,1)S(1)}, u32[]{:S(2)}, u32[]{:S(2)}) collective-permute-start(bf16[128,2048]{1,0:T(8,128)(2,1)} %collective-permute-done.7), channel_id=1, source_target_pairs={{0,1},{1,0},{2,3},{3,2},{4,5},{5,4},{6,7},{7,6},{8,9},{9,8},{10,11... | collective-permute-start | bytes 1572872 | tf_op jit(solution)/shard_map/ppermute | solution.py:22
  67.5 9.9 %collective-permute-start.10 = (bf16[128,2048]{1,0:T(8,128)(2,1)}, bf16[128,2048]{1,0:T(8,128)(2,1)S(1)}, u32[]{:S(2)}, u32[]{:S(2)}) collective-permute-start(bf16[128,2048]{1,0:T(8,128)(2,1)} %collective-permute-done.9), channel_id=1, source_target_pairs={{0,1},{1,0},{2,3},{3,2},{4,5},{5,4},{6,7},{7,6},{8,9},{9,8},{10,11... | collective-permute-start | bytes 1572872 | tf_op jit(solution)/shard_map/ppermute | solution.py:22
  67.5 15.6 %collective-permute-start.2 = (bf16[512,1024]{1,0:T(8,128)(2,1)}, bf16[512,1024]{1,0:T(8,128)(2,1)S(1)}, u32[]{:S(2)}, u32[]{:S(2)}) collective-permute-start(bf16[512,1024]{1,0:T(8,128)(2,1)} %collective-permute-done.1), channel_id=1, source_target_pairs={{0,1},{1,0},{2,3},{3,2},{4,5},{5,4},{6,7},{7,6},{8,9},{9,8},{10,11... | collective-permute-start | bytes 3145736 | tf_op jit(solution)/shard_map/ppermute | solution.py:22
  89.0 12.3 %collective-permute-start.5 = (bf16[16,64,64]{1,2,0:T(8,128)(2,1)S(1)}, bf16[16,64,64]{1,2,0:T(8,128)(2,1)S(1)}, u32[]{:S(2)}, u32[]{:S(2)}) collective-permute-start(bf16[16,64,64]{1,2,0:T(8,128)(2,1)S(1)} %fusion.12), channel_id=1, source_target_pairs={{0,3},{1,2},{4,7},{5,6},{8,11},{9,10},{12,15},{13,14},{16,19},{17,... | collective-permute-start | bytes 393224 | tf_op jit(solution)/shard_map/ppermute | solution.py:22
  92.6 11.3 %collective-permute-start.4 = (bf16[16,64,64]{1,2,0:T(8,128)(2,1)S(1)}, bf16[16,64,64]{1,2,0:T(8,128)(2,1)S(1)}, u32[]{:S(2)}, u32[]{:S(2)}) collective-permute-start(bf16[16,64,64]{1,2,0:T(8,128)(2,1)S(1)} %fusion.12), channel_id=1, source_target_pairs={{0,2},{1,3},{4,6},{5,7},{8,10},{9,11},{12,14},{13,15},{16,18},{17,... | collective-permute-start | bytes 393224 | tf_op jit(solution)/shard_map/ppermute | solution.py:22
  93.9 10.0 %collective-permute-start.3 = (bf16[16,64,64]{1,2,0:T(8,128)(2,1)S(1)}, bf16[16,64,64]{1,2,0:T(8,128)(2,1)S(1)}, u32[]{:S(2)}, u32[]{:S(2)}) collective-permute-start(bf16[16,64,64]{1,2,0:T(8,128)(2,1)S(1)} %fusion.12), channel_id=1, source_target_pairs={{0,1},{2,3},{4,5},{6,7},{8,9},{10,11},{12,13},{14,15},{16,17},{18,... | collective-permute-start | bytes 393224 | tf_op jit(solution)/shard_map/ppermute | solution.py:22
  104.9 6.5 %collective-permute-start.16 = (bf16[512,512]{0,1:T(8,128)(2,1)S(1)}, bf16[512,512]{0,1:T(8,128)(2,1)S(1)}, u32[]{:S(2)}, u32[]{:S(2)}) collective-permute-start(bf16[512,512]{0,1:T(8,128)(2,1)S(1)} %pad_maximum_fusion.2), channel_id=1, source_target_pairs={{0,1},{1,0},{2,3},{3,2},{4,5},{5,4},{6,7},{7,6},{8,9},{9,8},{10,11... | collective-permute-start | bytes 1572872 | tf_op jit(solution)/shard_map/ppermute | solution.py:22
  119.1 103.3 %all-to-all-start.1 = ((bf16[64,16,1024]{2,1,0:T(8,128)(2,1)}), bf16[64,16,1024]{2,1,0:T(8,128)(2,1)}, u32[]{:S(2)}, u32[]{:S(2)}) async-start(bf16[64,16,1024]{2,1,0:T(8,128)(2,1)} %gather_fusion), calls=%async_computation.1 | async-start | bytes 4194304 | tf_op jit(solution)/shard_map/all_to_all | solution.py:46
  136.2 25.9 %copy-start.2 = (bf16[1,512,1024]{1,2,0:T(8,128)(2,1)S(1)}, bf16[1,512,1024]{1,2,0:T(8,128)(2,1)}, u32[]{:S(2)}) copy-start(bf16[1,512,1024]{1,2,0:T(8,128)(2,1)} %copy-done.1) | copy-start | bytes 3145732
  136.2 34.4 %collective-permute-start.14 = (bf16[512,1024]{1,0:T(8,128)(2,1)}, bf16[512,1024]{1,0:T(8,128)(2,1)}, u32[]{:S(2)}, u32[]{:S(2)}) collective-permute-start(bf16[512,1024]{1,0:T(8,128)(2,1)} %pad_maximum_fusion.1), channel_id=1, source_target_pairs={{0,1},{1,0},{2,3},{3,2},{4,5},{5,4},{6,7},{7,6},{8,9},{9,8},{10,11... | collective-permute-start | bytes 3145736 | tf_op jit(solution)/shard_map/ppermute | solution.py:22
  137.0 16.8 %collective-permute-start.13 = (bf16[16,64,64]{1,2,0:T(8,128)(2,1)S(1)}, bf16[16,64,64]{1,2,0:T(8,128)(2,1)S(1)}, u32[]{:S(2)}, u32[]{:S(2)}) collective-permute-start(bf16[16,64,64]{1,2,0:T(8,128)(2,1)S(1)} %fusion.13), channel_id=1, source_target_pairs={{3,0},{2,1},{7,4},{6,5},{11,8},{10,9},{15,12},{14,13},{19,16},{18,... | collective-permute-start | bytes 393224 | tf_op jit(solution)/shard_map/ppermute | solution.py:22
  138.3 23.8 %collective-permute-start.12 = (bf16[16,64,64]{1,2,0:T(8,128)(2,1)S(1)}, bf16[16,64,64]{1,2,0:T(8,128)(2,1)S(1)}, u32[]{:S(2)}, u32[]{:S(2)}) collective-permute-start(bf16[16,64,64]{1,2,0:T(8,128)(2,1)S(1)} %fusion.13), channel_id=1, source_target_pairs={{2,0},{3,1},{6,4},{7,5},{10,8},{11,9},{14,12},{15,13},{18,16},{19,... | collective-permute-start | bytes 393224 | tf_op jit(solution)/shard_map/ppermute | solution.py:22
  139.6 22.5 %collective-permute-start.11 = (bf16[16,64,64]{1,2,0:T(8,128)(2,1)S(1)}, bf16[16,64,64]{1,2,0:T(8,128)(2,1)S(1)}, u32[]{:S(2)}, u32[]{:S(2)}) collective-permute-start(bf16[16,64,64]{1,2,0:T(8,128)(2,1)S(1)} %fusion.13), channel_id=1, source_target_pairs={{1,0},{3,2},{5,4},{7,6},{9,8},{11,10},{13,12},{15,14},{17,16},{19,... | collective-permute-start | bytes 393224 | tf_op jit(solution)/shard_map/ppermute | solution.py:22
  162.5 8.1 %collective-permute-start.15 = (bf16[512,1024]{0,1:T(8,128)(2,1)S(1)}, bf16[512,1024]{0,1:T(8,128)(2,1)}, u32[]{:S(2)}, u32[]{:S(2)}) collective-permute-start(bf16[512,1024]{0,1:T(8,128)(2,1)S(1)} %bitcast.144), channel_id=1, source_target_pairs={{0,1},{1,0},{2,3},{3,2},{4,5},{5,4},{6,7},{7,6},{8,9},{9,8},{10,11... | collective-permute-start | bytes 3145736 | tf_op jit(solution)/shard_map/ppermute | solution.py:22
  169.7 30.1 %collective-permute-start.18 = (bf16[256,2048]{1,0:T(8,128)(2,1)S(1)}, bf16[256,2048]{1,0:T(8,128)(2,1)S(1)}, u32[]{:S(2)}, u32[]{:S(2)}) collective-permute-start(bf16[256,2048]{1,0:T(8,128)(2,1)S(1)} %copy-done.15), channel_id=1, source_target_pairs={{0,2},{2,0},{1,3},{3,1},{4,6},{6,4},{5,7},{7,5},{8,10},{10,8},{9,1... | collective-permute-start | bytes 3145736 | tf_op jit(solution)/shard_map/ppermute | solution.py:22
  172.9 49.6 %collective-permute-start.19 = (bf16[512,1024]{1,0:T(8,128)(2,1)S(1)}, bf16[512,1024]{1,0:T(8,128)(2,1)}, u32[]{:S(2)}, u32[]{:S(2)}) collective-permute-start(bf16[512,1024]{1,0:T(8,128)(2,1)S(1)} %multiply_convert_fusion), channel_id=1, source_target_pairs={{0,2},{2,0},{1,3},{3,1},{4,6},{6,4},{5,7},{7,5},{8,10},{10,8},{9,1... | collective-permute-start | bytes 3145736 | tf_op jit(solution)/shard_map/ppermute | solution.py:22
  (18 other events, 134.2 us)
